TPU v7x, 256 devices: a whole 4x4x8 slice. The times are simulated.
256 devices in a mesh: band: 16 (over y_lo, x, core), grid: 16 (over y_hi, z).
Axes of the slice: x: 4, y: 4 (y_hi: 2, y_lo: 2; y = y_hi * 2 + y_lo), z: 8, core: 2. Of those that a mesh axis runs over, the one named last changes fastest.
Arguments:
- orbitals: float32 [64, 48, 2304], P('band', 'grid'), may hold values from -5.5 to 6.6
- occupation: int32 [64], P('band'), may hold values from 0 to 2
- cutoff: int32 [], replicated, may hold values from 144 to 1728
Outputs:
- exchange_term: float32 [64, 48, 2304], P('band', 'grid')
All inputs are finite; a program needn't handle non-finite values.
Results may differ from a plain program's by a relative error of at most 0.00005.
Values sent between devices are 32-bit elements; how exact they have to be, the bound alone decides.
No kernel may reach another device: no remote copies, remote signals or barrier semaphores. Data moves between devices by JAX's collectives and lax.ppermute only.
A program may use at most 128 MiB of HBM per device.

v0:
```python
import functools

import numpy as np
import jax
import jax.numpy as jnp
from jax import lax
from jax.experimental import pallas as pl
from jax.experimental.pallas import tpu as pltpu
from jax.sharding import PartitionSpec as P


G = 48
ROW = G * G
HALF = ROW // 2
WIDE = 256
YB = 8
LB = YB * G
VM = pl.BlockSpec(memory_space=pltpu.VMEM)
SM = pl.BlockSpec(memory_space=pltpu.SMEM)


def split2(x):
    hi = x.astype(jnp.bfloat16)
    lo = (x - hi.astype(jnp.float32)).astype(jnp.bfloat16)
    return jnp.concatenate([hi, lo], axis=0)


def apply(mat, x):
    both = jnp.dot(mat, split2(x), preferred_element_type=jnp.float32)
    return both[:G] + both[G:]


def f32(*shape):
    return jax.ShapeDtypeStruct(shape, jnp.float32)


def small_call(body, outs, *args, scalars=0):
    many = len(outs) > 1
    return pl.pallas_call(
        body,
        out_shape=outs if many else outs[0],
        in_specs=[SM] * scalars + [VM] * (len(args) - scalars),
        out_specs=[VM] * len(outs) if many else VM,
        cost_estimate=pl.CostEstimate(flops=10**6, bytes_accessed=10**6, transcendentals=0),
    )(*args)


def pack_body(y, slab, came, blk):
    flip = y[0] != 0
    for o in range(2):
        mine = slab[2 * y[0] + o]
        other = came[o]
        a = jnp.where(flip, other, mine)
        b = jnp.where(flip, mine, other)
        for h in range(2):
            r = o * 12 + h * 6
            blk[r:r + 3, :] = a[:, h * HALF:(h + 1) * HALF]
            blk[r + 3:r + 6, :] = b[:, h * HALF:(h + 1) * HALF]


def assemble_body(*refs):
    both, lone = refs[8], refs[9:]
    for k in range(8):
        for o in range(2):
            for h in range(2):
                r = o * 12 + h * 6
                rows, lanes = slice(6 * k, 6 * k + 6), slice(h * HALF, (h + 1) * HALF)
                piece = refs[k][r:r + 6, :]
                both[o, rows, lanes] = piece
                lone[o][rows, lanes] = piece


def disperse_body(a, b, c0, c1, *outs):
    back = (c0, c1)
    for k in range(8):
        for o in range(2):
            for h in range(2):
                r = o * 12 + h * 6
                rows, lanes = slice(6 * k, 6 * k + 6), slice(h * HALF, (h + 1) * HALF)
                outs[k][r:r + 6, :] = a[o, rows, lanes] + b[o, rows, lanes] + back[o][rows, lanes]


def unpack_body(y, *refs):
    keep, give = refs[8:]
    flip = y[0] != 0
    for o in range(2):
        for h in range(2):
            r = o * 12 + h * 6
            total = refs[0][r:r + 6, :]
            for k in range(1, 8):
                total = total + refs[k][r:r + 6, :]
            a, b = total[:3], total[3:]
            keep[o, :, h * HALF:(h + 1) * HALF] = jnp.where(flip, b, a)
            give[o, :, h * HALF:(h + 1) * HALF] = jnp.where(flip, a, b)


def kernel(first, idx, w_own, w_twin, w_vis, own, twin, vis, ktab, fx, ix, fz, iz, *refs):
    prior = () if first else refs[:2]
    home, away, back, spec, rows, cols, zed = refs[len(prior):]
    gi, gj = idx[0], idx[1]
    once = idx[2] if first else idx[3]
    slots = 5 if first else 4

    def pick(i, lanes):
        return jnp.where(i < 2, own[i & 1, :, lanes], twin[i & 1, :, lanes])

    def ours(i, lanes):
        return own[i, :, lanes] if i < 2 else twin[i - 2, :, lanes]

    def enter(yb, _):
        lanes = pl.ds(pl.multiple_of(yb * LB, LB), LB)
        for p in range(slots):
            r = ours(p, lanes) * vis[:, lanes] if p < 4 else pick(gi, lanes) * pick(gj, lanes)
            rows[p * G:(p + 1) * G, :] = apply(fx[...], r)
        for c in range(3):
            cols[c * 128:(c + 1) * 128, :] = rows[:, c * 128:(c + 1) * 128].T
        for y in range(YB):
            zed[y] = apply(fz[...], cols[y * G:(y + 1) * G, :])
        spec[:, pl.ds(pl.multiple_of(yb * YB, YB), YB), :] = jnp.swapaxes(zed[...], 0, 1)
        return 0

    lax.fori_loop(0, G // YB, enter, 0)

    def middle(k, _):
        for u in range(4):
            kz = k * 4 + u
            s = apply(fz[...], spec[kz]) * ktab[kz]
            spec[kz] = apply(iz[...], s)
        return 0

    lax.fori_loop(0, G // 4, middle, 0)

    keep = jnp.where(once != 0, 0.0, 1.0)
    wo = [w_own[0] * keep, w_own[1] * keep, w_twin[0] * keep, w_twin[1] * keep]
    wj = jnp.where(gj < 2, w_own[gj & 1], w_twin[gj & 1])
    wg = jnp.where(gi < 2, wj, 0.0)
    wt = jnp.where(gi < 2, 0.0, wj)

    def leave(yb, _):
        lanes = pl.ds(pl.multiple_of(yb * LB, LB), LB)
        zed[...] = jnp.swapaxes(spec[:, pl.ds(pl.multiple_of(yb * YB, YB), YB), :], 0, 1)
        for y in range(YB):
            cols[y * G:(y + 1) * G, :] = apply(iz[...], zed[y])
        for c in range(3):
            rows[:, c * 128:(c + 1) * 128] = cols[c * 128:(c + 1) * 128, :].T
        total = None
        v = vis[:, lanes] * w_vis[0]
        for i in range(4):
            p = apply(ix[...], rows[i * G:(i + 1) * G, :])
            side = i // 2
            term = v * p
            if not first:
                term = term + prior[side][i % 2, :, lanes]
            (home, away)[side][i % 2, :, lanes] = term
            o = ours(i, lanes) * wo[i] * p
            total = o if total is None else total + o
        back[:, lanes] = total
        if first:
            p = pick(gj, lanes) * apply(ix[...], rows[4 * G:5 * G, :])
            home[gi & 1, :, lanes] = home[gi & 1, :, lanes] + p * wg
            away[gi & 1, :, lanes] = away[gi & 1, :, lanes] + p * wt
        return 0

    lax.fori_loop(0, G // YB, leave, 0)


def pair_solver(first, *args):
    return pl.pallas_call(
        functools.partial(kernel, first),
        out_shape=[f32(2, G, ROW), f32(2, G, ROW), f32(G, ROW)],
        in_specs=[SM] * 4 + [VM] * (len(args) - 4),
        out_specs=[VM] * 3,
        scratch_shapes=[
            pltpu.VMEM((G, G, WIDE), jnp.float32),
            pltpu.VMEM((WIDE, LB), jnp.float32),
            pltpu.VMEM((LB, WIDE), jnp.float32),
            pltpu.VMEM((YB, G, WIDE), jnp.float32),
        ],
        compiler_params=pltpu.CompilerParams(vmem_limit_bytes=40 << 20),
        cost_estimate=pl.CostEstimate(flops=5 * 10**9, bytes_accessed=10**7, transcendentals=0),
    )(*args)


def stacked(m):
    top = lax.reduce_precision(m, 8, 7)
    hi = top.astype(jnp.bfloat16)
    lo = (m - top).astype(jnp.bfloat16)
    return jnp.concatenate([jnp.concatenate([hi, hi], 1), jnp.concatenate([lo, jnp.zeros_like(lo)], 1)], 0)


def plain_basis():
    k = np.arange(G)
    m = np.where(k <= G // 2, k, k - G // 2)
    ang = (2.0 * np.pi / G) * (m[:, None] * k[None, :] % G)
    return np.where((k <= G // 2)[:, None], np.cos(ang), np.sin(ang)).astype(np.float32)


def basis(place):
    k = jnp.arange(G, dtype=jnp.int32)
    m = jnp.where(k <= G // 2, k, k - G // 2)
    ang = (2.0 * np.pi / G) * ((m[:, None] * place[None, :]) % G).astype(jnp.float32)
    return jnp.where((k <= G // 2)[:, None], jnp.cos(ang), jnp.sin(ang))


def kernel_table(cutoff):
    def freq(shape, dim):
        k = lax.broadcasted_iota(jnp.int32, shape, dim) % G
        m = jnp.where(k <= G // 2, k, k - G // 2)
        return m * m, jnp.where((k == 0) | (k == G // 2), 1.0, 2.0)

    (a, wa), (b, wb), (c, wc) = freq((G, 1, 1), 0), freq((1, G, 1), 1), freq((1, 1, WIDE), 2)
    n = a + b + c
    ratios = n.astype(jnp.float32) * 0.5
    screen = jnp.where(n > 0, (1.0 - jnp.exp(-ratios)) / jnp.maximum(ratios, 0.5), 1.0)
    return jnp.where(n <= cutoff, 4.0 * screen * (wa * wb * wc / float(G**3)), 0.0)


def ring(block, axis, source):
    return lax.ppermute(block, axis, [(source(i), i) for i in range(lax.axis_size(axis))])


def partner(i):
    return (i + 8) % 16


def along(k):
    return lambda i: i // 8 * 8 + (i + k) % 8


def twin_of(i):
    return i ^ 1


OFFSETS = ((1, 0), (0, 1), (1, 1), (1, 3), (2, 1), (3, 2), None, (2, 0))
ORDER = ((2, 4, 6, 7, 0, 1, 3, 5), (0, 1, 3, 5, 2, 4, 6, 7))
MATCH = (5, 3, 2, 1, 4, 0, 6, 7)


def class_of(core, z, v):
    kind = ORDER[v][z]
    return MATCH[kind] if core else kind


def source_chip(kind, x, y):
    if kind == 6:
        px, py = x // 2, y // 2
        px, py = {(0, 0): (0, 1), (0, 1): (1, 0), (1, 0): (1, 1), (1, 1): (0, 0)}[(px, py)]
        return px * 2 + x % 2, py * 2 + y % 2
    dx, dy = OFFSETS[kind]
    return (x + dx) % 4, (y + dy) % 4


def visit_route(v, both_ways=True):
    pairs = []
    for b in range(16):
        for g in range(16):
            core, z = b % 2, g % 8
            kind = class_of(core, z, v)
            x, y = source_chip(kind, b // 2 % 4, g // 8 * 2 + b // 8)
            if both_ways or kind != 7:
                pairs.append(((((y % 2) * 4 + x) * 2 + core) * 16 + y // 2 * 8 + z, b * 16 + g))
    return pairs


def returned(back, v):
    return lax.ppermute(back, ("band", "grid"), [(d, s) for s, d in visit_route(v, False)])


def gather_blocks(b0):
    got = {0: b0}
    for k in (2, 6, 1, 7):
        got[k] = ring(b0, "grid", along(k))
    got[3] = ring(got[2], "grid", along(1))
    got[5] = ring(got[6], "grid", along(7))
    far = ring(got[2][:8], "grid", along(2))
    rest = ring(got[6][8:], "grid", along(6))
    got[4] = jnp.concatenate([far, rest], axis=0)
    return [got[k] for k in range(8)]


def scatter_blocks(part):
    return [part[0]] + [ring(part[k], "grid", along(-k)) for k in (4, 3, 5, 2, 6, 1, 7)]


def on_device(orbitals, occupation, cutoff):
    axes = ("band", "grid")
    g = lax.axis_index("grid")
    core = lax.axis_index("band") % 2
    z, y = g % 8, g // 8
    y1 = y.reshape(1)
    give = lax.dynamic_slice(orbitals, (2 * (1 - y), 0, 0), (2, 3, ROW))
    came = ring(give, "grid", partner)
    blk = small_call(pack_body, [f32(24, HALF)], y1, orbitals, came, scalars=1)

    got = gather_blocks(blk)
    own, *lone = small_call(assemble_body, [f32(2, G, ROW), f32(G, ROW), f32(G, ROW)], *got)
    first = lax.ppermute(lone[0], axes, visit_route(0))
    twin = ring(own, "band", twin_of)

    late = lax.optimization_barrier((occupation, own))[0]
    weights = late.astype(jnp.float32) * -0.5
    w_own = lax.dynamic_slice(weights, (2 * y,), (2,))
    w_twin = ring(w_own, "band", twin_of)
    w_first = lax.ppermute(w_own[:1], axes, visit_route(0))
    held, w_held, first = lax.optimization_barrier((lone[1], w_own[1:], first))
    second = lax.ppermute(held, axes, visit_route(1))
    w_second = lax.ppermute(w_held, axes, visit_route(1))

    e = z * 2 + core
    once = [z == ORDER[v].index(7) for v in range(2)]
    idx = jnp.stack([e // 4 ^ 2 * core, e % 4 ^ 2 * core] + [o.astype(jnp.int32) for o in once])
    r = jnp.arange(G, dtype=jnp.int32)
    turned = basis(3 * (r // 3 % 2 * 8 + (z + r // 6) % 8) + r % 3)
    plain = jnp.asarray(plain_basis())
    tables = (kernel_table(cutoff), stacked(turned), stacked(turned.T), stacked(plain), stacked(plain.T))
    home, away, back = pair_solver(True, idx, w_own, w_twin, w_first, own, twin, first, *tables)
    ret0 = returned(back, 0)
    home, away, back = pair_solver(False, idx, w_own, w_twin, w_second, own, twin, second, *tables, home, away)
    ret1 = returned(back, 1)
    swapped = ring(away, "band", twin_of)
    part = small_call(disperse_body, [f32(24, HALF)] * 8, home, swapped, ret0, ret1)
    keep, give = small_call(unpack_body, [f32(2, 3, ROW)] * 2, y1, *scatter_blocks(part), scalars=1)
    came = ring(give, "grid", partner)
    return jnp.concatenate([jnp.where(y == 0, keep, came), jnp.where(y == 0, came, keep)], axis=0)


def solution(mesh):
    placed = (P("band", "grid", None), P("band"), P())
    return jax.shard_map(
        on_device, mesh=mesh, in_specs=placed, out_specs=P("band", "grid", None), check_vma=False
    )
```

profile of v0, /device:TPU:1, one launch (start us, length us, event | category | flops | bytes accessed | tf_op | source)
XLA Modules:
  0.0 147.4 jit_solution(2898216427365876589)
XLA Ops:
  1.0 3.8 %collective-permute-start = (f32[2,3,2304]{2,1,0:T(4,128)S(1)}, f32[2,3,2304]{2,1,0:T(4,128)S(1)}, u32[]{:S(2)}, u32[]{:S(2)}) collective-permute-start(f32[2,3,2304]{2,1,0:T(4,128)S(1)} %constant_dynamic-slice_fusion), channel_id=1, source_target_pairs={{8,0},{9,1},{10,2},{11,3},{12,4},{13,5},{14,6},{15,7},{0,8},{1,9},... | collective-permute-start | bytes 165896 | tf_op jit(solution)/shard_map/ppermute | solution.py:219
  7.2 1.6 %shard_map.46.refs_0_ = f32[24,1152]{1,0:T(8,128)} custom-call(s32[1]{0:T(128)} %bitcast.y, f32[4,3,2304]{2,1,0:T(4,128)} %copy-done.4, f32[2,3,2304]{2,1,0:T(4,128)} %copy-done.21), custom_call_target="tpu_custom_call" | custom-call | flops 1000000 | bytes 1000000 | tf_op jit(solution)/shard_map/pallas_call | solution.py:39
  8.8 3.0 %collective-permute-start.5 = (f32[24,1152]{1,0:T(8,128)}, f32[24,1152]{1,0:T(8,128)S(1)}, u32[]{:S(2)}, u32[]{:S(2)}) collective-permute-start(f32[24,1152]{1,0:T(8,128)} %shard_map.46.refs_0_), channel_id=1, source_target_pairs={{6,0},{7,1},{0,2},{1,3},{2,4},{3,5},{4,6},{5,7},{14,8},{15,9},{8,1... | collective-permute-start | bytes 331784 | tf_op jit(solution)/shard_map/ppermute | solution.py:219
  11.9 3.0 %collective-permute-start.2 = (f32[24,1152]{1,0:T(8,128)}, f32[24,1152]{1,0:T(8,128)S(1)}, u32[]{:S(2)}, u32[]{:S(2)}) collective-permute-start(f32[24,1152]{1,0:T(8,128)} %shard_map.46.refs_0_), channel_id=1, source_target_pairs={{2,0},{3,1},{4,2},{5,3},{6,4},{7,5},{0,6},{1,7},{10,8},{11,9},{12,... | collective-permute-start | bytes 331784 | tf_op jit(solution)/shard_map/ppermute | solution.py:219
  14.9 2.4 %collective-permute-done.5.refs_6_ = f32[24,1152]{1,0:T(8,128)S(1)} collective-permute-done((f32[24,1152]{1,0:T(8,128)}, f32[24,1152]{1,0:T(8,128)S(1)}, u32[]{:S(2)}, u32[]{:S(2)}) %collective-permute-start.5) | collective-permute-done | bytes 110624 | tf_op jit(solution)/shard_map/ppermute | solution.py:219
  17.4 1.4 collective-permute-start.6
  18.7 1.3 collective-permute-done.2.refs_2_
  20.0 2.4 %collective-permute-start.4 = (f32[8,1152]{1,0:T(8,128)S(1)}, f32[8,1152]{1,0:T(8,128)S(1)}, u32[]{:S(2)}, u32[]{:S(2)}) collective-permute-start(f32[8,1152]{1,0:T(8,128)S(1)} %slice.16), channel_id=1, source_target_pairs={{2,0},{3,1},{4,2},{5,3},{6,4},{7,5},{0,6},{1,7},{10,8},{11,9},{12,... | collective-permute-start | bytes 110600 | tf_op jit(solution)/shard_map/ppermute | solution.py:219
  23.1 1.3 collective-permute-start.1
  25.6 1.5 collective-permute-start.3
  29.4 1.9 %collective-permute-done.3.refs_3_ = f32[24,1152]{1,0:T(8,128)S(1)} collective-permute-done((f32[24,1152]{1,0:T(8,128)S(1)}, f32[24,1152]{1,0:T(8,128)S(1)}, u32[]{:S(2)}, u32[]{:S(2)}) %collective-permute-start.3) | collective-permute-done | bytes 110624 | tf_op jit(solution)/shard_map/ppermute | solution.py:219
  32.6 2.7 %shard_map.47 = (f32[2,48,2304]{2,1,0:T(8,128)}, f32[48,2304]{1,0:T(8,128)}, f32[48,2304]{1,0:T(8,128)}) custom-call(f32[24,1152]{1,0:T(8,128)} %shard_map.46.refs_0_, f32[24,1152]{1,0:T(8,128)} %copy-done.15, f32[24,1152]{1,0:T(8,128)} %copy-done.9, f32[24,1152]{1,0:T(8,128)} %copy-done.18, f32[24,1152]{1,0:T(8,128)} %pad_maximum_fusion.1.refs_4_, ...), custom_call_target="tpu_custom_call" | custom-call | flops 1000000 | bytes 1000000 | tf_op jit(solution)/shard_map/pallas_call | solution.py:39
  35.3 5.0 %collective-permute-start.12 = (f32[2,48,2304]{2,1,0:T(8,128)}, f32[2,48,2304]{2,1,0:T(8,128)S(1)}, u32[]{:S(2)}, u32[]{:S(2)}) collective-permute-start(f32[2,48,2304]{2,1,0:T(8,128)} %get-tuple-element.28.own), channel_id=1, source_target_pairs={{16,0},{0,16},{48,32},{32,48},{80,64},{64,80},{112,96},{96,112},{1... | collective-permute-start | bytes 2654216 | tf_op jit(solution)/shard_map/ppermute | solution.py:219
  40.3 1.4 fusion.9.ktab
  41.8 5.0 %collective-permute-start.10 = (f32[48,2304]{1,0:T(8,128)S(1)}, f32[48,2304]{1,0:T(8,128)S(1)}, u32[]{:S(2)}, u32[]{:S(2)}) collective-permute-start(f32[48,2304]{1,0:T(8,128)S(1)} %copy-done.23), channel_id=1, source_target_pairs={{160,0},{193,1},{10,2},{67,3},{36,4},{133,5},{174,6},{111,7},{168,... | collective-permute-start | bytes 1327112 | tf_op jit(solution)/shard_map/ppermute | solution.py:297
  48.5 7.8 %collective-permute-done.10.vis = f32[48,2304]{1,0:T(8,128)S(1)} collective-permute-done((f32[48,2304]{1,0:T(8,128)S(1)}, f32[48,2304]{1,0:T(8,128)S(1)}, u32[]{:S(2)}, u32[]{:S(2)}) %collective-permute-start.10) | collective-permute-done | bytes 442400 | tf_op jit(solution)/shard_map/ppermute | solution.py:297
  56.3 2.0 %collective-permute-start.13 = (f32[48,2304]{1,0:T(8,128)S(1)}, f32[48,2304]{1,0:T(8,128)S(1)}, u32[]{:S(2)}, u32[]{:S(2)}) collective-permute-start(f32[48,2304]{1,0:T(8,128)S(1)} %copy-done.22), channel_id=1, source_target_pairs={{32,0},{129,1},{170,2},{107,3},{164,4},{197,5},{14,6},{71,7},{40,8... | collective-permute-start | bytes 1327112 | tf_op jit(solution)/shard_map/ppermute | solution.py:306
  59.3 12.9 %shard_map.48 = (f32[2,48,2304]{2,1,0:T(8,128)S(1)}, f32[2,48,2304]{2,1,0:T(8,128)S(1)}, f32[48,2304]{1,0:T(8,128)S(1)}) custom-call(s32[4]{0:T(128)S(1)} %pad_add_fusion.idx, f32[2]{0:T(128)S(1)} %dynamic_slice.7.w_own, f32[2]{0:T(128)S(1)} %collective-permute-done.9.w_twin, f32[1]{0:T(128)} %collective-permute-done.14.w_vis, f32[2,48,2304]{2,1,0:T(8,128)S(1)} %copy-done.1, ...), custom_call_target="tpu_custom_call" | custom-call | flops 5000000000 | bytes 10000000 | tf_op jit(solution)/shard_map/pallas_call | solution.py:168
  72.2 12.7 %shard_map.49 = (f32[2,48,2304]{2,1,0:T(8,128)S(1)}, f32[2,48,2304]{2,1,0:T(8,128)S(1)}, f32[48,2304]{1,0:T(8,128)S(1)}) custom-call(s32[4]{0:T(128)S(1)} %pad_add_fusion.idx, f32[2]{0:T(128)S(1)} %dynamic_slice.7.w_own, f32[2]{0:T(128)S(1)} %collective-permute-done.9.w_twin, f32[1]{0:T(128)} %collective-permute-done.11.w_vis, f32[2,48,2304]{2,1,0:T(8,128)S(1)} %copy-done.1, ...), custom_call_target="tpu_custom_call" | custom-call | flops 5000000000 | bytes 10000000 | tf_op jit(solution)/shard_map/pallas_call | solution.py:168
  86.0 6.0 %collective-permute-start.17 = (f32[48,2304]{1,0:T(8,128)S(1)}, f32[48,2304]{1,0:T(8,128)S(1)}, u32[]{:S(2)}, u32[]{:S(2)}) collective-permute-start(f32[48,2304]{1,0:T(8,128)S(1)} %get-tuple-element.40), channel_id=1, source_target_pairs={{0,32},{1,129},{2,170},{3,107},{4,164},{5,197},{6,14},{8,40},{9,13... | collective-permute-start | bytes 1327112 | tf_op jit(solution)/shard_map/ppermute | solution.py:266
  91.9 3.3 %collective-permute-start.16 = (f32[48,2304]{1,0:T(8,128)S(1)}, f32[48,2304]{1,0:T(8,128)S(1)}, u32[]{:S(2)}, u32[]{:S(2)}) collective-permute-start(f32[48,2304]{1,0:T(8,128)S(1)} %get-tuple-element.39), channel_id=1, source_target_pairs={{0,160},{1,193},{2,10},{4,36},{5,133},{6,174},{7,111},{8,168},{9,2... | collective-permute-start | bytes 1327112 | tf_op jit(solution)/shard_map/ppermute | solution.py:266
  95.2 3.1 %collective-permute-done.17.c1 = f32[48,2304]{1,0:T(8,128)S(1)} collective-permute-done((f32[48,2304]{1,0:T(8,128)S(1)}, f32[48,2304]{1,0:T(8,128)S(1)}, u32[]{:S(2)}, u32[]{:S(2)}) %collective-permute-start.17) | collective-permute-done | bytes 442400 | tf_op jit(solution)/shard_map/ppermute | solution.py:266
  98.3 11.1 %collective-permute-done.16.c0 = f32[48,2304]{1,0:T(8,128)S(1)} collective-permute-done((f32[48,2304]{1,0:T(8,128)S(1)}, f32[48,2304]{1,0:T(8,128)S(1)}, u32[]{:S(2)}, u32[]{:S(2)}) %collective-permute-start.16) | collective-permute-done | bytes 442400 | tf_op jit(solution)/shard_map/ppermute | solution.py:266
  110.4 2.9 %shard_map.50 = (f32[24,1152]{1,0:T(8,128)}, f32[24,1152]{1,0:T(8,128)}, f32[24,1152]{1,0:T(8,128)}, f32[24,1152]{1,0:T(8,128)}, f32[24,1152]{1,0:T(8,128)}, /*i...) custom-call(f32[2,48,2304]{2,1,0:T(8,128)} %copy-done, f32[2,48,2304]{2,1,0:T(8,128)} %copy-done.5, ...), custom_call_target="tpu_custom_call" | custom-call | flops 1000000 | bytes 1000000 | tf_op jit(solution)/shard_map/pallas_call | solution.py:39
  113.4 4.5 %collective-permute-start.20 = (f32[24,1152]{1,0:T(8,128)}, f32[24,1152]{1,0:T(8,128)S(1)}, u32[]{:S(2)}, u32[]{:S(2)}) collective-permute-start(f32[24,1152]{1,0:T(8,128)} %get-tuple-element.44), channel_id=1, source_target_pairs={{3,0},{4,1},{5,2},{6,3},{7,4},{0,5},{1,6},{2,7},{11,8},{12,9},{13,... | collective-permute-start | bytes 331784 | tf_op jit(solution)/shard_map/ppermute | solution.py:219
  117.8 2.4 %collective-permute-start.21 = (f32[24,1152]{1,0:T(8,128)}, f32[24,1152]{1,0:T(8,128)S(1)}, u32[]{:S(2)}, u32[]{:S(2)}) collective-permute-start(f32[24,1152]{1,0:T(8,128)} %get-tuple-element.45), channel_id=1, source_target_pairs={{6,0},{7,1},{0,2},{1,3},{2,4},{3,5},{4,6},{5,7},{14,8},{15,9},{8,1... | collective-permute-start | bytes 331784 | tf_op jit(solution)/shard_map/ppermute | solution.py:219
  120.2 3.2 %collective-permute-start.22 = (f32[24,1152]{1,0:T(8,128)}, f32[24,1152]{1,0:T(8,128)S(1)}, u32[]{:S(2)}, u32[]{:S(2)}) collective-permute-start(f32[24,1152]{1,0:T(8,128)} %get-tuple-element.46), channel_id=1, source_target_pairs={{2,0},{3,1},{4,2},{5,3},{6,4},{7,5},{0,6},{1,7},{10,8},{11,9},{12,... | collective-permute-start | bytes 331784 | tf_op jit(solution)/shard_map/ppermute | solution.py:219
  123.7 2.3 %collective-permute-done.19.refs_2_ = f32[24,1152]{1,0:T(8,128)S(1)} collective-permute-done((f32[24,1152]{1,0:T(8,128)}, f32[24,1152]{1,0:T(8,128)S(1)}, u32[]{:S(2)}, u32[]{:S(2)}) %collective-permute-start.19) | collective-permute-done | bytes 110624 | tf_op jit(solution)/shard_map/ppermute | solution.py:219
  126.1 9.4 %collective-permute-done.21.refs_4_ = f32[24,1152]{1,0:T(8,128)S(1)} collective-permute-done((f32[24,1152]{1,0:T(8,128)}, f32[24,1152]{1,0:T(8,128)S(1)}, u32[]{:S(2)}, u32[]{:S(2)}) %collective-permute-start.21) | collective-permute-done | bytes 110624 | tf_op jit(solution)/shard_map/ppermute | solution.py:219
  135.5 2.6 %collective-permute-done.23.refs_6_ = f32[24,1152]{1,0:T(8,128)S(1)} collective-permute-done((f32[24,1152]{1,0:T(8,128)}, f32[24,1152]{1,0:T(8,128)S(1)}, u32[]{:S(2)}, u32[]{:S(2)}) %collective-permute-start.23) | collective-permute-done | bytes 110624 | tf_op jit(solution)/shard_map/ppermute | solution.py:219
  138.8 2.0 %shard_map.51 = (f32[2,3,2304]{2,1,0:T(4,128)}, f32[2,3,2304]{2,1,0:T(4,128)}) custom-call(s32[1]{0:T(128)} %bitcast.y, f32[24,1152]{1,0:T(8,128)} %get-tuple-element.41.refs_0_, f32[24,1152]{1,0:T(8,128)} %copy-done.10, f32[24,1152]{1,0:T(8,128)} %copy-done.11, f32[24,1152]{1,0:T(8,128)} %copy-done.12, f32[24,1152]{1,0:T(8,128)} %copy-done.13, ...), custom_call_target="tpu_custom_call" | custom-call | flops 1000000 | bytes 1000000 | tf_op jit(solution)/shard_map/pallas_call | solution.py:39
  140.8 4.9 %collective-permute-done.25 = f32[2,3,2304]{2,1,0:T(4,128)S(1)} collective-permute-done((f32[2,3,2304]{2,1,0:T(4,128)}, f32[2,3,2304]{2,1,0:T(4,128)S(1)}, u32[]{:S(2)}, u32[]{:S(2)}) %collective-permute-start.25) | collective-permute-done | bytes 55328 | tf_op jit(solution)/shard_map/ppermute | solution.py:219
  (100 shorter events, 15.7 us)
Async XLA Ops:
  0.0 46.9 %copy-start.24 = (s32[4]{0:T(128)S(1)}, s32[4]{0:T(128)}, u32[]{:S(2)}) copy-start(s32[4]{0:T(128)} %param.5) | copy-start | bytes 52
  0.0 59.3 %copy-start.2 = (bf16[96,96]{1,0:T(8,128)(2,1)S(1)}, bf16[96,96]{1,0:T(8,128)(2,1)}, u32[]{:S(2)}) copy-start(bf16[96,96]{1,0:T(8,128)(2,1)} %constant.180.fz) | copy-start | bytes 55300
  0.0 59.3 %copy-start.3 = (bf16[96,96]{1,0:T(8,128)(2,1)S(1)}, bf16[96,96]{1,0:T(8,128)(2,1)}, u32[]{:S(2)}) copy-start(bf16[96,96]{1,0:T(8,128)(2,1)} %constant.188.iz) | copy-start | bytes 55300
  1.0 5.6 %collective-permute-start = (f32[2,3,2304]{2,1,0:T(4,128)S(1)}, f32[2,3,2304]{2,1,0:T(4,128)S(1)}, u32[]{:S(2)}, u32[]{:S(2)}) collective-permute-start(f32[2,3,2304]{2,1,0:T(4,128)S(1)} %constant_dynamic-slice_fusion), channel_id=1, source_target_pairs={{8,0},{9,1},{10,2},{11,3},{12,4},{13,5},{14,6},{15,7},{0,8},{1,9},... | collective-permute-start | bytes 165896 | tf_op jit(solution)/shard_map/ppermute | solution.py:219
  8.8 8.5 %collective-permute-start.5 = (f32[24,1152]{1,0:T(8,128)}, f32[24,1152]{1,0:T(8,128)S(1)}, u32[]{:S(2)}, u32[]{:S(2)}) collective-permute-start(f32[24,1152]{1,0:T(8,128)} %shard_map.46.refs_0_), channel_id=1, source_target_pairs={{6,0},{7,1},{0,2},{1,3},{2,4},{3,5},{4,6},{5,7},{14,8},{15,9},{8,1... | collective-permute-start | bytes 331784 | tf_op jit(solution)/shard_map/ppermute | solution.py:219
  11.9 8.1 %collective-permute-start.2 = (f32[24,1152]{1,0:T(8,128)}, f32[24,1152]{1,0:T(8,128)S(1)}, u32[]{:S(2)}, u32[]{:S(2)}) collective-permute-start(f32[24,1152]{1,0:T(8,128)} %shard_map.46.refs_0_), channel_id=1, source_target_pairs={{2,0},{3,1},{4,2},{5,3},{6,4},{7,5},{0,6},{1,7},{10,8},{11,9},{12,... | collective-permute-start | bytes 331784 | tf_op jit(solution)/shard_map/ppermute | solution.py:219
  17.4 9.7 %collective-permute-start.6 = (f32[16,1152]{1,0:T(8,128)S(1)}, f32[16,1152]{1,0:T(8,128)S(1)}, u32[]{:S(2)}, u32[]{:S(2)}) collective-permute-start(f32[16,1152]{1,0:T(8,128)S(1)} %slice.17), channel_id=1, source_target_pairs={{6,0},{7,1},{0,2},{1,3},{2,4},{3,5},{4,6},{5,7},{14,8},{15,9},{8,1... | collective-permute-start | bytes 221192 | tf_op jit(solution)/shard_map/ppermute | solution.py:219
  20.0 7.1 %collective-permute-start.4 = (f32[8,1152]{1,0:T(8,128)S(1)}, f32[8,1152]{1,0:T(8,128)S(1)}, u32[]{:S(2)}, u32[]{:S(2)}) collective-permute-start(f32[8,1152]{1,0:T(8,128)S(1)} %slice.16), channel_id=1, source_target_pairs={{2,0},{3,1},{4,2},{5,3},{6,4},{7,5},{0,6},{1,7},{10,8},{11,9},{12,... | collective-permute-start | bytes 110600 | tf_op jit(solution)/shard_map/ppermute | solution.py:219
  23.1 5.6 %collective-permute-start.1 = (f32[24,1152]{1,0:T(8,128)}, f32[24,1152]{1,0:T(8,128)S(1)}, u32[]{:S(2)}, u32[]{:S(2)}) collective-permute-start(f32[24,1152]{1,0:T(8,128)} %shard_map.46.refs_0_), channel_id=1, source_target_pairs={{1,0},{2,1},{3,2},{4,3},{5,4},{6,5},{7,6},{0,7},{9,8},{10,9},{11,1... | collective-permute-start | bytes 331784 | tf_op jit(solution)/shard_map/ppermute | solution.py:219
  24.4 5.0 %collective-permute-start.8 = (f32[24,1152]{1,0:T(8,128)}, f32[24,1152]{1,0:T(8,128)S(1)}, u32[]{:S(2)}, u32[]{:S(2)}) collective-permute-start(f32[24,1152]{1,0:T(8,128)} %shard_map.46.refs_0_), channel_id=1, source_target_pairs={{7,0},{0,1},{1,2},{2,3},{3,4},{4,5},{5,6},{6,7},{15,8},{8,9},{9,10... | collective-permute-start | bytes 331784 | tf_op jit(solution)/shard_map/ppermute | solution.py:219
  25.6 5.7 %collective-permute-start.3 = (f32[24,1152]{1,0:T(8,128)S(1)}, f32[24,1152]{1,0:T(8,128)S(1)}, u32[]{:S(2)}, u32[]{:S(2)}) collective-permute-start(f32[24,1152]{1,0:T(8,128)S(1)} %collective-permute-done.2.refs_2_), channel_id=1, source_target_pairs={{1,0},{2,1},{3,2},{4,3},{5,4},{6,5},{7,6},{0,7},{9,8},{10,9},{11,1... | collective-permute-start | bytes 331784 | tf_op jit(solution)/shard_map/ppermute | solution.py:219
  27.1 4.8 %collective-permute-start.7 = (f32[24,1152]{1,0:T(8,128)S(1)}, f32[24,1152]{1,0:T(8,128)S(1)}, u32[]{:S(2)}, u32[]{:S(2)}) collective-permute-start(f32[24,1152]{1,0:T(8,128)S(1)} %collective-permute-done.5.refs_6_), channel_id=1, source_target_pairs={{7,0},{0,1},{1,2},{2,3},{3,4},{4,5},{5,6},{6,7},{15,8},{8,9},{9,10... | collective-permute-start | bytes 331784 | tf_op jit(solution)/shard_map/ppermute | solution.py:219
  35.3 21.0 %copy-start.22 = (f32[48,2304]{1,0:T(8,128)S(1)}, f32[48,2304]{1,0:T(8,128)}, u32[]{:S(2)}) copy-start(f32[48,2304]{1,0:T(8,128)} %get-tuple-element.33) | copy-start | bytes 1327108
  35.3 24.0 %copy-start.1 = (f32[2,48,2304]{2,1,0:T(8,128)S(1)}, f32[2,48,2304]{2,1,0:T(8,128)}, u32[]{:S(2)}) copy-start(f32[2,48,2304]{2,1,0:T(8,128)} %get-tuple-element.28.own) | copy-start | bytes 2654212
  35.3 24.0 %collective-permute-start.12 = (f32[2,48,2304]{2,1,0:T(8,128)}, f32[2,48,2304]{2,1,0:T(8,128)S(1)}, u32[]{:S(2)}, u32[]{:S(2)}) collective-permute-start(f32[2,48,2304]{2,1,0:T(8,128)} %get-tuple-element.28.own), channel_id=1, source_target_pairs={{16,0},{0,16},{48,32},{32,48},{80,64},{64,80},{112,96},{96,112},{1... | collective-permute-start | bytes 2654216 | tf_op jit(solution)/shard_map/ppermute | solution.py:219
  41.8 14.5 %collective-permute-start.10 = (f32[48,2304]{1,0:T(8,128)S(1)}, f32[48,2304]{1,0:T(8,128)S(1)}, u32[]{:S(2)}, u32[]{:S(2)}) collective-permute-start(f32[48,2304]{1,0:T(8,128)S(1)} %copy-done.23), channel_id=1, source_target_pairs={{160,0},{193,1},{10,2},{67,3},{36,4},{133,5},{174,6},{111,7},{168,... | collective-permute-start | bytes 1327112 | tf_op jit(solution)/shard_map/ppermute | solution.py:297
  46.9 12.4 %collective-permute-start.9 = (f32[2]{0:T(128)S(1)}, f32[2]{0:T(128)S(1)}, u32[]{:S(2)}, u32[]{:S(2)}) collective-permute-start(f32[2]{0:T(128)S(1)} %dynamic_slice.7.w_own), channel_id=1, source_target_pairs={{16,0},{0,16},{48,32},{32,48},{80,64},{64,80},{112,96},{96,112},{1... | collective-permute-start | bytes 32 | tf_op jit(solution)/shard_map/ppermute | solution.py:219
  47.8 11.5 %collective-permute-start.14 = (f32[1]{0:T(128)}, f32[1]{0:T(128)}, u32[]{:S(2)}, u32[]{:S(2)}) collective-permute-start(f32[1]{0:T(128)} %get-tuple-element.57), channel_id=1, source_target_pairs={{160,0},{193,1},{10,2},{67,3},{36,4},{133,5},{174,6},{111,7},{168,... | collective-permute-start | bytes 20 | tf_op jit(solution)/shard_map/ppermute | solution.py:304
  56.3 15.9 %collective-permute-start.13 = (f32[48,2304]{1,0:T(8,128)S(1)}, f32[48,2304]{1,0:T(8,128)S(1)}, u32[]{:S(2)}, u32[]{:S(2)}) collective-permute-start(f32[48,2304]{1,0:T(8,128)S(1)} %copy-done.22), channel_id=1, source_target_pairs={{32,0},{129,1},{170,2},{107,3},{164,4},{197,5},{14,6},{71,7},{40,8... | collective-permute-start | bytes 1327112 | tf_op jit(solution)/shard_map/ppermute | solution.py:306
  58.3 13.9 %collective-permute-start.11 = (f32[1]{0:T(128)}, f32[1]{0:T(128)}, u32[]{:S(2)}, u32[]{:S(2)}) collective-permute-start(f32[1]{0:T(128)} %get-tuple-element.32), channel_id=1, source_target_pairs={{32,0},{129,1},{170,2},{107,3},{164,4},{197,5},{14,6},{71,7},{40,8... | collective-permute-start | bytes 20 | tf_op jit(solution)/shard_map/ppermute | solution.py:307
  85.9 23.4 %collective-permute-start.15 = (f32[2,48,2304]{2,1,0:T(8,128)S(1)}, f32[2,48,2304]{2,1,0:T(8,128)S(1)}, u32[]{:S(2)}, u32[]{:S(2)}) collective-permute-start(f32[2,48,2304]{2,1,0:T(8,128)S(1)} %get-tuple-element.38), channel_id=1, source_target_pairs={{16,0},{0,16},{48,32},{32,48},{80,64},{64,80},{112,96},{96,112},{1... | collective-permute-start | bytes 2654216 | tf_op jit(solution)/shard_map/ppermute | solution.py:219
  86.0 12.3 %collective-permute-start.17 = (f32[48,2304]{1,0:T(8,128)S(1)}, f32[48,2304]{1,0:T(8,128)S(1)}, u32[]{:S(2)}, u32[]{:S(2)}) collective-permute-start(f32[48,2304]{1,0:T(8,128)S(1)} %get-tuple-element.40), channel_id=1, source_target_pairs={{0,32},{1,129},{2,170},{3,107},{4,164},{5,197},{6,14},{8,40},{9,13... | collective-permute-start | bytes 1327112 | tf_op jit(solution)/shard_map/ppermute | solution.py:266
  91.9 17.4 %collective-permute-start.16 = (f32[48,2304]{1,0:T(8,128)S(1)}, f32[48,2304]{1,0:T(8,128)S(1)}, u32[]{:S(2)}, u32[]{:S(2)}) collective-permute-start(f32[48,2304]{1,0:T(8,128)S(1)} %get-tuple-element.39), channel_id=1, source_target_pairs={{0,160},{1,193},{2,10},{4,36},{5,133},{6,174},{7,111},{8,168},{9,2... | collective-permute-start | bytes 1327112 | tf_op jit(solution)/shard_map/ppermute | solution.py:266
  113.3 10.1 %collective-permute-start.18 = (f32[24,1152]{1,0:T(8,128)}, f32[24,1152]{1,0:T(8,128)S(1)}, u32[]{:S(2)}, u32[]{:S(2)}) collective-permute-start(f32[24,1152]{1,0:T(8,128)} %get-tuple-element.42), channel_id=1, source_target_pairs={{4,0},{5,1},{6,2},{7,3},{0,4},{1,5},{2,6},{3,7},{12,8},{13,9},{14,... | collective-permute-start | bytes 331784 | tf_op jit(solution)/shard_map/ppermute | solution.py:219
  113.3 12.7 %collective-permute-start.19 = (f32[24,1152]{1,0:T(8,128)}, f32[24,1152]{1,0:T(8,128)S(1)}, u32[]{:S(2)}, u32[]{:S(2)}) collective-permute-start(f32[24,1152]{1,0:T(8,128)} %get-tuple-element.43), channel_id=1, source_target_pairs={{5,0},{6,1},{7,2},{0,3},{1,4},{2,5},{3,6},{4,7},{13,8},{14,9},{15,... | collective-permute-start | bytes 331784 | tf_op jit(solution)/shard_map/ppermute | solution.py:219
  113.4 12.8 %collective-permute-start.20 = (f32[24,1152]{1,0:T(8,128)}, f32[24,1152]{1,0:T(8,128)S(1)}, u32[]{:S(2)}, u32[]{:S(2)}) collective-permute-start(f32[24,1152]{1,0:T(8,128)} %get-tuple-element.44), channel_id=1, source_target_pairs={{3,0},{4,1},{5,2},{6,3},{7,4},{0,5},{1,6},{2,7},{11,8},{12,9},{13,... | collective-permute-start | bytes 331784 | tf_op jit(solution)/shard_map/ppermute | solution.py:219
  117.8 17.7 %collective-permute-start.21 = (f32[24,1152]{1,0:T(8,128)}, f32[24,1152]{1,0:T(8,128)S(1)}, u32[]{:S(2)}, u32[]{:S(2)}) collective-permute-start(f32[24,1152]{1,0:T(8,128)} %get-tuple-element.45), channel_id=1, source_target_pairs={{6,0},{7,1},{0,2},{1,3},{2,4},{3,5},{4,6},{5,7},{14,8},{15,9},{8,1... | collective-permute-start | bytes 331784 | tf_op jit(solution)/shard_map/ppermute | solution.py:219
  120.2 15.3 %collective-permute-start.22 = (f32[24,1152]{1,0:T(8,128)}, f32[24,1152]{1,0:T(8,128)S(1)}, u32[]{:S(2)}, u32[]{:S(2)}) collective-permute-start(f32[24,1152]{1,0:T(8,128)} %get-tuple-element.46), channel_id=1, source_target_pairs={{2,0},{3,1},{4,2},{5,3},{6,4},{7,5},{0,6},{1,7},{10,8},{11,9},{12,... | collective-permute-start | bytes 331784 | tf_op jit(solution)/shard_map/ppermute | solution.py:219
  123.4 14.7 %copy-start.10 = (f32[24,1152]{1,0:T(8,128)}, f32[24,1152]{1,0:T(8,128)S(1)}, u32[]{:S(2)}) copy-start(f32[24,1152]{1,0:T(8,128)S(1)} %collective-permute-done.18.refs_1_) | copy-start | bytes 331780
  123.4 14.7 %collective-permute-start.23 = (f32[24,1152]{1,0:T(8,128)}, f32[24,1152]{1,0:T(8,128)S(1)}, u32[]{:S(2)}, u32[]{:S(2)}) collective-permute-start(f32[24,1152]{1,0:T(8,128)} %get-tuple-element.47), channel_id=1, source_target_pairs={{7,0},{0,1},{1,2},{2,3},{3,4},{4,5},{5,6},{6,7},{15,8},{8,9},{9,10... | collective-permute-start | bytes 331784 | tf_op jit(solution)/shard_map/ppermute | solution.py:219
  126.0 12.1 %collective-permute-start.24 = (f32[24,1152]{1,0:T(8,128)}, f32[24,1152]{1,0:T(8,128)S(1)}, u32[]{:S(2)}, u32[]{:S(2)}) collective-permute-start(f32[24,1152]{1,0:T(8,128)} %get-tuple-element.48), channel_id=1, source_target_pairs={{1,0},{2,1},{3,2},{4,3},{5,4},{6,5},{7,6},{0,7},{9,8},{10,9},{11,1... | collective-permute-start | bytes 331784 | tf_op jit(solution)/shard_map/ppermute | solution.py:219
  140.8 4.9 %collective-permute-start.25 = (f32[2,3,2304]{2,1,0:T(4,128)}, f32[2,3,2304]{2,1,0:T(4,128)S(1)}, u32[]{:S(2)}, u32[]{:S(2)}) collective-permute-start(f32[2,3,2304]{2,1,0:T(4,128)} %get-tuple-element.50), channel_id=1, source_target_pairs={{8,0},{9,1},{10,2},{11,3},{12,4},{13,5},{14,6},{15,7},{0,8},{1,9},... | collective-permute-start | bytes 165896 | tf_op jit(solution)/shard_map/ppermute | solution.py:219
  (19 other events, 90.8 us)
where the time goes:
time: 148 us; the launch traced here: 147 us
  starting transfers between devices  51.5 us (35%)
  waiting for transfers between devices  50.1 us (34%)
  Pallas kernels  34.9 us (24%)
  local copies, waits for them, and re-layouts  6.28 us (4%)
  other arithmetic  3.69 us (2%)
    ppermute x20, starting transfers between devices, ring(): lax.ppermute(block, axis, [(source(i), i) for i in range(lax.axis_size(ax...  33.5 us
    ppermute x20, waiting for transfers between devices, ring(): lax.ppermute(block, axis, [(source(i), i) for i in range(lax.axis_size(ax...  28.3 us
    pallas_call x2, Pallas kernels, pair_solver(): pl.pallas_call(functools.partial(kernel, first), out_shape=[f32(2, G, ROW...  25.6 us
    ppermute x2, waiting for transfers between devices, returned(): lax.ppermute(back, ('band', 'grid'), [(d, s) for s, d in visit_route(v, F...  14.1 us
    pallas_call x4, Pallas kernels, small_call(): pl.pallas_call(body, out_shape=outs if many else outs[0], in_specs=[SM] *...  9.26 us
    ppermute x2, starting transfers between devices, returned(): lax.ppermute(back, ('band', 'grid'), [(d, s) for s, d in visit_route(v, F...  9.23 us
    ppermute x1, waiting for transfers between devices, on_device(): first = lax.ppermute(lone[0], axes, visit_route(0))  7.75 us
    ppermute x1, starting transfers between devices, on_device(): first = lax.ppermute(lone[0], axes, visit_route(0))  5 us
  transfers between devices with their start and end apart: 26, of which 14 were waited for; matrix products, arithmetic and copies ran while one was open for 2% of the time, Pallas kernels for 9%

commit v1 on v0

--- a/solution.py
+++ b/solution.py
@@ -41,6 +41,7 @@
         out_shape=outs if many else outs[0],
         in_specs=[SM] * scalars + [VM] * (len(args) - scalars),
         out_specs=[VM] * len(outs) if many else VM,
+        compiler_params=pltpu.CompilerParams(vmem_limit_bytes=8 << 20),
         cost_estimate=pl.CostEstimate(flops=10**6, bytes_accessed=10**6, transcendentals=0),
     )(*args)
 
@@ -96,7 +97,7 @@
 
 def kernel(first, idx, w_own, w_twin, w_vis, own, twin, vis, ktab, fx, ix, fz, iz, *refs):
     prior = () if first else refs[:2]
-    home, away, back, spec, rows, cols, zed = refs[len(prior):]
+    home, away, back, spec, *bufs = refs[len(prior):]
     gi, gj = idx[0], idx[1]
     once = idx[2] if first else idx[3]
     slots = 5 if first else 4
@@ -107,7 +108,7 @@
     def ours(i, lanes):
         return own[i, :, lanes] if i < 2 else twin[i - 2, :, lanes]
 
-    def enter(yb, _):
+    def enter_one(yb, rows, cols, zed):
         lanes = pl.ds(pl.multiple_of(yb * LB, LB), LB)
         for p in range(slots):
             r = ours(p, lanes) * vis[:, lanes] if p < 4 else pick(gi, lanes) * pick(gj, lanes)
@@ -117,18 +118,31 @@
         for y in range(YB):
             zed[y] = apply(fz[...], cols[y * G:(y + 1) * G, :])
         spec[:, pl.ds(pl.multiple_of(yb * YB, YB), YB), :] = jnp.swapaxes(zed[...], 0, 1)
+
+    def enter(k, _):
+        for u in range(3):
+            enter_one(k * 3 + u, *bufs[u % 2 * 3:u % 2 * 3 + 3])
         return 0
 
-    lax.fori_loop(0, G // YB, enter, 0)
+    lax.fori_loop(0, G // YB // 3, enter, 0)
+
+    def half_in(kz):
+        return apply(fz[...], spec[kz]) * ktab[kz]
+
+    for u in range(12):
+        bufs[-1][u] = half_in(u)
 
     def middle(k, _):
-        for u in range(4):
-            kz = k * 4 + u
-            s = apply(fz[...], spec[kz]) * ktab[kz]
-            spec[kz] = apply(iz[...], s)
+        done = [apply(iz[...], bufs[-1][u]) for u in range(12)]
+        for u in range(12):
+            bufs[-1][u] = half_in((k + 1) * 12 + u)
+        for u in range(12):
+            spec[k * 12 + u] = done[u]
         return 0
 
-    lax.fori_loop(0, G // 4, middle, 0)
+    lax.fori_loop(0, G // 12 - 1, middle, 0)
+    for u in range(12):
+        spec[G - 12 + u] = apply(iz[...], bufs[-1][u])
 
     keep = jnp.where(once != 0, 0.0, 1.0)
     wo = [w_own[0] * keep, w_own[1] * keep, w_twin[0] * keep, w_twin[1] * keep]
@@ -136,7 +150,7 @@
     wg = jnp.where(gi < 2, wj, 0.0)
     wt = jnp.where(gi < 2, 0.0, wj)
 
-    def leave(yb, _):
+    def leave_one(yb, rows, cols, zed):
         lanes = pl.ds(pl.multiple_of(yb * LB, LB), LB)
         zed[...] = jnp.swapaxes(spec[:, pl.ds(pl.multiple_of(yb * YB, YB), YB), :], 0, 1)
         for y in range(YB):
@@ -159,9 +173,13 @@
             p = pick(gj, lanes) * apply(ix[...], rows[4 * G:5 * G, :])
             home[gi & 1, :, lanes] = home[gi & 1, :, lanes] + p * wg
             away[gi & 1, :, lanes] = away[gi & 1, :, lanes] + p * wt
+
+    def leave(k, _):
+        for u in range(3):
+            leave_one(k * 3 + u, *bufs[u % 2 * 3:u % 2 * 3 + 3])
         return 0
 
-    lax.fori_loop(0, G // YB, leave, 0)
+    lax.fori_loop(0, G // YB // 3, leave, 0)
 
 
 def pair_solver(first, *args):
@@ -172,11 +190,12 @@
         out_specs=[VM] * 3,
         scratch_shapes=[
             pltpu.VMEM((G, G, WIDE), jnp.float32),
+        ] + [
             pltpu.VMEM((WIDE, LB), jnp.float32),
             pltpu.VMEM((LB, WIDE), jnp.float32),
             pltpu.VMEM((YB, G, WIDE), jnp.float32),
-        ],
-        compiler_params=pltpu.CompilerParams(vmem_limit_bytes=40 << 20),
+        ] * 2 + [pltpu.VMEM((12, G, WIDE), jnp.float32)],
+        compiler_params=pltpu.CompilerParams(vmem_limit_bytes=24 << 20),
         cost_estimate=pl.CostEstimate(flops=5 * 10**9, bytes_accessed=10**7, transcendentals=0),
     )(*args)
 

time: 148 us -> 126 us (0.85)
  Pallas kernels: 34.9 us -> 18.6 us
  local copies, waits for them, and re-layouts: 6.28 us -> 2.41 us
  other arithmetic: 3.69 us -> 2.17 us
    pallas_call x4, Pallas kernels: 9.26 us -> 0.74 us  [small_call(): pl.pallas_call(body, out_shape=outs if many else outs[0], in_specs=[SM] *...]
    pallas_call x2, Pallas kernels: 25.6 us -> 17.9 us  [pair_solver(): pl.pallas_call(functools.partial(kernel, first), out_shape=[f32(2, G, ROW...]
    unnamed x51 -> x7, local copies, waits for them, and re-layouts: 4.95 us -> 0.98 us
  transfers between devices with their start and end apart: 26 -> 26, of which waited for: 14 -> 14; matrix products, arithmetic and copies ran while one was open for 2% -> 2% of each run, Pallas kernels for 9% -> 7%
where the time goes in v1:
time: 126 us
  starting transfers between devices  51 us (40%)
  waiting for transfers between devices  50.9 us (40%)
  Pallas kernels  18.6 us (15%)
  local copies, waits for them, and re-layouts  2.41 us (2%)
  other arithmetic  2.17 us (2%)
    ppermute x20, starting transfers between devices, ring(): lax.ppermute(block, axis, [(source(i), i) for i in range(lax.axis_size(ax...  33.1 us
    ppermute x20, waiting for transfers between devices, ring(): lax.ppermute(block, axis, [(source(i), i) for i in range(lax.axis_size(ax...  29.1 us
    pallas_call x2, Pallas kernels, pair_solver(): pl.pallas_call(functools.partial(kernel, first), out_shape=[f32(2, G, ROW...  17.9 us
    ppermute x2, waiting for transfers between devices, returned(): lax.ppermute(back, ('band', 'grid'), [(d, s) for s, d in visit_route(v, F...  14.2 us
    ppermute x2, starting transfers between devices, returned(): lax.ppermute(back, ('band', 'grid'), [(d, s) for s, d in visit_route(v, F...  9.22 us
    ppermute x1, waiting for transfers between devices, on_device(): first = lax.ppermute(lone[0], axes, visit_route(0))  7.66 us
    ppermute x1, starting transfers between devices, on_device(): first = lax.ppermute(lone[0], axes, visit_route(0))  5.01 us
  transfers between devices with their start and end apart: 26, of which 14 were waited for; matrix products, arithmetic and copies ran while one was open for 2% of the time, Pallas kernels for 7%

profile of v1, /device:TPU:1, one launch (start us, length us, event | category | flops | bytes accessed | tf_op | source)
XLA Modules:
  0.0 126.0 jit_solution(4805057586696885590)
XLA Ops:
  1.0 3.8 %collective-permute-start = (f32[2,3,2304]{2,1,0:T(4,128)S(1)}, f32[2,3,2304]{2,1,0:T(4,128)S(1)}, u32[]{:S(2)}, u32[]{:S(2)}) collective-permute-start(f32[2,3,2304]{2,1,0:T(4,128)S(1)} %constant_dynamic-slice_fusion), channel_id=1, source_target_pairs={{8,0},{9,1},{10,2},{11,3},{12,4},{13,5},{14,6},{15,7},{0,8},{1,9},... | collective-permute-start | bytes 165896 | tf_op jit(solution)/shard_map/ppermute | solution.py:238
  5.4 1.2 collective-permute-done.came
  6.6 3.1 %collective-permute-start.5 = (f32[24,1152]{1,0:T(8,128)S(1)}, f32[24,1152]{1,0:T(8,128)S(1)}, u32[]{:S(2)}, u32[]{:S(2)}) collective-permute-start(f32[24,1152]{1,0:T(8,128)S(1)} %shard_map.46.refs_0_), channel_id=1, source_target_pairs={{6,0},{7,1},{0,2},{1,3},{2,4},{3,5},{4,6},{5,7},{14,8},{15,9},{8,1... | collective-permute-start | bytes 331784 | tf_op jit(solution)/shard_map/ppermute | solution.py:238
  9.7 3.1 %collective-permute-start.2 = (f32[24,1152]{1,0:T(8,128)S(1)}, f32[24,1152]{1,0:T(8,128)S(1)}, u32[]{:S(2)}, u32[]{:S(2)}) collective-permute-start(f32[24,1152]{1,0:T(8,128)S(1)} %shard_map.46.refs_0_), channel_id=1, source_target_pairs={{2,0},{3,1},{4,2},{5,3},{6,4},{7,5},{0,6},{1,7},{10,8},{11,9},{12,... | collective-permute-start | bytes 331784 | tf_op jit(solution)/shard_map/ppermute | solution.py:238
  12.9 2.1 %collective-permute-done.5.refs_6_ = f32[24,1152]{1,0:T(8,128)S(1)} collective-permute-done((f32[24,1152]{1,0:T(8,128)S(1)}, f32[24,1152]{1,0:T(8,128)S(1)}, u32[]{:S(2)}, u32[]{:S(2)}) %collective-permute-start.5) | collective-permute-done | bytes 110624 | tf_op jit(solution)/shard_map/ppermute | solution.py:238
  15.0 1.2 collective-permute-start.6
  16.2 1.4 %collective-permute-done.2.refs_2_ = f32[24,1152]{1,0:T(8,128)S(1)} collective-permute-done((f32[24,1152]{1,0:T(8,128)S(1)}, f32[24,1152]{1,0:T(8,128)S(1)}, u32[]{:S(2)}, u32[]{:S(2)}) %collective-permute-start.2) | collective-permute-done | bytes 110624 | tf_op jit(solution)/shard_map/ppermute | solution.py:238
  17.6 2.5 %collective-permute-start.4 = (f32[8,1152]{1,0:T(8,128)S(1)}, f32[8,1152]{1,0:T(8,128)S(1)}, u32[]{:S(2)}, u32[]{:S(2)}) collective-permute-start(f32[8,1152]{1,0:T(8,128)S(1)} %slice.16), channel_id=1, source_target_pairs={{2,0},{3,1},{4,2},{5,3},{6,4},{7,5},{0,6},{1,7},{10,8},{11,9},{12,... | collective-permute-start | bytes 110600 | tf_op jit(solution)/shard_map/ppermute | solution.py:238
  20.8 1.1 collective-permute-start.1
  21.9 1.2 collective-permute-start.8
  23.1 1.5 %collective-permute-start.3 = (f32[24,1152]{1,0:T(8,128)S(1)}, f32[24,1152]{1,0:T(8,128)S(1)}, u32[]{:S(2)}, u32[]{:S(2)}) collective-permute-start(f32[24,1152]{1,0:T(8,128)S(1)} %collective-permute-done.2.refs_2_), channel_id=1, source_target_pairs={{1,0},{2,1},{3,2},{4,3},{5,4},{6,5},{7,6},{0,7},{9,8},{10,9},{11,1... | collective-permute-start | bytes 331784 | tf_op jit(solution)/shard_map/ppermute | solution.py:238
  24.6 1.3 collective-permute-done.1.refs_1_
  26.7 1.8 %collective-permute-done.3.refs_3_ = f32[24,1152]{1,0:T(8,128)S(1)} collective-permute-done((f32[24,1152]{1,0:T(8,128)S(1)}, f32[24,1152]{1,0:T(8,128)S(1)}, u32[]{:S(2)}, u32[]{:S(2)}) %collective-permute-start.3) | collective-permute-done | bytes 110624 | tf_op jit(solution)/shard_map/ppermute | solution.py:238
  28.5 1.3 %collective-permute-done.7.refs_5_ = f32[24,1152]{1,0:T(8,128)S(1)} collective-permute-done((f32[24,1152]{1,0:T(8,128)S(1)}, f32[24,1152]{1,0:T(8,128)S(1)}, u32[]{:S(2)}, u32[]{:S(2)}) %collective-permute-start.7) | collective-permute-done | bytes 110624 | tf_op jit(solution)/shard_map/ppermute | solution.py:238
  30.1 4.6 %collective-permute-start.12 = (f32[2,48,2304]{2,1,0:T(8,128)S(1)}, f32[2,48,2304]{2,1,0:T(8,128)S(1)}, u32[]{:S(2)}, u32[]{:S(2)}) collective-permute-start(f32[2,48,2304]{2,1,0:T(8,128)S(1)} %get-tuple-element.28.own), channel_id=1, source_target_pairs={{16,0},{0,16},{48,32},{32,48},{80,64},{64,80},{112,96},{96,112},{1... | collective-permute-start | bytes 2654216 | tf_op jit(solution)/shard_map/ppermute | solution.py:238
  34.6 1.4 %fusion.9.ktab = f32[48,48,256]{2,1,0:T(8,128)S(1)} fusion(f32[256]{0:T(256)S(1)} %or_select_fusion, f32[48,48]{1,0:T(8,128)S(1)} %broadcast_multiply_fusion, s32[]{:T(128)S(6)} %copy.8, s32[256]{0:T(256)S(1)} %fusion.26, s32[48,48]{1,0:T(8,128)S(1)} %broadcast_add_fusion), kind=kLoop, calls=%fused_computation.12 | loop fusion | flops 8847360 | bytes 2379780 | tf_op jit(solution)/shard_map/jit(_where)/select_n | solution.py:234
  36.1 5.0 %collective-permute-start.10 = (f32[48,2304]{1,0:T(8,128)S(1)}, f32[48,2304]{1,0:T(8,128)S(1)}, u32[]{:S(2)}, u32[]{:S(2)}) collective-permute-start(f32[48,2304]{1,0:T(8,128)S(1)} %get-tuple-element.31), channel_id=1, source_target_pairs={{160,0},{193,1},{10,2},{67,3},{36,4},{133,5},{174,6},{111,7},{168,... | collective-permute-start | bytes 1327112 | tf_op jit(solution)/shard_map/ppermute | solution.py:316
  42.9 7.7 %collective-permute-done.10.vis = f32[48,2304]{1,0:T(8,128)S(1)} collective-permute-done((f32[48,2304]{1,0:T(8,128)S(1)}, f32[48,2304]{1,0:T(8,128)S(1)}, u32[]{:S(2)}, u32[]{:S(2)}) %collective-permute-start.10) | collective-permute-done | bytes 442400 | tf_op jit(solution)/shard_map/ppermute | solution.py:316
  50.6 2.0 %collective-permute-start.13 = (f32[48,2304]{1,0:T(8,128)S(1)}, f32[48,2304]{1,0:T(8,128)S(1)}, u32[]{:S(2)}, u32[]{:S(2)}) collective-permute-start(f32[48,2304]{1,0:T(8,128)S(1)} %get-tuple-element.33), channel_id=1, source_target_pairs={{32,0},{129,1},{170,2},{107,3},{164,4},{197,5},{14,6},{71,7},{40,8... | collective-permute-start | bytes 1327112 | tf_op jit(solution)/shard_map/ppermute | solution.py:325
  53.6 9.0 %shard_map.48 = (f32[2,48,2304]{2,1,0:T(8,128)S(1)}, f32[2,48,2304]{2,1,0:T(8,128)S(1)}, f32[48,2304]{1,0:T(8,128)S(1)}) custom-call(s32[4]{0:T(128)S(1)} %pad_add_fusion.idx, f32[2]{0:T(128)S(1)} %dynamic_slice.7.w_own, f32[2]{0:T(128)S(1)} %collective-permute-done.9.w_twin, f32[1]{0:T(128)} %collective-permute-done.14.w_vis, ...), custom_call_target="tpu_custom_call" | custom-call | flops 5000000000 | bytes 10000000 | tf_op jit(solution)/shard_map/pallas_call | solution.py:186
  62.7 8.8 %shard_map.49 = (f32[2,48,2304]{2,1,0:T(8,128)S(1)}, f32[2,48,2304]{2,1,0:T(8,128)S(1)}, f32[48,2304]{1,0:T(8,128)S(1)}) custom-call(s32[4]{0:T(128)S(1)} %pad_add_fusion.idx, f32[2]{0:T(128)S(1)} %dynamic_slice.7.w_own, f32[2]{0:T(128)S(1)} %collective-permute-done.9.w_twin, f32[1]{0:T(128)} %collective-permute-done.11.w_vis, ...), custom_call_target="tpu_custom_call" | custom-call | flops 5000000000 | bytes 10000000 | tf_op jit(solution)/shard_map/pallas_call | solution.py:186
  71.7 6.0 %collective-permute-start.17 = (f32[48,2304]{1,0:T(8,128)S(1)}, f32[48,2304]{1,0:T(8,128)S(1)}, u32[]{:S(2)}, u32[]{:S(2)}) collective-permute-start(f32[48,2304]{1,0:T(8,128)S(1)} %get-tuple-element.40), channel_id=1, source_target_pairs={{0,32},{1,129},{2,170},{3,107},{4,164},{5,197},{6,14},{8,40},{9,13... | collective-permute-start | bytes 1327112 | tf_op jit(solution)/shard_map/ppermute | solution.py:285
  77.7 3.2 %collective-permute-start.16 = (f32[48,2304]{1,0:T(8,128)S(1)}, f32[48,2304]{1,0:T(8,128)S(1)}, u32[]{:S(2)}, u32[]{:S(2)}) collective-permute-start(f32[48,2304]{1,0:T(8,128)S(1)} %get-tuple-element.39), channel_id=1, source_target_pairs={{0,160},{1,193},{2,10},{4,36},{5,133},{6,174},{7,111},{8,168},{9,2... | collective-permute-start | bytes 1327112 | tf_op jit(solution)/shard_map/ppermute | solution.py:285
  80.9 3.1 %collective-permute-done.17.c1 = f32[48,2304]{1,0:T(8,128)S(1)} collective-permute-done((f32[48,2304]{1,0:T(8,128)S(1)}, f32[48,2304]{1,0:T(8,128)S(1)}, u32[]{:S(2)}, u32[]{:S(2)}) %collective-permute-start.17) | collective-permute-done | bytes 442400 | tf_op jit(solution)/shard_map/ppermute | solution.py:285
  84.0 11.1 %collective-permute-done.16.c0 = f32[48,2304]{1,0:T(8,128)S(1)} collective-permute-done((f32[48,2304]{1,0:T(8,128)S(1)}, f32[48,2304]{1,0:T(8,128)S(1)}, u32[]{:S(2)}, u32[]{:S(2)}) %collective-permute-start.16) | collective-permute-done | bytes 442400 | tf_op jit(solution)/shard_map/ppermute | solution.py:285
  95.9 4.5 %collective-permute-start.20 = (f32[24,1152]{1,0:T(8,128)S(1)}, f32[24,1152]{1,0:T(8,128)S(1)}, u32[]{:S(2)}, u32[]{:S(2)}) collective-permute-start(f32[24,1152]{1,0:T(8,128)S(1)} %get-tuple-element.44), channel_id=1, source_target_pairs={{3,0},{4,1},{5,2},{6,3},{7,4},{0,5},{1,6},{2,7},{11,8},{12,9},{13,... | collective-permute-start | bytes 331784 | tf_op jit(solution)/shard_map/ppermute | solution.py:238
  100.4 2.0 %collective-permute-start.21 = (f32[24,1152]{1,0:T(8,128)S(1)}, f32[24,1152]{1,0:T(8,128)S(1)}, u32[]{:S(2)}, u32[]{:S(2)}) collective-permute-start(f32[24,1152]{1,0:T(8,128)S(1)} %get-tuple-element.45), channel_id=1, source_target_pairs={{6,0},{7,1},{0,2},{1,3},{2,4},{3,5},{4,6},{5,7},{14,8},{15,9},{8,1... | collective-permute-start | bytes 331784 | tf_op jit(solution)/shard_map/ppermute | solution.py:238
  102.4 3.2 %collective-permute-start.22 = (f32[24,1152]{1,0:T(8,128)S(1)}, f32[24,1152]{1,0:T(8,128)S(1)}, u32[]{:S(2)}, u32[]{:S(2)}) collective-permute-start(f32[24,1152]{1,0:T(8,128)S(1)} %get-tuple-element.46), channel_id=1, source_target_pairs={{2,0},{3,1},{4,2},{5,3},{6,4},{7,5},{0,6},{1,7},{10,8},{11,9},{12,... | collective-permute-start | bytes 331784 | tf_op jit(solution)/shard_map/ppermute | solution.py:238
  105.9 5.3 %collective-permute-done.19.refs_2_ = f32[24,1152]{1,0:T(8,128)S(1)} collective-permute-done((f32[24,1152]{1,0:T(8,128)S(1)}, f32[24,1152]{1,0:T(8,128)S(1)}, u32[]{:S(2)}, u32[]{:S(2)}) %collective-permute-start.19) | collective-permute-done | bytes 110624 | tf_op jit(solution)/shard_map/ppermute | solution.py:238
  111.2 6.6 %collective-permute-done.21.refs_4_ = f32[24,1152]{1,0:T(8,128)S(1)} collective-permute-done((f32[24,1152]{1,0:T(8,128)S(1)}, f32[24,1152]{1,0:T(8,128)S(1)}, u32[]{:S(2)}, u32[]{:S(2)}) %collective-permute-start.21) | collective-permute-done | bytes 110624 | tf_op jit(solution)/shard_map/ppermute | solution.py:238
  117.9 2.4 %collective-permute-done.23.refs_6_ = f32[24,1152]{1,0:T(8,128)S(1)} collective-permute-done((f32[24,1152]{1,0:T(8,128)S(1)}, f32[24,1152]{1,0:T(8,128)S(1)}, u32[]{:S(2)}, u32[]{:S(2)}) %collective-permute-start.23) | collective-permute-done | bytes 110624 | tf_op jit(solution)/shard_map/ppermute | solution.py:238
  120.6 4.7 %collective-permute-done.25 = f32[2,3,2304]{2,1,0:T(4,128)S(1)} collective-permute-done((f32[2,3,2304]{2,1,0:T(4,128)S(1)}, f32[2,3,2304]{2,1,0:T(4,128)S(1)}, u32[]{:S(2)}, u32[]{:S(2)}) %collective-permute-start.25) | collective-permute-done | bytes 55328 | tf_op jit(solution)/shard_map/ppermute | solution.py:238
  (56 shorter events, 7.8 us)
Async XLA Ops:
  0.0 41.2 %copy-start.2 = (s32[4]{0:T(128)S(1)}, s32[4]{0:T(128)}, u32[]{:S(2)}) copy-start(s32[4]{0:T(128)} %param.5) | copy-start | bytes 52
  0.0 53.6 %copy-start = (bf16[96,96]{1,0:T(8,128)(2,1)S(1)}, bf16[96,96]{1,0:T(8,128)(2,1)}, u32[]{:S(2)}) copy-start(bf16[96,96]{1,0:T(8,128)(2,1)} %constant.180.fz) | copy-start | bytes 55300
  0.0 53.6 %copy-start.1 = (bf16[96,96]{1,0:T(8,128)(2,1)S(1)}, bf16[96,96]{1,0:T(8,128)(2,1)}, u32[]{:S(2)}) copy-start(bf16[96,96]{1,0:T(8,128)(2,1)} %constant.188.iz) | copy-start | bytes 55300
  1.0 5.6 %collective-permute-start = (f32[2,3,2304]{2,1,0:T(4,128)S(1)}, f32[2,3,2304]{2,1,0:T(4,128)S(1)}, u32[]{:S(2)}, u32[]{:S(2)}) collective-permute-start(f32[2,3,2304]{2,1,0:T(4,128)S(1)} %constant_dynamic-slice_fusion), channel_id=1, source_target_pairs={{8,0},{9,1},{10,2},{11,3},{12,4},{13,5},{14,6},{15,7},{0,8},{1,9},... | collective-permute-start | bytes 165896 | tf_op jit(solution)/shard_map/ppermute | solution.py:238
  6.6 8.4 %collective-permute-start.5 = (f32[24,1152]{1,0:T(8,128)S(1)}, f32[24,1152]{1,0:T(8,128)S(1)}, u32[]{:S(2)}, u32[]{:S(2)}) collective-permute-start(f32[24,1152]{1,0:T(8,128)S(1)} %shard_map.46.refs_0_), channel_id=1, source_target_pairs={{6,0},{7,1},{0,2},{1,3},{2,4},{3,5},{4,6},{5,7},{14,8},{15,9},{8,1... | collective-permute-start | bytes 331784 | tf_op jit(solution)/shard_map/ppermute | solution.py:238
  9.7 7.9 %collective-permute-start.2 = (f32[24,1152]{1,0:T(8,128)S(1)}, f32[24,1152]{1,0:T(8,128)S(1)}, u32[]{:S(2)}, u32[]{:S(2)}) collective-permute-start(f32[24,1152]{1,0:T(8,128)S(1)} %shard_map.46.refs_0_), channel_id=1, source_target_pairs={{2,0},{3,1},{4,2},{5,3},{6,4},{7,5},{0,6},{1,7},{10,8},{11,9},{12,... | collective-permute-start | bytes 331784 | tf_op jit(solution)/shard_map/ppermute | solution.py:238
  15.0 9.6 %collective-permute-start.6 = (f32[16,1152]{1,0:T(8,128)S(1)}, f32[16,1152]{1,0:T(8,128)S(1)}, u32[]{:S(2)}, u32[]{:S(2)}) collective-permute-start(f32[16,1152]{1,0:T(8,128)S(1)} %slice.17), channel_id=1, source_target_pairs={{6,0},{7,1},{0,2},{1,3},{2,4},{3,5},{4,6},{5,7},{14,8},{15,9},{8,1... | collective-permute-start | bytes 221192 | tf_op jit(solution)/shard_map/ppermute | solution.py:238
  17.6 6.9 %collective-permute-start.4 = (f32[8,1152]{1,0:T(8,128)S(1)}, f32[8,1152]{1,0:T(8,128)S(1)}, u32[]{:S(2)}, u32[]{:S(2)}) collective-permute-start(f32[8,1152]{1,0:T(8,128)S(1)} %slice.16), channel_id=1, source_target_pairs={{2,0},{3,1},{4,2},{5,3},{6,4},{7,5},{0,6},{1,7},{10,8},{11,9},{12,... | collective-permute-start | bytes 110600 | tf_op jit(solution)/shard_map/ppermute | solution.py:238
  20.8 5.0 %collective-permute-start.1 = (f32[24,1152]{1,0:T(8,128)S(1)}, f32[24,1152]{1,0:T(8,128)S(1)}, u32[]{:S(2)}, u32[]{:S(2)}) collective-permute-start(f32[24,1152]{1,0:T(8,128)S(1)} %shard_map.46.refs_0_), channel_id=1, source_target_pairs={{1,0},{2,1},{3,2},{4,3},{5,4},{6,5},{7,6},{0,7},{9,8},{10,9},{11,1... | collective-permute-start | bytes 331784 | tf_op jit(solution)/shard_map/ppermute | solution.py:238
  21.9 4.8 %collective-permute-start.8 = (f32[24,1152]{1,0:T(8,128)S(1)}, f32[24,1152]{1,0:T(8,128)S(1)}, u32[]{:S(2)}, u32[]{:S(2)}) collective-permute-start(f32[24,1152]{1,0:T(8,128)S(1)} %shard_map.46.refs_0_), channel_id=1, source_target_pairs={{7,0},{0,1},{1,2},{2,3},{3,4},{4,5},{5,6},{6,7},{15,8},{8,9},{9,10... | collective-permute-start | bytes 331784 | tf_op jit(solution)/shard_map/ppermute | solution.py:238
  23.1 5.4 %collective-permute-start.3 = (f32[24,1152]{1,0:T(8,128)S(1)}, f32[24,1152]{1,0:T(8,128)S(1)}, u32[]{:S(2)}, u32[]{:S(2)}) collective-permute-start(f32[24,1152]{1,0:T(8,128)S(1)} %collective-permute-done.2.refs_2_), channel_id=1, source_target_pairs={{1,0},{2,1},{3,2},{4,3},{5,4},{6,5},{7,6},{0,7},{9,8},{10,9},{11,1... | collective-permute-start | bytes 331784 | tf_op jit(solution)/shard_map/ppermute | solution.py:238
  24.6 5.3 %collective-permute-start.7 = (f32[24,1152]{1,0:T(8,128)S(1)}, f32[24,1152]{1,0:T(8,128)S(1)}, u32[]{:S(2)}, u32[]{:S(2)}) collective-permute-start(f32[24,1152]{1,0:T(8,128)S(1)} %collective-permute-done.5.refs_6_), channel_id=1, source_target_pairs={{7,0},{0,1},{1,2},{2,3},{3,4},{4,5},{5,6},{6,7},{15,8},{8,9},{9,10... | collective-permute-start | bytes 331784 | tf_op jit(solution)/shard_map/ppermute | solution.py:238
  30.1 23.5 %collective-permute-start.12 = (f32[2,48,2304]{2,1,0:T(8,128)S(1)}, f32[2,48,2304]{2,1,0:T(8,128)S(1)}, u32[]{:S(2)}, u32[]{:S(2)}) collective-permute-start(f32[2,48,2304]{2,1,0:T(8,128)S(1)} %get-tuple-element.28.own), channel_id=1, source_target_pairs={{16,0},{0,16},{48,32},{32,48},{80,64},{64,80},{112,96},{96,112},{1... | collective-permute-start | bytes 2654216 | tf_op jit(solution)/shard_map/ppermute | solution.py:238
  36.1 14.5 %collective-permute-start.10 = (f32[48,2304]{1,0:T(8,128)S(1)}, f32[48,2304]{1,0:T(8,128)S(1)}, u32[]{:S(2)}, u32[]{:S(2)}) collective-permute-start(f32[48,2304]{1,0:T(8,128)S(1)} %get-tuple-element.31), channel_id=1, source_target_pairs={{160,0},{193,1},{10,2},{67,3},{36,4},{133,5},{174,6},{111,7},{168,... | collective-permute-start | bytes 1327112 | tf_op jit(solution)/shard_map/ppermute | solution.py:316
  41.2 12.4 %collective-permute-start.9 = (f32[2]{0:T(128)S(1)}, f32[2]{0:T(128)S(1)}, u32[]{:S(2)}, u32[]{:S(2)}) collective-permute-start(f32[2]{0:T(128)S(1)} %dynamic_slice.7.w_own), channel_id=1, source_target_pairs={{16,0},{0,16},{48,32},{32,48},{80,64},{64,80},{112,96},{96,112},{1... | collective-permute-start | bytes 32 | tf_op jit(solution)/shard_map/ppermute | solution.py:238
  42.2 11.4 %collective-permute-start.14 = (f32[1]{0:T(128)}, f32[1]{0:T(128)}, u32[]{:S(2)}, u32[]{:S(2)}) collective-permute-start(f32[1]{0:T(128)} %get-tuple-element.57), channel_id=1, source_target_pairs={{160,0},{193,1},{10,2},{67,3},{36,4},{133,5},{174,6},{111,7},{168,... | collective-permute-start | bytes 20 | tf_op jit(solution)/shard_map/ppermute | solution.py:323
  50.6 12.1 %collective-permute-start.13 = (f32[48,2304]{1,0:T(8,128)S(1)}, f32[48,2304]{1,0:T(8,128)S(1)}, u32[]{:S(2)}, u32[]{:S(2)}) collective-permute-start(f32[48,2304]{1,0:T(8,128)S(1)} %get-tuple-element.33), channel_id=1, source_target_pairs={{32,0},{129,1},{170,2},{107,3},{164,4},{197,5},{14,6},{71,7},{40,8... | collective-permute-start | bytes 1327112 | tf_op jit(solution)/shard_map/ppermute | solution.py:325
  52.6 10.1 %collective-permute-start.11 = (f32[1]{0:T(128)}, f32[1]{0:T(128)}, u32[]{:S(2)}, u32[]{:S(2)}) collective-permute-start(f32[1]{0:T(128)} %get-tuple-element.32), channel_id=1, source_target_pairs={{32,0},{129,1},{170,2},{107,3},{164,4},{197,5},{14,6},{71,7},{40,8... | collective-permute-start | bytes 20 | tf_op jit(solution)/shard_map/ppermute | solution.py:326
  71.5 23.5 %collective-permute-start.15 = (f32[2,48,2304]{2,1,0:T(8,128)S(1)}, f32[2,48,2304]{2,1,0:T(8,128)S(1)}, u32[]{:S(2)}, u32[]{:S(2)}) collective-permute-start(f32[2,48,2304]{2,1,0:T(8,128)S(1)} %get-tuple-element.38), channel_id=1, source_target_pairs={{16,0},{0,16},{48,32},{32,48},{80,64},{64,80},{112,96},{96,112},{1... | collective-permute-start | bytes 2654216 | tf_op jit(solution)/shard_map/ppermute | solution.py:238
  71.7 12.3 %collective-permute-start.17 = (f32[48,2304]{1,0:T(8,128)S(1)}, f32[48,2304]{1,0:T(8,128)S(1)}, u32[]{:S(2)}, u32[]{:S(2)}) collective-permute-start(f32[48,2304]{1,0:T(8,128)S(1)} %get-tuple-element.40), channel_id=1, source_target_pairs={{0,32},{1,129},{2,170},{3,107},{4,164},{5,197},{6,14},{8,40},{9,13... | collective-permute-start | bytes 1327112 | tf_op jit(solution)/shard_map/ppermute | solution.py:285
  77.7 17.4 %collective-permute-start.16 = (f32[48,2304]{1,0:T(8,128)S(1)}, f32[48,2304]{1,0:T(8,128)S(1)}, u32[]{:S(2)}, u32[]{:S(2)}) collective-permute-start(f32[48,2304]{1,0:T(8,128)S(1)} %get-tuple-element.39), channel_id=1, source_target_pairs={{0,160},{1,193},{2,10},{4,36},{5,133},{6,174},{7,111},{8,168},{9,2... | collective-permute-start | bytes 1327112 | tf_op jit(solution)/shard_map/ppermute | solution.py:285
  95.4 10.2 %collective-permute-start.18 = (f32[24,1152]{1,0:T(8,128)S(1)}, f32[24,1152]{1,0:T(8,128)S(1)}, u32[]{:S(2)}, u32[]{:S(2)}) collective-permute-start(f32[24,1152]{1,0:T(8,128)S(1)} %get-tuple-element.42), channel_id=1, source_target_pairs={{4,0},{5,1},{6,2},{7,3},{0,4},{1,5},{2,6},{3,7},{12,8},{13,9},{14,... | collective-permute-start | bytes 331784 | tf_op jit(solution)/shard_map/ppermute | solution.py:238
  95.9 15.3 %collective-permute-start.19 = (f32[24,1152]{1,0:T(8,128)S(1)}, f32[24,1152]{1,0:T(8,128)S(1)}, u32[]{:S(2)}, u32[]{:S(2)}) collective-permute-start(f32[24,1152]{1,0:T(8,128)S(1)} %get-tuple-element.43), channel_id=1, source_target_pairs={{5,0},{6,1},{7,2},{0,3},{1,4},{2,5},{3,6},{4,7},{13,8},{14,9},{15,... | collective-permute-start | bytes 331784 | tf_op jit(solution)/shard_map/ppermute | solution.py:238
  95.9 15.3 %collective-permute-start.20 = (f32[24,1152]{1,0:T(8,128)S(1)}, f32[24,1152]{1,0:T(8,128)S(1)}, u32[]{:S(2)}, u32[]{:S(2)}) collective-permute-start(f32[24,1152]{1,0:T(8,128)S(1)} %get-tuple-element.44), channel_id=1, source_target_pairs={{3,0},{4,1},{5,2},{6,3},{7,4},{0,5},{1,6},{2,7},{11,8},{12,9},{13,... | collective-permute-start | bytes 331784 | tf_op jit(solution)/shard_map/ppermute | solution.py:238
  100.4 17.5 %collective-permute-start.21 = (f32[24,1152]{1,0:T(8,128)S(1)}, f32[24,1152]{1,0:T(8,128)S(1)}, u32[]{:S(2)}, u32[]{:S(2)}) collective-permute-start(f32[24,1152]{1,0:T(8,128)S(1)} %get-tuple-element.45), channel_id=1, source_target_pairs={{6,0},{7,1},{0,2},{1,3},{2,4},{3,5},{4,6},{5,7},{14,8},{15,9},{8,1... | collective-permute-start | bytes 331784 | tf_op jit(solution)/shard_map/ppermute | solution.py:238
  102.4 15.5 %collective-permute-start.22 = (f32[24,1152]{1,0:T(8,128)S(1)}, f32[24,1152]{1,0:T(8,128)S(1)}, u32[]{:S(2)}, u32[]{:S(2)}) collective-permute-start(f32[24,1152]{1,0:T(8,128)S(1)} %get-tuple-element.46), channel_id=1, source_target_pairs={{2,0},{3,1},{4,2},{5,3},{6,4},{7,5},{0,6},{1,7},{10,8},{11,9},{12,... | collective-permute-start | bytes 331784 | tf_op jit(solution)/shard_map/ppermute | solution.py:238
  105.6 14.7 %collective-permute-start.23 = (f32[24,1152]{1,0:T(8,128)S(1)}, f32[24,1152]{1,0:T(8,128)S(1)}, u32[]{:S(2)}, u32[]{:S(2)}) collective-permute-start(f32[24,1152]{1,0:T(8,128)S(1)} %get-tuple-element.47), channel_id=1, source_target_pairs={{7,0},{0,1},{1,2},{2,3},{3,4},{4,5},{5,6},{6,7},{15,8},{8,9},{9,10... | collective-permute-start | bytes 331784 | tf_op jit(solution)/shard_map/ppermute | solution.py:238
  111.2 9.1 %collective-permute-start.24 = (f32[24,1152]{1,0:T(8,128)S(1)}, f32[24,1152]{1,0:T(8,128)S(1)}, u32[]{:S(2)}, u32[]{:S(2)}) collective-permute-start(f32[24,1152]{1,0:T(8,128)S(1)} %get-tuple-element.48), channel_id=1, source_target_pairs={{1,0},{2,1},{3,2},{4,3},{5,4},{6,5},{7,6},{0,7},{9,8},{10,9},{11,1... | collective-permute-start | bytes 331784 | tf_op jit(solution)/shard_map/ppermute | solution.py:238
  120.5 4.8 %collective-permute-start.25 = (f32[2,3,2304]{2,1,0:T(4,128)S(1)}, f32[2,3,2304]{2,1,0:T(4,128)S(1)}, u32[]{:S(2)}, u32[]{:S(2)}) collective-permute-start(f32[2,3,2304]{2,1,0:T(4,128)S(1)} %get-tuple-element.50), channel_id=1, source_target_pairs={{8,0},{9,1},{10,2},{11,3},{12,4},{13,5},{14,6},{15,7},{0,8},{1,9},... | collective-permute-start | bytes 165896 | tf_op jit(solution)/shard_map/ppermute | solution.py:238

commit v2 on v1

--- a/solution.py
+++ b/solution.py
@@ -12,6 +12,7 @@
 G = 48
 ROW = G * G
 HALF = ROW // 2
+WITH_W = ROW + 128
 WIDE = 256
 YB = 8
 LB = YB * G
@@ -59,8 +60,12 @@
             blk[r + 3:r + 6, :] = b[:, h * HALF:(h + 1) * HALF]
 
 
-def assemble_body(*refs):
+def assemble_body(y, occupation, *refs):
     both, lone = refs[8], refs[9:]
+    for o in range(2):
+        w = jnp.full((G, 128), occupation[2 * y[0] + o].astype(jnp.float32) * -0.5, jnp.float32)
+        both[o, :, ROW:] = w
+        lone[o][:, ROW:] = w
     for k in range(8):
         for o in range(2):
             for h in range(2):
@@ -95,7 +100,7 @@
             give[o, :, h * HALF:(h + 1) * HALF] = jnp.where(flip, a, b)
 
 
-def kernel(first, idx, w_own, w_twin, w_vis, own, twin, vis, ktab, fx, ix, fz, iz, *refs):
+def kernel(first, idx, own, twin, vis, ktab, fx, ix, fz, iz, *refs):
     prior = () if first else refs[:2]
     home, away, back, spec, *bufs = refs[len(prior):]
     gi, gj = idx[0], idx[1]
@@ -144,11 +149,17 @@
     for u in range(12):
         spec[G - 12 + u] = apply(iz[...], bufs[-1][u])
 
+    def spread(w):
+        return jnp.concatenate([w] * (LB // 128), axis=1)
+
     keep = jnp.where(once != 0, 0.0, 1.0)
-    wo = [w_own[0] * keep, w_own[1] * keep, w_twin[0] * keep, w_twin[1] * keep]
-    wj = jnp.where(gj < 2, w_own[gj & 1], w_twin[gj & 1])
-    wg = jnp.where(gi < 2, wj, 0.0)
-    wt = jnp.where(gi < 2, 0.0, wj)
+    tail = slice(ROW, WITH_W)
+    wo = [spread((own if i < 2 else twin)[i % 2, 0:1, tail] * keep) for i in range(4)]
+    wv = spread(vis[0:1, tail])
+    if first:
+        wj = spread(jnp.where(gj < 2, own[gj & 1, 0:1, tail], twin[gj & 1, 0:1, tail]))
+        wg = jnp.where(gi < 2, wj, 0.0)
+        wt = jnp.where(gi < 2, 0.0, wj)
 
     def leave_one(yb, rows, cols, zed):
         lanes = pl.ds(pl.multiple_of(yb * LB, LB), LB)
@@ -158,7 +169,7 @@
         for c in range(3):
             rows[:, c * 128:(c + 1) * 128] = cols[c * 128:(c + 1) * 128, :].T
         total = None
-        v = vis[:, lanes] * w_vis[0]
+        v = vis[:, lanes] * wv
         for i in range(4):
             p = apply(ix[...], rows[i * G:(i + 1) * G, :])
             side = i // 2
@@ -186,7 +197,7 @@
     return pl.pallas_call(
         functools.partial(kernel, first),
         out_shape=[f32(2, G, ROW), f32(2, G, ROW), f32(G, ROW)],
-        in_specs=[SM] * 4 + [VM] * (len(args) - 4),
+        in_specs=[SM] + [VM] * (len(args) - 1),
         out_specs=[VM] * 3,
         scratch_shapes=[
             pltpu.VMEM((G, G, WIDE), jnp.float32),
@@ -287,13 +298,11 @@
 
 def gather_blocks(b0):
     got = {0: b0}
-    for k in (2, 6, 1, 7):
-        got[k] = ring(b0, "grid", along(k))
-    got[3] = ring(got[2], "grid", along(1))
-    got[5] = ring(got[6], "grid", along(7))
-    far = ring(got[2][:8], "grid", along(2))
-    rest = ring(got[6][8:], "grid", along(6))
-    got[4] = jnp.concatenate([far, rest], axis=0)
+    for k, source, hop in (
+        (2, 0, 2), (6, 0, 6), (1, 0, 1), (7, 0, 7),
+        (3, 2, 1), (5, 6, 7), (4, 2, 2),
+    ):
+        got[k] = ring(got[source], "grid", along(hop))
     return [got[k] for k in range(8)]
 
 
@@ -312,19 +321,6 @@
     blk = small_call(pack_body, [f32(24, HALF)], y1, orbitals, came, scalars=1)
 
     got = gather_blocks(blk)
-    own, *lone = small_call(assemble_body, [f32(2, G, ROW), f32(G, ROW), f32(G, ROW)], *got)
-    first = lax.ppermute(lone[0], axes, visit_route(0))
-    twin = ring(own, "band", twin_of)
-
-    late = lax.optimization_barrier((occupation, own))[0]
-    weights = late.astype(jnp.float32) * -0.5
-    w_own = lax.dynamic_slice(weights, (2 * y,), (2,))
-    w_twin = ring(w_own, "band", twin_of)
-    w_first = lax.ppermute(w_own[:1], axes, visit_route(0))
-    held, w_held, first = lax.optimization_barrier((lone[1], w_own[1:], first))
-    second = lax.ppermute(held, axes, visit_route(1))
-    w_second = lax.ppermute(w_held, axes, visit_route(1))
-
     e = z * 2 + core
     once = [z == ORDER[v].index(7) for v in range(2)]
     idx = jnp.stack([e // 4 ^ 2 * core, e % 4 ^ 2 * core] + [o.astype(jnp.int32) for o in once])
@@ -332,9 +328,18 @@
     turned = basis(3 * (r // 3 % 2 * 8 + (z + r // 6) % 8) + r % 3)
     plain = jnp.asarray(plain_basis())
     tables = (kernel_table(cutoff), stacked(turned), stacked(turned.T), stacked(plain), stacked(plain.T))
-    home, away, back = pair_solver(True, idx, w_own, w_twin, w_first, own, twin, first, *tables)
+    got, idx, tables = lax.optimization_barrier((got, idx, tables))
+    own, *lone = small_call(
+        assemble_body, [f32(2, G, WITH_W), f32(G, WITH_W), f32(G, WITH_W)], y1, occupation, *got, scalars=2
+    )
+    vis0 = lax.ppermute(lone[0], axes, visit_route(0))
+    twin = ring(own, "band", twin_of)
+    held, vis0 = lax.optimization_barrier((lone[1], vis0))
+    vis1 = lax.ppermute(held, axes, visit_route(1))
+
+    home, away, back = pair_solver(True, idx, own, twin, vis0, *tables)
     ret0 = returned(back, 0)
-    home, away, back = pair_solver(False, idx, w_own, w_twin, w_second, own, twin, second, *tables, home, away)
+    home, away, back = pair_solver(False, idx, own, twin, vis1, *tables, home, away)
     ret1 = returned(back, 1)
     swapped = ring(away, "band", twin_of)
     part = small_call(disperse_body, [f32(24, HALF)] * 8, home, swapped, ret0, ret1)

time: 126 us -> 119 us (0.944)
  the two profiles are of different devices: /device:TPU:1 before, /device:TPU:8 now
where the time goes in v2:
time: 119 us
  starting transfers between devices  48.2 us (41%)
  waiting for transfers between devices  47.6 us (40%)
  Pallas kernels  18.1 us (15%)
  other arithmetic  2.15 us (2%)
  local copies, waits for them, and re-layouts  1.66 us (1%)
    ppermute x18, starting transfers between devices, ring(): lax.ppermute(block, axis, [(source(i), i) for i in range(lax.axis_size(ax...  34.1 us
    ppermute x18, waiting for transfers between devices, ring(): lax.ppermute(block, axis, [(source(i), i) for i in range(lax.axis_size(ax...  21.8 us
    pallas_call x2, Pallas kernels, pair_solver(): pl.pallas_call(functools.partial(kernel, first), out_shape=[f32(2, G, ROW...  16.7 us
    ppermute x2, waiting for transfers between devices, returned(): lax.ppermute(back, ('band', 'grid'), [(d, s) for s, d in visit_route(v, F...  15.3 us
    ppermute x1, waiting for transfers between devices, on_device(): vis0 = lax.ppermute(lone[0], axes, visit_route(0))  10.5 us
    ppermute x2, starting transfers between devices, returned(): lax.ppermute(back, ('band', 'grid'), [(d, s) for s, d in visit_route(v, F...  6.74 us
    ppermute x1, starting transfers between devices, on_device(): vis0 = lax.ppermute(lone[0], axes, visit_route(0))  4.19 us
    ppermute x1, starting transfers between devices, on_device(): vis1 = lax.ppermute(held, axes, visit_route(1))  3.24 us
  transfers between devices with their start and end apart: 22, of which 12 were waited for; matrix products, arithmetic and copies ran while one was open for 2% of the time, Pallas kernels for 7%

profile of v2, /device:TPU:8, one launch (start us, length us, event | category | flops | bytes accessed | tf_op | source)
XLA Modules:
  0.0 118.7 jit_solution(1634834237547435832)
XLA Ops:
  0.0 1.0 copy.6.slab
  1.0 2.4 %collective-permute-start = (f32[2,3,2304]{2,1,0:T(4,128)S(1)}, f32[2,3,2304]{2,1,0:T(4,128)S(1)}, u32[]{:S(2)}, u32[]{:S(2)}) collective-permute-start(f32[2,3,2304]{2,1,0:T(4,128)S(1)} %constant_dynamic-slice_fusion), channel_id=1, source_target_pairs={{8,0},{9,1},{10,2},{11,3},{12,4},{13,5},{14,6},{15,7},{0,8},{1,9},... | collective-permute-start | bytes 165896 | tf_op jit(solution)/shard_map/ppermute | solution.py:249
  4.3 1.4 %fusion.9.ktab = f32[48,48,256]{2,1,0:T(8,128)S(1)} fusion(f32[256]{0:T(256)S(1)} %or_select_fusion, f32[48,48]{1,0:T(8,128)S(1)} %broadcast_multiply_fusion, s32[]{:T(128)S(6)} %copy.8, s32[256]{0:T(256)S(1)} %fusion.26, s32[48,48]{1,0:T(8,128)S(1)} %broadcast_add_fusion), kind=kLoop, calls=%fused_computation.12 | loop fusion | flops 8847360 | bytes 2379780 | tf_op jit(solution)/shard_map/jit(_where)/select_n | solution.py:245
  6.1 0.9 collective-permute-done.came
  7.0 6.4 %collective-permute-start.2 = (f32[24,1152]{1,0:T(8,128)S(1)}, f32[24,1152]{1,0:T(8,128)S(1)}, u32[]{:S(2)}, u32[]{:S(2)}) collective-permute-start(f32[24,1152]{1,0:T(8,128)S(1)} %shard_map.46.refs_0_), channel_id=1, source_target_pairs={{2,0},{3,1},{4,2},{5,3},{6,4},{7,5},{0,6},{1,7},{10,8},{11,9},{12,... | collective-permute-start | bytes 331784 | tf_op jit(solution)/shard_map/ppermute | solution.py:249
  13.5 3.7 %collective-permute-start.1 = (f32[24,1152]{1,0:T(8,128)S(1)}, f32[24,1152]{1,0:T(8,128)S(1)}, u32[]{:S(2)}, u32[]{:S(2)}) collective-permute-start(f32[24,1152]{1,0:T(8,128)S(1)} %shard_map.46.refs_0_), channel_id=1, source_target_pairs={{1,0},{2,1},{3,2},{4,3},{5,4},{6,5},{7,6},{0,7},{9,8},{10,9},{11,1... | collective-permute-start | bytes 331784 | tf_op jit(solution)/shard_map/ppermute | solution.py:249
  17.3 3.1 %collective-permute-start.3 = (f32[24,1152]{1,0:T(8,128)S(1)}, f32[24,1152]{1,0:T(8,128)S(1)}, u32[]{:S(2)}, u32[]{:S(2)}) collective-permute-start(f32[24,1152]{1,0:T(8,128)S(1)} %collective-permute-done.2.refs_2_), channel_id=1, source_target_pairs={{1,0},{2,1},{3,2},{4,3},{5,4},{6,5},{7,6},{0,7},{9,8},{10,9},{11,1... | collective-permute-start | bytes 331784 | tf_op jit(solution)/shard_map/ppermute | solution.py:249
  20.4 1.6 %collective-permute-start.4 = (f32[24,1152]{1,0:T(8,128)S(1)}, f32[24,1152]{1,0:T(8,128)S(1)}, u32[]{:S(2)}, u32[]{:S(2)}) collective-permute-start(f32[24,1152]{1,0:T(8,128)S(1)} %collective-permute-done.2.refs_2_), channel_id=1, source_target_pairs={{2,0},{3,1},{4,2},{5,3},{6,4},{7,5},{0,6},{1,7},{10,8},{11,9},{12,... | collective-permute-start | bytes 331784 | tf_op jit(solution)/shard_map/ppermute | solution.py:249
  22.1 2.0 %collective-permute-start.6 = (f32[24,1152]{1,0:T(8,128)S(1)}, f32[24,1152]{1,0:T(8,128)S(1)}, u32[]{:S(2)}, u32[]{:S(2)}) collective-permute-start(f32[24,1152]{1,0:T(8,128)S(1)} %collective-permute-done.5.refs_6_), channel_id=1, source_target_pairs={{7,0},{0,1},{1,2},{2,3},{3,4},{4,5},{5,6},{6,7},{15,8},{8,9},{9,10... | collective-permute-start | bytes 331784 | tf_op jit(solution)/shard_map/ppermute | solution.py:249
  24.2 2.9 %collective-permute-done.4.refs_4_ = f32[24,1152]{1,0:T(8,128)S(1)} collective-permute-done((f32[24,1152]{1,0:T(8,128)S(1)}, f32[24,1152]{1,0:T(8,128)S(1)}, u32[]{:S(2)}, u32[]{:S(2)}) %collective-permute-start.4) | collective-permute-done | bytes 110624 | tf_op jit(solution)/shard_map/ppermute | solution.py:249
  27.1 0.9 collective-permute-done.6.refs_5_
  28.0 0.8 shard_map.47
  28.9 4.2 %collective-permute-start.9 = (f32[48,2432]{1,0:T(8,128)S(1)}, f32[48,2432]{1,0:T(8,128)S(1)}, u32[]{:S(2)}, u32[]{:S(2)}) collective-permute-start(f32[48,2432]{1,0:T(8,128)S(1)} %get-tuple-element.51), channel_id=1, source_target_pairs={{160,0},{193,1},{10,2},{67,3},{36,4},{133,5},{174,6},{111,7},{168,... | collective-permute-start | bytes 1400840 | tf_op jit(solution)/shard_map/ppermute | solution.py:335
  33.1 10.5 %collective-permute-done.9.vis = f32[48,2432]{1,0:T(8,128)S(1)} collective-permute-done((f32[48,2432]{1,0:T(8,128)S(1)}, f32[48,2432]{1,0:T(8,128)S(1)}, u32[]{:S(2)}, u32[]{:S(2)}) %collective-permute-start.9) | collective-permute-done | bytes 466976 | tf_op jit(solution)/shard_map/ppermute | solution.py:335
  43.7 3.2 %collective-permute-start.10 = (f32[48,2432]{1,0:T(8,128)S(1)}, f32[48,2432]{1,0:T(8,128)S(1)}, u32[]{:S(2)}, u32[]{:S(2)}) collective-permute-start(f32[48,2432]{1,0:T(8,128)S(1)} %get-tuple-element.52), channel_id=1, source_target_pairs={{32,0},{129,1},{170,2},{107,3},{164,4},{197,5},{14,6},{71,7},{40,8... | collective-permute-start | bytes 1400840 | tf_op jit(solution)/shard_map/ppermute | solution.py:338
  46.9 8.5 %shard_map.48 = (f32[2,48,2304]{2,1,0:T(8,128)S(1)}, f32[2,48,2304]{2,1,0:T(8,128)S(1)}, f32[48,2304]{1,0:T(8,128)S(1)}) custom-call(s32[4]{0:T(128)S(1)} %pad_add_fusion.idx, f32[2,48,2432]{2,1,0:T(8,128)S(1)} %get-tuple-element.49.own, f32[2,48,2432]{2,1,0:T(8,128)S(1)} %collective-permute-done.8.twin, f32[48,2432]{1,0:T(8,128)S(1)} %collective-permute-done.9.vis, ...), custom_call_target="tpu_custom_call" | custom-call | flops 5000000000 | bytes 10000000 | tf_op jit(solution)/shard_map/pallas_call | solution.py:197
  55.4 8.2 %shard_map.49 = (f32[2,48,2304]{2,1,0:T(8,128)S(1)}, f32[2,48,2304]{2,1,0:T(8,128)S(1)}, f32[48,2304]{1,0:T(8,128)S(1)}) custom-call(s32[4]{0:T(128)S(1)} %pad_add_fusion.idx, f32[2,48,2432]{2,1,0:T(8,128)S(1)} %get-tuple-element.49.own, f32[2,48,2432]{2,1,0:T(8,128)S(1)} %collective-permute-done.8.twin, f32[48,2432]{1,0:T(8,128)S(1)} %collective-permute-done.10.vis, ...), custom_call_target="tpu_custom_call" | custom-call | flops 5000000000 | bytes 10000000 | tf_op jit(solution)/shard_map/pallas_call | solution.py:197
  63.7 3.1 %collective-permute-start.13 = (f32[48,2304]{1,0:T(8,128)S(1)}, f32[48,2304]{1,0:T(8,128)S(1)}, u32[]{:S(2)}, u32[]{:S(2)}) collective-permute-start(f32[48,2304]{1,0:T(8,128)S(1)} %get-tuple-element.64), channel_id=1, source_target_pairs={{0,32},{1,129},{2,170},{3,107},{4,164},{5,197},{6,14},{8,40},{9,13... | collective-permute-start | bytes 1327112 | tf_op jit(solution)/shard_map/ppermute | solution.py:296
  66.8 3.6 %collective-permute-start.12 = (f32[48,2304]{1,0:T(8,128)S(1)}, f32[48,2304]{1,0:T(8,128)S(1)}, u32[]{:S(2)}, u32[]{:S(2)}) collective-permute-start(f32[48,2304]{1,0:T(8,128)S(1)} %get-tuple-element.63), channel_id=1, source_target_pairs={{0,160},{1,193},{2,10},{4,36},{5,133},{6,174},{7,111},{8,168},{9,2... | collective-permute-start | bytes 1327112 | tf_op jit(solution)/shard_map/ppermute | solution.py:296
  70.5 4.7 %collective-permute-done.13.c1 = f32[48,2304]{1,0:T(8,128)S(1)} collective-permute-done((f32[48,2304]{1,0:T(8,128)S(1)}, f32[48,2304]{1,0:T(8,128)S(1)}, u32[]{:S(2)}, u32[]{:S(2)}) %collective-permute-start.13) | collective-permute-done | bytes 442400 | tf_op jit(solution)/shard_map/ppermute | solution.py:296
  75.2 10.6 %collective-permute-done.12.c0 = f32[48,2304]{1,0:T(8,128)S(1)} collective-permute-done((f32[48,2304]{1,0:T(8,128)S(1)}, f32[48,2304]{1,0:T(8,128)S(1)}, u32[]{:S(2)}, u32[]{:S(2)}) %collective-permute-start.12) | collective-permute-done | bytes 442400 | tf_op jit(solution)/shard_map/ppermute | solution.py:296
  86.3 1.4 %collective-permute-start.14 = (f32[24,1152]{1,0:T(8,128)S(1)}, f32[24,1152]{1,0:T(8,128)S(1)}, u32[]{:S(2)}, u32[]{:S(2)}) collective-permute-start(f32[24,1152]{1,0:T(8,128)S(1)} %get-tuple-element.66), channel_id=1, source_target_pairs={{4,0},{5,1},{6,2},{7,3},{0,4},{1,5},{2,6},{3,7},{12,8},{13,9},{14,... | collective-permute-start | bytes 331784 | tf_op jit(solution)/shard_map/ppermute | solution.py:249
  87.7 5.0 %collective-permute-start.16 = (f32[24,1152]{1,0:T(8,128)S(1)}, f32[24,1152]{1,0:T(8,128)S(1)}, u32[]{:S(2)}, u32[]{:S(2)}) collective-permute-start(f32[24,1152]{1,0:T(8,128)S(1)} %get-tuple-element.68), channel_id=1, source_target_pairs={{3,0},{4,1},{5,2},{6,3},{7,4},{0,5},{1,6},{2,7},{11,8},{12,9},{13,... | collective-permute-start | bytes 331784 | tf_op jit(solution)/shard_map/ppermute | solution.py:249
  92.7 3.2 %collective-permute-start.17 = (f32[24,1152]{1,0:T(8,128)S(1)}, f32[24,1152]{1,0:T(8,128)S(1)}, u32[]{:S(2)}, u32[]{:S(2)}) collective-permute-start(f32[24,1152]{1,0:T(8,128)S(1)} %get-tuple-element.69), channel_id=1, source_target_pairs={{6,0},{7,1},{0,2},{1,3},{2,4},{3,5},{4,6},{5,7},{14,8},{15,9},{8,1... | collective-permute-start | bytes 331784 | tf_op jit(solution)/shard_map/ppermute | solution.py:249
  96.0 3.5 %collective-permute-start.18 = (f32[24,1152]{1,0:T(8,128)S(1)}, f32[24,1152]{1,0:T(8,128)S(1)}, u32[]{:S(2)}, u32[]{:S(2)}) collective-permute-start(f32[24,1152]{1,0:T(8,128)S(1)} %get-tuple-element.70), channel_id=1, source_target_pairs={{2,0},{3,1},{4,2},{5,3},{6,4},{7,5},{0,6},{1,7},{10,8},{11,9},{12,... | collective-permute-start | bytes 331784 | tf_op jit(solution)/shard_map/ppermute | solution.py:249
  100.0 2.9 %collective-permute-done.15.refs_2_ = f32[24,1152]{1,0:T(8,128)S(1)} collective-permute-done((f32[24,1152]{1,0:T(8,128)S(1)}, f32[24,1152]{1,0:T(8,128)S(1)}, u32[]{:S(2)}, u32[]{:S(2)}) %collective-permute-start.15) | collective-permute-done | bytes 110624 | tf_op jit(solution)/shard_map/ppermute | solution.py:249
  102.9 2.4 %collective-permute-done.16.refs_3_ = f32[24,1152]{1,0:T(8,128)S(1)} collective-permute-done((f32[24,1152]{1,0:T(8,128)S(1)}, f32[24,1152]{1,0:T(8,128)S(1)}, u32[]{:S(2)}, u32[]{:S(2)}) %collective-permute-start.16) | collective-permute-done | bytes 110624 | tf_op jit(solution)/shard_map/ppermute | solution.py:249
  105.3 4.2 %collective-permute-done.17.refs_4_ = f32[24,1152]{1,0:T(8,128)S(1)} collective-permute-done((f32[24,1152]{1,0:T(8,128)S(1)}, f32[24,1152]{1,0:T(8,128)S(1)}, u32[]{:S(2)}, u32[]{:S(2)}) %collective-permute-start.17) | collective-permute-done | bytes 110624 | tf_op jit(solution)/shard_map/ppermute | solution.py:249
  109.5 2.3 %collective-permute-done.19.refs_6_ = f32[24,1152]{1,0:T(8,128)S(1)} collective-permute-done((f32[24,1152]{1,0:T(8,128)S(1)}, f32[24,1152]{1,0:T(8,128)S(1)}, u32[]{:S(2)}, u32[]{:S(2)}) %collective-permute-start.19) | collective-permute-done | bytes 110624 | tf_op jit(solution)/shard_map/ppermute | solution.py:249
  112.0 0.9 collective-permute-start.21
  112.9 5.0 %collective-permute-done.21 = f32[2,3,2304]{2,1,0:T(4,128)S(1)} collective-permute-done((f32[2,3,2304]{2,1,0:T(4,128)S(1)}, f32[2,3,2304]{2,1,0:T(4,128)S(1)}, u32[]{:S(2)}, u32[]{:S(2)}) %collective-permute-start.21) | collective-permute-done | bytes 55328 | tf_op jit(solution)/shard_map/ppermute | solution.py:249
  118.0 0.7 copy.7
  (42 shorter events, 2.3 us)
Async XLA Ops:
  0.0 46.9 %copy-start.1 = (bf16[96,96]{1,0:T(8,128)(2,1)S(1)}, bf16[96,96]{1,0:T(8,128)(2,1)}, u32[]{:S(2)}) copy-start(bf16[96,96]{1,0:T(8,128)(2,1)} %constant.178.fz) | copy-start | bytes 55300
  0.0 46.9 %copy-start.2 = (bf16[96,96]{1,0:T(8,128)(2,1)S(1)}, bf16[96,96]{1,0:T(8,128)(2,1)}, u32[]{:S(2)}) copy-start(bf16[96,96]{1,0:T(8,128)(2,1)} %constant.186.iz) | copy-start | bytes 55300
  0.0 28.0 %copy-start = (s32[4]{0:T(128)S(1)}, s32[4]{0:T(128)}, u32[]{:S(2)}) copy-start(s32[4]{0:T(128)} %occupation.1) | copy-start | bytes 52
  1.0 5.9 %collective-permute-start = (f32[2,3,2304]{2,1,0:T(4,128)S(1)}, f32[2,3,2304]{2,1,0:T(4,128)S(1)}, u32[]{:S(2)}, u32[]{:S(2)}) collective-permute-start(f32[2,3,2304]{2,1,0:T(4,128)S(1)} %constant_dynamic-slice_fusion), channel_id=1, source_target_pairs={{8,0},{9,1},{10,2},{11,3},{12,4},{13,5},{14,6},{15,7},{0,8},{1,9},... | collective-permute-start | bytes 165896 | tf_op jit(solution)/shard_map/ppermute | solution.py:249
  7.0 10.3 %collective-permute-start.2 = (f32[24,1152]{1,0:T(8,128)S(1)}, f32[24,1152]{1,0:T(8,128)S(1)}, u32[]{:S(2)}, u32[]{:S(2)}) collective-permute-start(f32[24,1152]{1,0:T(8,128)S(1)} %shard_map.46.refs_0_), channel_id=1, source_target_pairs={{2,0},{3,1},{4,2},{5,3},{6,4},{7,5},{0,6},{1,7},{10,8},{11,9},{12,... | collective-permute-start | bytes 331784 | tf_op jit(solution)/shard_map/ppermute | solution.py:249
  13.4 8.7 %collective-permute-start.5 = (f32[24,1152]{1,0:T(8,128)S(1)}, f32[24,1152]{1,0:T(8,128)S(1)}, u32[]{:S(2)}, u32[]{:S(2)}) collective-permute-start(f32[24,1152]{1,0:T(8,128)S(1)} %shard_map.46.refs_0_), channel_id=1, source_target_pairs={{6,0},{7,1},{0,2},{1,3},{2,4},{3,5},{4,6},{5,7},{14,8},{15,9},{8,1... | collective-permute-start | bytes 331784 | tf_op jit(solution)/shard_map/ppermute | solution.py:249
  13.5 10.7 %collective-permute-start.1 = (f32[24,1152]{1,0:T(8,128)S(1)}, f32[24,1152]{1,0:T(8,128)S(1)}, u32[]{:S(2)}, u32[]{:S(2)}) collective-permute-start(f32[24,1152]{1,0:T(8,128)S(1)} %shard_map.46.refs_0_), channel_id=1, source_target_pairs={{1,0},{2,1},{3,2},{4,3},{5,4},{6,5},{7,6},{0,7},{9,8},{10,9},{11,1... | collective-permute-start | bytes 331784 | tf_op jit(solution)/shard_map/ppermute | solution.py:249
  17.2 7.0 %collective-permute-start.7 = (f32[24,1152]{1,0:T(8,128)S(1)}, f32[24,1152]{1,0:T(8,128)S(1)}, u32[]{:S(2)}, u32[]{:S(2)}) collective-permute-start(f32[24,1152]{1,0:T(8,128)S(1)} %shard_map.46.refs_0_), channel_id=1, source_target_pairs={{7,0},{0,1},{1,2},{2,3},{3,4},{4,5},{5,6},{6,7},{15,8},{8,9},{9,10... | collective-permute-start | bytes 331784 | tf_op jit(solution)/shard_map/ppermute | solution.py:249
  17.3 6.9 %collective-permute-start.3 = (f32[24,1152]{1,0:T(8,128)S(1)}, f32[24,1152]{1,0:T(8,128)S(1)}, u32[]{:S(2)}, u32[]{:S(2)}) collective-permute-start(f32[24,1152]{1,0:T(8,128)S(1)} %collective-permute-done.2.refs_2_), channel_id=1, source_target_pairs={{1,0},{2,1},{3,2},{4,3},{5,4},{6,5},{7,6},{0,7},{9,8},{10,9},{11,1... | collective-permute-start | bytes 331784 | tf_op jit(solution)/shard_map/ppermute | solution.py:249
  20.4 6.7 %collective-permute-start.4 = (f32[24,1152]{1,0:T(8,128)S(1)}, f32[24,1152]{1,0:T(8,128)S(1)}, u32[]{:S(2)}, u32[]{:S(2)}) collective-permute-start(f32[24,1152]{1,0:T(8,128)S(1)} %collective-permute-done.2.refs_2_), channel_id=1, source_target_pairs={{2,0},{3,1},{4,2},{5,3},{6,4},{7,5},{0,6},{1,7},{10,8},{11,9},{12,... | collective-permute-start | bytes 331784 | tf_op jit(solution)/shard_map/ppermute | solution.py:249
  22.1 6.0 %collective-permute-start.6 = (f32[24,1152]{1,0:T(8,128)S(1)}, f32[24,1152]{1,0:T(8,128)S(1)}, u32[]{:S(2)}, u32[]{:S(2)}) collective-permute-start(f32[24,1152]{1,0:T(8,128)S(1)} %collective-permute-done.5.refs_6_), channel_id=1, source_target_pairs={{7,0},{0,1},{1,2},{2,3},{3,4},{4,5},{5,6},{6,7},{15,8},{8,9},{9,10... | collective-permute-start | bytes 331784 | tf_op jit(solution)/shard_map/ppermute | solution.py:249
  28.8 18.1 %collective-permute-start.8 = (f32[2,48,2432]{2,1,0:T(8,128)S(1)}, f32[2,48,2432]{2,1,0:T(8,128)S(1)}, u32[]{:S(2)}, u32[]{:S(2)}) collective-permute-start(f32[2,48,2432]{2,1,0:T(8,128)S(1)} %get-tuple-element.49.own), channel_id=1, source_target_pairs={{16,0},{0,16},{48,32},{32,48},{80,64},{64,80},{112,96},{96,112},{1... | collective-permute-start | bytes 2801672 | tf_op jit(solution)/shard_map/ppermute | solution.py:249
  28.9 14.7 %collective-permute-start.9 = (f32[48,2432]{1,0:T(8,128)S(1)}, f32[48,2432]{1,0:T(8,128)S(1)}, u32[]{:S(2)}, u32[]{:S(2)}) collective-permute-start(f32[48,2432]{1,0:T(8,128)S(1)} %get-tuple-element.51), channel_id=1, source_target_pairs={{160,0},{193,1},{10,2},{67,3},{36,4},{133,5},{174,6},{111,7},{168,... | collective-permute-start | bytes 1400840 | tf_op jit(solution)/shard_map/ppermute | solution.py:335
  43.7 11.7 %collective-permute-start.10 = (f32[48,2432]{1,0:T(8,128)S(1)}, f32[48,2432]{1,0:T(8,128)S(1)}, u32[]{:S(2)}, u32[]{:S(2)}) collective-permute-start(f32[48,2432]{1,0:T(8,128)S(1)} %get-tuple-element.52), channel_id=1, source_target_pairs={{32,0},{129,1},{170,2},{107,3},{164,4},{197,5},{14,6},{71,7},{40,8... | collective-permute-start | bytes 1400840 | tf_op jit(solution)/shard_map/ppermute | solution.py:338
  63.6 22.2 %collective-permute-start.11 = (f32[2,48,2304]{2,1,0:T(8,128)S(1)}, f32[2,48,2304]{2,1,0:T(8,128)S(1)}, u32[]{:S(2)}, u32[]{:S(2)}) collective-permute-start(f32[2,48,2304]{2,1,0:T(8,128)S(1)} %get-tuple-element.62), channel_id=1, source_target_pairs={{16,0},{0,16},{48,32},{32,48},{80,64},{64,80},{112,96},{96,112},{1... | collective-permute-start | bytes 2654216 | tf_op jit(solution)/shard_map/ppermute | solution.py:249
  63.7 11.5 %collective-permute-start.13 = (f32[48,2304]{1,0:T(8,128)S(1)}, f32[48,2304]{1,0:T(8,128)S(1)}, u32[]{:S(2)}, u32[]{:S(2)}) collective-permute-start(f32[48,2304]{1,0:T(8,128)S(1)} %get-tuple-element.64), channel_id=1, source_target_pairs={{0,32},{1,129},{2,170},{3,107},{4,164},{5,197},{6,14},{8,40},{9,13... | collective-permute-start | bytes 1327112 | tf_op jit(solution)/shard_map/ppermute | solution.py:296
  66.8 19.0 %collective-permute-start.12 = (f32[48,2304]{1,0:T(8,128)S(1)}, f32[48,2304]{1,0:T(8,128)S(1)}, u32[]{:S(2)}, u32[]{:S(2)}) collective-permute-start(f32[48,2304]{1,0:T(8,128)S(1)} %get-tuple-element.63), channel_id=1, source_target_pairs={{0,160},{1,193},{2,10},{4,36},{5,133},{6,174},{7,111},{8,168},{9,2... | collective-permute-start | bytes 1327112 | tf_op jit(solution)/shard_map/ppermute | solution.py:296
  86.3 13.2 %collective-permute-start.14 = (f32[24,1152]{1,0:T(8,128)S(1)}, f32[24,1152]{1,0:T(8,128)S(1)}, u32[]{:S(2)}, u32[]{:S(2)}) collective-permute-start(f32[24,1152]{1,0:T(8,128)S(1)} %get-tuple-element.66), channel_id=1, source_target_pairs={{4,0},{5,1},{6,2},{7,3},{0,4},{1,5},{2,6},{3,7},{12,8},{13,9},{14,... | collective-permute-start | bytes 331784 | tf_op jit(solution)/shard_map/ppermute | solution.py:249
  87.7 15.2 %collective-permute-start.15 = (f32[24,1152]{1,0:T(8,128)S(1)}, f32[24,1152]{1,0:T(8,128)S(1)}, u32[]{:S(2)}, u32[]{:S(2)}) collective-permute-start(f32[24,1152]{1,0:T(8,128)S(1)} %get-tuple-element.67), channel_id=1, source_target_pairs={{5,0},{6,1},{7,2},{0,3},{1,4},{2,5},{3,6},{4,7},{13,8},{14,9},{15,... | collective-permute-start | bytes 331784 | tf_op jit(solution)/shard_map/ppermute | solution.py:249
  87.7 17.6 %collective-permute-start.16 = (f32[24,1152]{1,0:T(8,128)S(1)}, f32[24,1152]{1,0:T(8,128)S(1)}, u32[]{:S(2)}, u32[]{:S(2)}) collective-permute-start(f32[24,1152]{1,0:T(8,128)S(1)} %get-tuple-element.68), channel_id=1, source_target_pairs={{3,0},{4,1},{5,2},{6,3},{7,4},{0,5},{1,6},{2,7},{11,8},{12,9},{13,... | collective-permute-start | bytes 331784 | tf_op jit(solution)/shard_map/ppermute | solution.py:249
  92.7 16.8 %collective-permute-start.17 = (f32[24,1152]{1,0:T(8,128)S(1)}, f32[24,1152]{1,0:T(8,128)S(1)}, u32[]{:S(2)}, u32[]{:S(2)}) collective-permute-start(f32[24,1152]{1,0:T(8,128)S(1)} %get-tuple-element.69), channel_id=1, source_target_pairs={{6,0},{7,1},{0,2},{1,3},{2,4},{3,5},{4,6},{5,7},{14,8},{15,9},{8,1... | collective-permute-start | bytes 331784 | tf_op jit(solution)/shard_map/ppermute | solution.py:249
  96.0 13.5 %collective-permute-start.18 = (f32[24,1152]{1,0:T(8,128)S(1)}, f32[24,1152]{1,0:T(8,128)S(1)}, u32[]{:S(2)}, u32[]{:S(2)}) collective-permute-start(f32[24,1152]{1,0:T(8,128)S(1)} %get-tuple-element.70), channel_id=1, source_target_pairs={{2,0},{3,1},{4,2},{5,3},{6,4},{7,5},{0,6},{1,7},{10,8},{11,9},{12,... | collective-permute-start | bytes 331784 | tf_op jit(solution)/shard_map/ppermute | solution.py:249
  99.5 12.4 %collective-permute-start.19 = (f32[24,1152]{1,0:T(8,128)S(1)}, f32[24,1152]{1,0:T(8,128)S(1)}, u32[]{:S(2)}, u32[]{:S(2)}) collective-permute-start(f32[24,1152]{1,0:T(8,128)S(1)} %get-tuple-element.71), channel_id=1, source_target_pairs={{7,0},{0,1},{1,2},{2,3},{3,4},{4,5},{5,6},{6,7},{15,8},{8,9},{9,10... | collective-permute-start | bytes 331784 | tf_op jit(solution)/shard_map/ppermute | solution.py:249
  102.9 9.0 %collective-permute-start.20 = (f32[24,1152]{1,0:T(8,128)S(1)}, f32[24,1152]{1,0:T(8,128)S(1)}, u32[]{:S(2)}, u32[]{:S(2)}) collective-permute-start(f32[24,1152]{1,0:T(8,128)S(1)} %get-tuple-element.72), channel_id=1, source_target_pairs={{1,0},{2,1},{3,2},{4,3},{5,4},{6,5},{7,6},{0,7},{9,8},{10,9},{11,1... | collective-permute-start | bytes 331784 | tf_op jit(solution)/shard_map/ppermute | solution.py:249
  112.0 5.9 %collective-permute-start.21 = (f32[2,3,2304]{2,1,0:T(4,128)S(1)}, f32[2,3,2304]{2,1,0:T(4,128)S(1)}, u32[]{:S(2)}, u32[]{:S(2)}) collective-permute-start(f32[2,3,2304]{2,1,0:T(4,128)S(1)} %get-tuple-element.74), channel_id=1, source_target_pairs={{8,0},{9,1},{10,2},{11,3},{12,4},{13,5},{14,6},{15,7},{0,8},{1,9},... | collective-permute-start | bytes 165896 | tf_op jit(solution)/shard_map/ppermute | solution.py:249

commit v3 on v2

--- a/solution.py
+++ b/solution.py
@@ -76,24 +76,40 @@
                 lone[o][rows, lanes] = piece
 
 
-def disperse_body(a, b, c0, c1, *outs):
+def disperse_body(a, b, c0, c1, own, up1, up2, down1, down2, far_up, far_down):
     back = (c0, c1)
+    near = {0: own, 1: up1, 2: up2, 7: down1, 6: down2}
     for k in range(8):
         for o in range(2):
             for h in range(2):
                 r = o * 12 + h * 6
                 rows, lanes = slice(6 * k, 6 * k + 6), slice(h * HALF, (h + 1) * HALF)
-                outs[k][r:r + 6, :] = a[o, rows, lanes] + b[o, rows, lanes] + back[o][rows, lanes]
+                total = a[o, rows, lanes] + b[o, rows, lanes] + back[o][rows, lanes]
+                if k in near:
+                    near[k][r:r + 6, :] = total
+                elif k != 4:
+                    (far_up if k == 3 else far_down)[r:r + 6, :] = total
+                else:
+                    (far_down if o else far_up)[24 + h * 6:30 + h * 6, :] = total
+
+
+def merge_body(up1, up2, down1, down2, far_up, far_down, to_up1, to_up2, to_down1, to_down2):
+    to_up1[...] = up1[...] + far_up[:24, :]
+    to_down1[...] = down1[...] + far_down[:24, :]
+    to_up2[:12, :] = up2[:12, :] + far_up[24:, :]
+    to_up2[12:, :] = up2[12:, :]
+    to_down2[:12, :] = down2[:12, :]
+    to_down2[12:, :] = down2[12:, :] + far_down[24:, :]
 
 
 def unpack_body(y, *refs):
-    keep, give = refs[8:]
+    keep, give = refs[5:]
     flip = y[0] != 0
     for o in range(2):
         for h in range(2):
             r = o * 12 + h * 6
             total = refs[0][r:r + 6, :]
-            for k in range(1, 8):
+            for k in range(1, 5):
                 total = total + refs[k][r:r + 6, :]
             a, b = total[:3], total[3:]
             keep[o, :, h * HALF:(h + 1) * HALF] = jnp.where(flip, b, a)
@@ -125,11 +141,11 @@
         spec[:, pl.ds(pl.multiple_of(yb * YB, YB), YB), :] = jnp.swapaxes(zed[...], 0, 1)
 
     def enter(k, _):
-        for u in range(3):
-            enter_one(k * 3 + u, *bufs[u % 2 * 3:u % 2 * 3 + 3])
+        for u in range(6):
+            enter_one(k * 6 + u, *bufs[u % 2 * 3:u % 2 * 3 + 3])
         return 0
 
-    lax.fori_loop(0, G // YB // 3, enter, 0)
+    lax.fori_loop(0, G // YB // 6, enter, 0)
 
     def half_in(kz):
         return apply(fz[...], spec[kz]) * ktab[kz]
@@ -186,11 +202,11 @@
             away[gi & 1, :, lanes] = away[gi & 1, :, lanes] + p * wt
 
     def leave(k, _):
-        for u in range(3):
-            leave_one(k * 3 + u, *bufs[u % 2 * 3:u % 2 * 3 + 3])
+        for u in range(6):
+            leave_one(k * 6 + u, *bufs[u % 2 * 3:u % 2 * 3 + 3])
         return 0
 
-    lax.fori_loop(0, G // YB // 3, leave, 0)
+    lax.fori_loop(0, G // YB // 6, leave, 0)
 
 
 def pair_solver(first, *args):
@@ -306,8 +322,14 @@
     return [got[k] for k in range(8)]
 
 
-def scatter_blocks(part):
-    return [part[0]] + [ring(part[k], "grid", along(-k)) for k in (4, 3, 5, 2, 6, 1, 7)]
+def scatter_blocks(own, up1, up2, down1, down2, far_up, far_down):
+    far_up = ring(far_up, "grid", along(-2))
+    far_down = ring(far_down, "grid", along(2))
+    up1, up2, down1, down2 = small_call(
+        merge_body, [f32(24, HALF)] * 4, up1, up2, down1, down2, far_up, far_down
+    )
+    hops = ((up2, -2), (down2, 2), (up1, -1), (down1, 1))
+    return [own] + [ring(block, "grid", along(hop)) for block, hop in hops]
 
 
 def on_device(orbitals, occupation, cutoff):
@@ -342,8 +364,8 @@
     home, away, back = pair_solver(False, idx, own, twin, vis1, *tables, home, away)
     ret1 = returned(back, 1)
     swapped = ring(away, "band", twin_of)
-    part = small_call(disperse_body, [f32(24, HALF)] * 8, home, swapped, ret0, ret1)
-    keep, give = small_call(unpack_body, [f32(2, 3, ROW)] * 2, y1, *scatter_blocks(part), scalars=1)
+    part = small_call(disperse_body, [f32(24, HALF)] * 5 + [f32(36, HALF)] * 2, home, swapped, ret0, ret1)
+    keep, give = small_call(unpack_body, [f32(2, 3, ROW)] * 2, y1, *scatter_blocks(*part), scalars=1)
     came = ring(give, "grid", partner)
     return jnp.concatenate([jnp.where(y == 0, keep, came), jnp.where(y == 0, came, keep)], axis=0)
 

time: 119 us -> 118 us (level)
  the two profiles are of different devices: /device:TPU:8 before, /device:TPU:7 now
where the time goes in v3:
time: 118 us; the launch traced here: 115 us
  starting transfers between devices  48.5 us (41%)
  waiting for transfers between devices  45.1 us (38%)
  Pallas kernels  16.9 us (14%)
  other arithmetic  2.15 us (2%)
  local copies, waits for them, and re-layouts  1.66 us (1%)
    ppermute x17, starting transfers between devices, ring(): lax.ppermute(block, axis, [(source(i), i) for i in range(lax.axis_size(ax...  37.8 us
    ppermute x17, waiting for transfers between devices, ring(): lax.ppermute(block, axis, [(source(i), i) for i in range(lax.axis_size(ax...  19.5 us
    pallas_call x2, Pallas kernels, pair_solver(): pl.pallas_call(functools.partial(kernel, first), out_shape=[f32(2, G, ROW...  15.5 us
    ppermute x1, waiting for transfers between devices, on_device(): vis0 = lax.ppermute(lone[0], axes, visit_route(0))  12.7 us
    ppermute x2, waiting for transfers between devices, returned(): lax.ppermute(back, ('band', 'grid'), [(d, s) for s, d in visit_route(v, F...  11 us
    ppermute x2, starting transfers between devices, returned(): lax.ppermute(back, ('band', 'grid'), [(d, s) for s, d in visit_route(v, F...  8.96 us
  transfers between devices with their start and end apart: 21, of which 12 were waited for; matrix products, arithmetic and copies ran while one was open for 2% of the time, Pallas kernels for 7%

profile of v3, /device:TPU:7, one launch (start us, length us, event | category | flops | bytes accessed | tf_op | source)
XLA Modules:
  0.0 115.2 jit_solution(16645713000093426090)
XLA Ops:
  0.0 1.0 copy.6.slab
  1.0 3.0 %collective-permute-start = (f32[2,3,2304]{2,1,0:T(4,128)S(1)}, f32[2,3,2304]{2,1,0:T(4,128)S(1)}, u32[]{:S(2)}, u32[]{:S(2)}) collective-permute-start(f32[2,3,2304]{2,1,0:T(4,128)S(1)} %constant_dynamic-slice_fusion), channel_id=1, source_target_pairs={{8,0},{9,1},{10,2},{11,3},{12,4},{13,5},{14,6},{15,7},{0,8},{1,9},... | collective-permute-start | bytes 165896 | tf_op jit(solution)/shard_map/ppermute | solution.py:265
  4.9 1.4 %fusion.9.ktab = f32[48,48,256]{2,1,0:T(8,128)S(1)} fusion(f32[256]{0:T(256)S(1)} %or_select_fusion, f32[48,48]{1,0:T(8,128)S(1)} %broadcast_multiply_fusion, s32[]{:T(128)S(6)} %copy.8, s32[256]{0:T(256)S(1)} %fusion.26, s32[48,48]{1,0:T(8,128)S(1)} %broadcast_add_fusion), kind=kLoop, calls=%fused_computation.12 | loop fusion | flops 8847360 | bytes 2379780 | tf_op jit(solution)/shard_map/jit(_where)/select_n | solution.py:261
  6.8 6.1 %collective-permute-start.2 = (f32[24,1152]{1,0:T(8,128)S(1)}, f32[24,1152]{1,0:T(8,128)S(1)}, u32[]{:S(2)}, u32[]{:S(2)}) collective-permute-start(f32[24,1152]{1,0:T(8,128)S(1)} %shard_map.46.refs_0_), channel_id=1, source_target_pairs={{2,0},{3,1},{4,2},{5,3},{6,4},{7,5},{0,6},{1,7},{10,8},{11,9},{12,... | collective-permute-start | bytes 331784 | tf_op jit(solution)/shard_map/ppermute | solution.py:265
  12.9 3.2 %collective-permute-start.1 = (f32[24,1152]{1,0:T(8,128)S(1)}, f32[24,1152]{1,0:T(8,128)S(1)}, u32[]{:S(2)}, u32[]{:S(2)}) collective-permute-start(f32[24,1152]{1,0:T(8,128)S(1)} %shard_map.46.refs_0_), channel_id=1, source_target_pairs={{1,0},{2,1},{3,2},{4,3},{5,4},{6,5},{7,6},{0,7},{9,8},{10,9},{11,1... | collective-permute-start | bytes 331784 | tf_op jit(solution)/shard_map/ppermute | solution.py:265
  16.1 3.9 %collective-permute-start.3 = (f32[24,1152]{1,0:T(8,128)S(1)}, f32[24,1152]{1,0:T(8,128)S(1)}, u32[]{:S(2)}, u32[]{:S(2)}) collective-permute-start(f32[24,1152]{1,0:T(8,128)S(1)} %collective-permute-done.2.refs_2_), channel_id=1, source_target_pairs={{1,0},{2,1},{3,2},{4,3},{5,4},{6,5},{7,6},{0,7},{9,8},{10,9},{11,1... | collective-permute-start | bytes 331784 | tf_op jit(solution)/shard_map/ppermute | solution.py:265
  20.1 1.4 %collective-permute-start.6 = (f32[24,1152]{1,0:T(8,128)S(1)}, f32[24,1152]{1,0:T(8,128)S(1)}, u32[]{:S(2)}, u32[]{:S(2)}) collective-permute-start(f32[24,1152]{1,0:T(8,128)S(1)} %collective-permute-done.5.refs_6_), channel_id=1, source_target_pairs={{7,0},{0,1},{1,2},{2,3},{3,4},{4,5},{5,6},{6,7},{15,8},{8,9},{9,10... | collective-permute-start | bytes 331784 | tf_op jit(solution)/shard_map/ppermute | solution.py:265
  21.6 2.0 %collective-permute-done.7.refs_7_ = f32[24,1152]{1,0:T(8,128)S(1)} collective-permute-done((f32[24,1152]{1,0:T(8,128)S(1)}, f32[24,1152]{1,0:T(8,128)S(1)}, u32[]{:S(2)}, u32[]{:S(2)}) %collective-permute-start.7) | collective-permute-done | bytes 110624 | tf_op jit(solution)/shard_map/ppermute | solution.py:265
  23.6 2.8 %collective-permute-done.4.refs_4_ = f32[24,1152]{1,0:T(8,128)S(1)} collective-permute-done((f32[24,1152]{1,0:T(8,128)S(1)}, f32[24,1152]{1,0:T(8,128)S(1)}, u32[]{:S(2)}, u32[]{:S(2)}) %collective-permute-start.4) | collective-permute-done | bytes 110624 | tf_op jit(solution)/shard_map/ppermute | solution.py:265
  26.4 0.8 shard_map.47
  27.2 3.9 %collective-permute-start.8 = (f32[2,48,2432]{2,1,0:T(8,128)S(1)}, f32[2,48,2432]{2,1,0:T(8,128)S(1)}, u32[]{:S(2)}, u32[]{:S(2)}) collective-permute-start(f32[2,48,2432]{2,1,0:T(8,128)S(1)} %get-tuple-element.52.own), channel_id=1, source_target_pairs={{16,0},{0,16},{48,32},{32,48},{80,64},{64,80},{112,96},{96,112},{1... | collective-permute-start | bytes 2801672 | tf_op jit(solution)/shard_map/ppermute | solution.py:265
  31.1 1.5 %collective-permute-start.9 = (f32[48,2432]{1,0:T(8,128)S(1)}, f32[48,2432]{1,0:T(8,128)S(1)}, u32[]{:S(2)}, u32[]{:S(2)}) collective-permute-start(f32[48,2432]{1,0:T(8,128)S(1)} %get-tuple-element.54), channel_id=1, source_target_pairs={{160,0},{193,1},{10,2},{67,3},{36,4},{133,5},{174,6},{111,7},{168,... | collective-permute-start | bytes 1400840 | tf_op jit(solution)/shard_map/ppermute | solution.py:357
  32.6 12.7 %collective-permute-done.9.vis = f32[48,2432]{1,0:T(8,128)S(1)} collective-permute-done((f32[48,2432]{1,0:T(8,128)S(1)}, f32[48,2432]{1,0:T(8,128)S(1)}, u32[]{:S(2)}, u32[]{:S(2)}) %collective-permute-start.9) | collective-permute-done | bytes 466976 | tf_op jit(solution)/shard_map/ppermute | solution.py:357
  45.5 7.8 %shard_map.48 = (f32[2,48,2304]{2,1,0:T(8,128)S(1)}, f32[2,48,2304]{2,1,0:T(8,128)S(1)}, f32[48,2304]{1,0:T(8,128)S(1)}) custom-call(s32[4]{0:T(128)S(1)} %pad_add_fusion.idx, f32[2,48,2432]{2,1,0:T(8,128)S(1)} %get-tuple-element.52.own, f32[2,48,2432]{2,1,0:T(8,128)S(1)} %collective-permute-done.8.twin, f32[48,2432]{1,0:T(8,128)S(1)} %collective-permute-done.9.vis, ...), custom_call_target="tpu_custom_call" | custom-call | flops 5000000000 | bytes 10000000 | tf_op jit(solution)/shard_map/pallas_call | solution.py:213
  53.3 1.8 %collective-permute-done.10.vis = f32[48,2432]{1,0:T(8,128)S(1)} collective-permute-done((f32[48,2432]{1,0:T(8,128)S(1)}, f32[48,2432]{1,0:T(8,128)S(1)}, u32[]{:S(2)}, u32[]{:S(2)}) %collective-permute-start.10) | collective-permute-done | bytes 466976 | tf_op jit(solution)/shard_map/ppermute | solution.py:360
  55.2 7.6 %shard_map.49 = (f32[2,48,2304]{2,1,0:T(8,128)S(1)}, f32[2,48,2304]{2,1,0:T(8,128)S(1)}, f32[48,2304]{1,0:T(8,128)S(1)}) custom-call(s32[4]{0:T(128)S(1)} %pad_add_fusion.idx, f32[2,48,2432]{2,1,0:T(8,128)S(1)} %get-tuple-element.52.own, f32[2,48,2432]{2,1,0:T(8,128)S(1)} %collective-permute-done.8.twin, f32[48,2432]{1,0:T(8,128)S(1)} %collective-permute-done.10.vis, ...), custom_call_target="tpu_custom_call" | custom-call | flops 5000000000 | bytes 10000000 | tf_op jit(solution)/shard_map/pallas_call | solution.py:213
  62.8 1.0 collective-permute-start.11
  63.8 2.9 %collective-permute-start.13 = (f32[48,2304]{1,0:T(8,128)S(1)}, f32[48,2304]{1,0:T(8,128)S(1)}, u32[]{:S(2)}, u32[]{:S(2)}) collective-permute-start(f32[48,2304]{1,0:T(8,128)S(1)} %get-tuple-element.67), channel_id=1, source_target_pairs={{0,32},{1,129},{2,170},{3,107},{4,164},{5,197},{6,14},{8,40},{9,13... | collective-permute-start | bytes 1327112 | tf_op jit(solution)/shard_map/ppermute | solution.py:312
  66.7 6.0 %collective-permute-start.12 = (f32[48,2304]{1,0:T(8,128)S(1)}, f32[48,2304]{1,0:T(8,128)S(1)}, u32[]{:S(2)}, u32[]{:S(2)}) collective-permute-start(f32[48,2304]{1,0:T(8,128)S(1)} %get-tuple-element.66), channel_id=1, source_target_pairs={{0,160},{1,193},{2,10},{4,36},{5,133},{6,174},{7,111},{8,168},{9,2... | collective-permute-start | bytes 1327112 | tf_op jit(solution)/shard_map/ppermute | solution.py:312
  72.8 5.7 %collective-permute-done.13.c1 = f32[48,2304]{1,0:T(8,128)S(1)} collective-permute-done((f32[48,2304]{1,0:T(8,128)S(1)}, f32[48,2304]{1,0:T(8,128)S(1)}, u32[]{:S(2)}, u32[]{:S(2)}) %collective-permute-start.13) | collective-permute-done | bytes 442400 | tf_op jit(solution)/shard_map/ppermute | solution.py:312
  78.5 5.3 %collective-permute-done.12.c0 = f32[48,2304]{1,0:T(8,128)S(1)} collective-permute-done((f32[48,2304]{1,0:T(8,128)S(1)}, f32[48,2304]{1,0:T(8,128)S(1)}, u32[]{:S(2)}, u32[]{:S(2)}) %collective-permute-start.12) | collective-permute-done | bytes 442400 | tf_op jit(solution)/shard_map/ppermute | solution.py:312
  83.8 0.5 shard_map.50
  84.6 3.6 %collective-permute-start.15 = (f32[36,1152]{1,0:T(8,128)S(1)}, f32[36,1152]{1,0:T(8,128)S(1)}, u32[]{:S(2)}, u32[]{:S(2)}) collective-permute-start(f32[36,1152]{1,0:T(8,128)S(1)} %get-tuple-element.74), channel_id=1, source_target_pairs={{2,0},{3,1},{4,2},{5,3},{6,4},{7,5},{0,6},{1,7},{10,8},{11,9},{12,... | collective-permute-start | bytes 497672 | tf_op jit(solution)/shard_map/ppermute | solution.py:265
  88.1 3.0 %collective-permute-done.14.far_up = f32[36,1152]{1,0:T(8,128)S(1)} collective-permute-done((f32[36,1152]{1,0:T(8,128)S(1)}, f32[36,1152]{1,0:T(8,128)S(1)}, u32[]{:S(2)}, u32[]{:S(2)}) %collective-permute-start.14) | collective-permute-done | bytes 165920 | tf_op jit(solution)/shard_map/ppermute | solution.py:265
  91.2 0.6 collective-permute-done.15.far_down
  91.8 2.7 %collective-permute-start.16 = (f32[24,1152]{1,0:T(8,128)S(1)}, f32[24,1152]{1,0:T(8,128)S(1)}, u32[]{:S(2)}, u32[]{:S(2)}) collective-permute-start(f32[24,1152]{1,0:T(8,128)S(1)} %get-tuple-element.75), channel_id=1, source_target_pairs={{6,0},{7,1},{0,2},{1,3},{2,4},{3,5},{4,6},{5,7},{14,8},{15,9},{8,1... | collective-permute-start | bytes 331784 | tf_op jit(solution)/shard_map/ppermute | solution.py:265
  94.5 1.2 %collective-permute-start.17 = (f32[24,1152]{1,0:T(8,128)S(1)}, f32[24,1152]{1,0:T(8,128)S(1)}, u32[]{:S(2)}, u32[]{:S(2)}) collective-permute-start(f32[24,1152]{1,0:T(8,128)S(1)} %get-tuple-element.76), channel_id=1, source_target_pairs={{2,0},{3,1},{4,2},{5,3},{6,4},{7,5},{0,6},{1,7},{10,8},{11,9},{12,... | collective-permute-start | bytes 331784 | tf_op jit(solution)/shard_map/ppermute | solution.py:265
  95.7 7.6 %collective-permute-start.18 = (f32[24,1152]{1,0:T(8,128)S(1)}, f32[24,1152]{1,0:T(8,128)S(1)}, u32[]{:S(2)}, u32[]{:S(2)}) collective-permute-start(f32[24,1152]{1,0:T(8,128)S(1)} %get-tuple-element.77), channel_id=1, source_target_pairs={{7,0},{0,1},{1,2},{2,3},{3,4},{4,5},{5,6},{6,7},{15,8},{8,9},{9,10... | collective-permute-start | bytes 331784 | tf_op jit(solution)/shard_map/ppermute | solution.py:265
  103.3 5.3 %collective-permute-done.18.refs_3_ = f32[24,1152]{1,0:T(8,128)S(1)} collective-permute-done((f32[24,1152]{1,0:T(8,128)S(1)}, f32[24,1152]{1,0:T(8,128)S(1)}, u32[]{:S(2)}, u32[]{:S(2)}) %collective-permute-start.18) | collective-permute-done | bytes 110624 | tf_op jit(solution)/shard_map/ppermute | solution.py:265
  108.6 0.9 collective-permute-done.19.refs_4_
  109.8 4.7 %collective-permute-done.20 = f32[2,3,2304]{2,1,0:T(4,128)S(1)} collective-permute-done((f32[2,3,2304]{2,1,0:T(4,128)S(1)}, f32[2,3,2304]{2,1,0:T(4,128)S(1)}, u32[]{:S(2)}, u32[]{:S(2)}) %collective-permute-start.20) | collective-permute-done | bytes 55328 | tf_op jit(solution)/shard_map/ppermute | solution.py:265
  114.5 0.7 copy.7
  (41 shorter events, 1.6 us)
Async XLA Ops:
  0.0 45.5 %copy-start.1 = (bf16[96,96]{1,0:T(8,128)(2,1)S(1)}, bf16[96,96]{1,0:T(8,128)(2,1)}, u32[]{:S(2)}) copy-start(bf16[96,96]{1,0:T(8,128)(2,1)} %constant.178.fz) | copy-start | bytes 55300
  0.0 45.5 %copy-start.2 = (bf16[96,96]{1,0:T(8,128)(2,1)S(1)}, bf16[96,96]{1,0:T(8,128)(2,1)}, u32[]{:S(2)}) copy-start(bf16[96,96]{1,0:T(8,128)(2,1)} %constant.186.iz) | copy-start | bytes 55300
  0.0 26.4 %copy-start = (s32[4]{0:T(128)S(1)}, s32[4]{0:T(128)}, u32[]{:S(2)}) copy-start(s32[4]{0:T(128)} %occupation.1) | copy-start | bytes 52
  1.0 5.7 %collective-permute-start = (f32[2,3,2304]{2,1,0:T(4,128)S(1)}, f32[2,3,2304]{2,1,0:T(4,128)S(1)}, u32[]{:S(2)}, u32[]{:S(2)}) collective-permute-start(f32[2,3,2304]{2,1,0:T(4,128)S(1)} %constant_dynamic-slice_fusion), channel_id=1, source_target_pairs={{8,0},{9,1},{10,2},{11,3},{12,4},{13,5},{14,6},{15,7},{0,8},{1,9},... | collective-permute-start | bytes 165896 | tf_op jit(solution)/shard_map/ppermute | solution.py:265
  6.8 9.4 %collective-permute-start.2 = (f32[24,1152]{1,0:T(8,128)S(1)}, f32[24,1152]{1,0:T(8,128)S(1)}, u32[]{:S(2)}, u32[]{:S(2)}) collective-permute-start(f32[24,1152]{1,0:T(8,128)S(1)} %shard_map.46.refs_0_), channel_id=1, source_target_pairs={{2,0},{3,1},{4,2},{5,3},{6,4},{7,5},{0,6},{1,7},{10,8},{11,9},{12,... | collective-permute-start | bytes 331784 | tf_op jit(solution)/shard_map/ppermute | solution.py:265
  12.8 7.3 %collective-permute-start.5 = (f32[24,1152]{1,0:T(8,128)S(1)}, f32[24,1152]{1,0:T(8,128)S(1)}, u32[]{:S(2)}, u32[]{:S(2)}) collective-permute-start(f32[24,1152]{1,0:T(8,128)S(1)} %shard_map.46.refs_0_), channel_id=1, source_target_pairs={{6,0},{7,1},{0,2},{1,3},{2,4},{3,5},{4,6},{5,7},{14,8},{15,9},{8,1... | collective-permute-start | bytes 331784 | tf_op jit(solution)/shard_map/ppermute | solution.py:265
  12.9 8.7 %collective-permute-start.1 = (f32[24,1152]{1,0:T(8,128)S(1)}, f32[24,1152]{1,0:T(8,128)S(1)}, u32[]{:S(2)}, u32[]{:S(2)}) collective-permute-start(f32[24,1152]{1,0:T(8,128)S(1)} %shard_map.46.refs_0_), channel_id=1, source_target_pairs={{1,0},{2,1},{3,2},{4,3},{5,4},{6,5},{7,6},{0,7},{9,8},{10,9},{11,1... | collective-permute-start | bytes 331784 | tf_op jit(solution)/shard_map/ppermute | solution.py:265
  16.1 7.5 %collective-permute-start.7 = (f32[24,1152]{1,0:T(8,128)S(1)}, f32[24,1152]{1,0:T(8,128)S(1)}, u32[]{:S(2)}, u32[]{:S(2)}) collective-permute-start(f32[24,1152]{1,0:T(8,128)S(1)} %shard_map.46.refs_0_), channel_id=1, source_target_pairs={{7,0},{0,1},{1,2},{2,3},{3,4},{4,5},{5,6},{6,7},{15,8},{8,9},{9,10... | collective-permute-start | bytes 331784 | tf_op jit(solution)/shard_map/ppermute | solution.py:265
  16.1 7.5 %collective-permute-start.3 = (f32[24,1152]{1,0:T(8,128)S(1)}, f32[24,1152]{1,0:T(8,128)S(1)}, u32[]{:S(2)}, u32[]{:S(2)}) collective-permute-start(f32[24,1152]{1,0:T(8,128)S(1)} %collective-permute-done.2.refs_2_), channel_id=1, source_target_pairs={{1,0},{2,1},{3,2},{4,3},{5,4},{6,5},{7,6},{0,7},{9,8},{10,9},{11,1... | collective-permute-start | bytes 331784 | tf_op jit(solution)/shard_map/ppermute | solution.py:265
  20.0 6.4 %collective-permute-start.4 = (f32[24,1152]{1,0:T(8,128)S(1)}, f32[24,1152]{1,0:T(8,128)S(1)}, u32[]{:S(2)}, u32[]{:S(2)}) collective-permute-start(f32[24,1152]{1,0:T(8,128)S(1)} %collective-permute-done.2.refs_2_), channel_id=1, source_target_pairs={{2,0},{3,1},{4,2},{5,3},{6,4},{7,5},{0,6},{1,7},{10,8},{11,9},{12,... | collective-permute-start | bytes 331784 | tf_op jit(solution)/shard_map/ppermute | solution.py:265
  20.1 6.3 %collective-permute-start.6 = (f32[24,1152]{1,0:T(8,128)S(1)}, f32[24,1152]{1,0:T(8,128)S(1)}, u32[]{:S(2)}, u32[]{:S(2)}) collective-permute-start(f32[24,1152]{1,0:T(8,128)S(1)} %collective-permute-done.5.refs_6_), channel_id=1, source_target_pairs={{7,0},{0,1},{1,2},{2,3},{3,4},{4,5},{5,6},{6,7},{15,8},{8,9},{9,10... | collective-permute-start | bytes 331784 | tf_op jit(solution)/shard_map/ppermute | solution.py:265
  27.2 18.3 %collective-permute-start.8 = (f32[2,48,2432]{2,1,0:T(8,128)S(1)}, f32[2,48,2432]{2,1,0:T(8,128)S(1)}, u32[]{:S(2)}, u32[]{:S(2)}) collective-permute-start(f32[2,48,2432]{2,1,0:T(8,128)S(1)} %get-tuple-element.52.own), channel_id=1, source_target_pairs={{16,0},{0,16},{48,32},{32,48},{80,64},{64,80},{112,96},{96,112},{1... | collective-permute-start | bytes 2801672 | tf_op jit(solution)/shard_map/ppermute | solution.py:265
  31.1 14.3 %collective-permute-start.9 = (f32[48,2432]{1,0:T(8,128)S(1)}, f32[48,2432]{1,0:T(8,128)S(1)}, u32[]{:S(2)}, u32[]{:S(2)}) collective-permute-start(f32[48,2432]{1,0:T(8,128)S(1)} %get-tuple-element.54), channel_id=1, source_target_pairs={{160,0},{193,1},{10,2},{67,3},{36,4},{133,5},{174,6},{111,7},{168,... | collective-permute-start | bytes 1400840 | tf_op jit(solution)/shard_map/ppermute | solution.py:357
  45.3 9.8 %collective-permute-start.10 = (f32[48,2432]{1,0:T(8,128)S(1)}, f32[48,2432]{1,0:T(8,128)S(1)}, u32[]{:S(2)}, u32[]{:S(2)}) collective-permute-start(f32[48,2432]{1,0:T(8,128)S(1)} %get-tuple-element.55), channel_id=1, source_target_pairs={{32,0},{129,1},{170,2},{107,3},{164,4},{197,5},{14,6},{71,7},{40,8... | collective-permute-start | bytes 1400840 | tf_op jit(solution)/shard_map/ppermute | solution.py:360
  62.8 21.0 %collective-permute-start.11 = (f32[2,48,2304]{2,1,0:T(8,128)S(1)}, f32[2,48,2304]{2,1,0:T(8,128)S(1)}, u32[]{:S(2)}, u32[]{:S(2)}) collective-permute-start(f32[2,48,2304]{2,1,0:T(8,128)S(1)} %get-tuple-element.65), channel_id=1, source_target_pairs={{16,0},{0,16},{48,32},{32,48},{80,64},{64,80},{112,96},{96,112},{1... | collective-permute-start | bytes 2654216 | tf_op jit(solution)/shard_map/ppermute | solution.py:265
  63.8 14.7 %collective-permute-start.13 = (f32[48,2304]{1,0:T(8,128)S(1)}, f32[48,2304]{1,0:T(8,128)S(1)}, u32[]{:S(2)}, u32[]{:S(2)}) collective-permute-start(f32[48,2304]{1,0:T(8,128)S(1)} %get-tuple-element.67), channel_id=1, source_target_pairs={{0,32},{1,129},{2,170},{3,107},{4,164},{5,197},{6,14},{8,40},{9,13... | collective-permute-start | bytes 1327112 | tf_op jit(solution)/shard_map/ppermute | solution.py:312
  66.7 17.1 %collective-permute-start.12 = (f32[48,2304]{1,0:T(8,128)S(1)}, f32[48,2304]{1,0:T(8,128)S(1)}, u32[]{:S(2)}, u32[]{:S(2)}) collective-permute-start(f32[48,2304]{1,0:T(8,128)S(1)} %get-tuple-element.66), channel_id=1, source_target_pairs={{0,160},{1,193},{2,10},{4,36},{5,133},{6,174},{7,111},{8,168},{9,2... | collective-permute-start | bytes 1327112 | tf_op jit(solution)/shard_map/ppermute | solution.py:312
  84.3 6.9 %collective-permute-start.14 = (f32[36,1152]{1,0:T(8,128)S(1)}, f32[36,1152]{1,0:T(8,128)S(1)}, u32[]{:S(2)}, u32[]{:S(2)}) collective-permute-start(f32[36,1152]{1,0:T(8,128)S(1)} %get-tuple-element.73), channel_id=1, source_target_pairs={{6,0},{7,1},{0,2},{1,3},{2,4},{3,5},{4,6},{5,7},{14,8},{15,9},{8,1... | collective-permute-start | bytes 497672 | tf_op jit(solution)/shard_map/ppermute | solution.py:265
  84.6 7.2 %collective-permute-start.15 = (f32[36,1152]{1,0:T(8,128)S(1)}, f32[36,1152]{1,0:T(8,128)S(1)}, u32[]{:S(2)}, u32[]{:S(2)}) collective-permute-start(f32[36,1152]{1,0:T(8,128)S(1)} %get-tuple-element.74), channel_id=1, source_target_pairs={{2,0},{3,1},{4,2},{5,3},{6,4},{7,5},{0,6},{1,7},{10,8},{11,9},{12,... | collective-permute-start | bytes 497672 | tf_op jit(solution)/shard_map/ppermute | solution.py:265
  91.8 11.5 %collective-permute-start.16 = (f32[24,1152]{1,0:T(8,128)S(1)}, f32[24,1152]{1,0:T(8,128)S(1)}, u32[]{:S(2)}, u32[]{:S(2)}) collective-permute-start(f32[24,1152]{1,0:T(8,128)S(1)} %get-tuple-element.75), channel_id=1, source_target_pairs={{6,0},{7,1},{0,2},{1,3},{2,4},{3,5},{4,6},{5,7},{14,8},{15,9},{8,1... | collective-permute-start | bytes 331784 | tf_op jit(solution)/shard_map/ppermute | solution.py:265
  94.5 8.8 %collective-permute-start.17 = (f32[24,1152]{1,0:T(8,128)S(1)}, f32[24,1152]{1,0:T(8,128)S(1)}, u32[]{:S(2)}, u32[]{:S(2)}) collective-permute-start(f32[24,1152]{1,0:T(8,128)S(1)} %get-tuple-element.76), channel_id=1, source_target_pairs={{2,0},{3,1},{4,2},{5,3},{6,4},{7,5},{0,6},{1,7},{10,8},{11,9},{12,... | collective-permute-start | bytes 331784 | tf_op jit(solution)/shard_map/ppermute | solution.py:265
  95.7 12.9 %collective-permute-start.18 = (f32[24,1152]{1,0:T(8,128)S(1)}, f32[24,1152]{1,0:T(8,128)S(1)}, u32[]{:S(2)}, u32[]{:S(2)}) collective-permute-start(f32[24,1152]{1,0:T(8,128)S(1)} %get-tuple-element.77), channel_id=1, source_target_pairs={{7,0},{0,1},{1,2},{2,3},{3,4},{4,5},{5,6},{6,7},{15,8},{8,9},{9,10... | collective-permute-start | bytes 331784 | tf_op jit(solution)/shard_map/ppermute | solution.py:265
  103.3 6.3 %collective-permute-start.19 = (f32[24,1152]{1,0:T(8,128)S(1)}, f32[24,1152]{1,0:T(8,128)S(1)}, u32[]{:S(2)}, u32[]{:S(2)}) collective-permute-start(f32[24,1152]{1,0:T(8,128)S(1)} %get-tuple-element.78), channel_id=1, source_target_pairs={{1,0},{2,1},{3,2},{4,3},{5,4},{6,5},{7,6},{0,7},{9,8},{10,9},{11,1... | collective-permute-start | bytes 331784 | tf_op jit(solution)/shard_map/ppermute | solution.py:265
  109.7 4.8 %collective-permute-start.20 = (f32[2,3,2304]{2,1,0:T(4,128)S(1)}, f32[2,3,2304]{2,1,0:T(4,128)S(1)}, u32[]{:S(2)}, u32[]{:S(2)}) collective-permute-start(f32[2,3,2304]{2,1,0:T(4,128)S(1)} %get-tuple-element.80), channel_id=1, source_target_pairs={{8,0},{9,1},{10,2},{11,3},{12,4},{13,5},{14,6},{15,7},{0,8},{1,9},... | collective-permute-start | bytes 165896 | tf_op jit(solution)/shard_map/ppermute | solution.py:265

commit v4 on v2

--- a/solution.py
+++ b/solution.py
@@ -50,14 +50,15 @@
 def pack_body(y, slab, came, blk):
     flip = y[0] != 0
     for o in range(2):
-        mine = slab[2 * y[0] + o]
-        other = came[o]
-        a = jnp.where(flip, other, mine)
-        b = jnp.where(flip, mine, other)
-        for h in range(2):
-            r = o * 12 + h * 6
-            blk[r:r + 3, :] = a[:, h * HALF:(h + 1) * HALF]
-            blk[r + 3:r + 6, :] = b[:, h * HALF:(h + 1) * HALF]
+        for x in range(3):
+            mine = jnp.where(flip, slab[x, o + 2:o + 3, :], slab[x, o:o + 1, :])
+            other = came[x, o:o + 1, :]
+            a = jnp.where(flip, other, mine)
+            b = jnp.where(flip, mine, other)
+            for h in range(2):
+                r = o * 12 + h * 6 + x
+                blk[r:r + 1, :] = a[:, h * HALF:(h + 1) * HALF]
+                blk[r + 3:r + 4, :] = b[:, h * HALF:(h + 1) * HALF]
 
 
 def assemble_body(y, occupation, *refs):
@@ -86,18 +87,25 @@
                 outs[k][r:r + 6, :] = a[o, rows, lanes] + b[o, rows, lanes] + back[o][rows, lanes]
 
 
+def merge_body(core, up2, down2, far, to_up2, to_down2):
+    moved = far[...]
+    to_up2[...] = up2[...] + jnp.where(core[0] == 0, moved, 0.0)
+    to_down2[...] = down2[...] + jnp.where(core[0] == 0, 0.0, moved)
+
+
 def unpack_body(y, *refs):
-    keep, give = refs[8:]
+    keep, give = refs[7:]
     flip = y[0] != 0
     for o in range(2):
         for h in range(2):
             r = o * 12 + h * 6
             total = refs[0][r:r + 6, :]
-            for k in range(1, 8):
+            for k in range(1, 7):
                 total = total + refs[k][r:r + 6, :]
-            a, b = total[:3], total[3:]
-            keep[o, :, h * HALF:(h + 1) * HALF] = jnp.where(flip, b, a)
-            give[o, :, h * HALF:(h + 1) * HALF] = jnp.where(flip, a, b)
+            for x in range(3):
+                a, b = total[x:x + 1], total[x + 3:x + 4]
+                keep[x, o:o + 1, h * HALF:(h + 1) * HALF] = jnp.where(flip, b, a)
+                give[x, o:o + 1, h * HALF:(h + 1) * HALF] = jnp.where(flip, a, b)
 
 
 def kernel(first, idx, own, twin, vis, ktab, fx, ix, fz, iz, *refs):
@@ -125,11 +133,11 @@
         spec[:, pl.ds(pl.multiple_of(yb * YB, YB), YB), :] = jnp.swapaxes(zed[...], 0, 1)
 
     def enter(k, _):
-        for u in range(3):
-            enter_one(k * 3 + u, *bufs[u % 2 * 3:u % 2 * 3 + 3])
+        for u in range(6):
+            enter_one(k * 6 + u, *bufs[u % 2 * 3:u % 2 * 3 + 3])
         return 0
 
-    lax.fori_loop(0, G // YB // 3, enter, 0)
+    lax.fori_loop(0, G // YB // 6, enter, 0)
 
     def half_in(kz):
         return apply(fz[...], spec[kz]) * ktab[kz]
@@ -186,11 +194,11 @@
             away[gi & 1, :, lanes] = away[gi & 1, :, lanes] + p * wt
 
     def leave(k, _):
-        for u in range(3):
-            leave_one(k * 3 + u, *bufs[u % 2 * 3:u % 2 * 3 + 3])
+        for u in range(6):
+            leave_one(k * 6 + u, *bufs[u % 2 * 3:u % 2 * 3 + 3])
         return 0
 
-    lax.fori_loop(0, G // YB // 3, leave, 0)
+    lax.fori_loop(0, G // YB // 6, leave, 0)
 
 
 def pair_solver(first, *args):
@@ -296,18 +304,32 @@
     return lax.ppermute(back, ("band", "grid"), [(d, s) for s, d in visit_route(v, False)])
 
 
-def gather_blocks(b0):
+def by_core(hop):
+    return [
+        (b * 16 + along(-hop if b % 2 else hop)(g), b * 16 + g) for b in range(16) for g in range(16)
+    ]
+
+
+def gather_blocks(b0, core):
     got = {0: b0}
     for k, source, hop in (
         (2, 0, 2), (6, 0, 6), (1, 0, 1), (7, 0, 7),
-        (3, 2, 1), (5, 6, 7), (4, 2, 2),
+        (3, 2, 1), (5, 6, 7),
     ):
         got[k] = ring(got[source], "grid", along(hop))
+    got[4] = lax.ppermute(jnp.where(core == 0, got[2], got[6]), ("band", "grid"), by_core(2))
     return [got[k] for k in range(8)]
 
 
-def scatter_blocks(part):
-    return [part[0]] + [ring(part[k], "grid", along(-k)) for k in (4, 3, 5, 2, 6, 1, 7)]
+def scatter_blocks(core, own, up1, up2, up3, far, down3, down2, down1):
+    far = lax.ppermute(far, ("band", "grid"), by_core(-2))
+    came = [own]
+    for block, hop in ((up3, -3), (down3, 3), (up1, -1), (down1, 1)):
+        came.append(ring(block, "grid", along(hop)))
+    up2, down2 = small_call(
+        merge_body, [f32(24, HALF)] * 2, core.reshape(1), up2, down2, far, scalars=1
+    )
+    return came + [ring(up2, "grid", along(-2)), ring(down2, "grid", along(2))]
 
 
 def on_device(orbitals, occupation, cutoff):
@@ -316,11 +338,12 @@
     core = lax.axis_index("band") % 2
     z, y = g % 8, g // 8
     y1 = y.reshape(1)
-    give = lax.dynamic_slice(orbitals, (2 * (1 - y), 0, 0), (2, 3, ROW))
+    slab = orbitals.transpose(1, 0, 2)
+    give = jnp.where(y == 0, slab[:, 2:], slab[:, :2])
     came = ring(give, "grid", partner)
-    blk = small_call(pack_body, [f32(24, HALF)], y1, orbitals, came, scalars=1)
-
-    got = gather_blocks(blk)
+    blk = small_call(pack_body, [f32(24, HALF)], y1, slab, came, scalars=1)
+
+    got = gather_blocks(blk, core)
     e = z * 2 + core
     once = [z == ORDER[v].index(7) for v in range(2)]
     idx = jnp.stack([e // 4 ^ 2 * core, e % 4 ^ 2 * core] + [o.astype(jnp.int32) for o in once])
@@ -343,9 +366,10 @@
     ret1 = returned(back, 1)
     swapped = ring(away, "band", twin_of)
     part = small_call(disperse_body, [f32(24, HALF)] * 8, home, swapped, ret0, ret1)
-    keep, give = small_call(unpack_body, [f32(2, 3, ROW)] * 2, y1, *scatter_blocks(part), scalars=1)
+    keep, give = small_call(unpack_body, [f32(3, 2, ROW)] * 2, y1, *scatter_blocks(core, *part), scalars=1)
     came = ring(give, "grid", partner)
-    return jnp.concatenate([jnp.where(y == 0, keep, came), jnp.where(y == 0, came, keep)], axis=0)
+    out = jnp.concatenate([jnp.where(y == 0, keep, came), jnp.where(y == 0, came, keep)], axis=1)
+    return out.transpose(1, 0, 2)
 
 
 def solution(mesh):

time: 119 us -> 118 us (level)
  starting transfers between devices: 48.2 us -> 53.9 us
  waiting for transfers between devices: 47.6 us -> 42.6 us
  other arithmetic: 2.15 us -> 3.9 us
  local copies, waits for them, and re-layouts: 1.66 us -> 0.02 us
  Pallas kernels: 18.1 us -> 16.9 us
    ppermute x0 -> x2, starting transfers between devices: none -> 11.6 us  [the longest x1 9.38 us: scatter_blocks(): far = lax.ppermute(far, ('band', 'grid'), by_core(-2))]
    ppermute x18 -> x16, starting transfers between devices: 34.1 us -> 28.7 us  [ring(): lax.ppermute(block, axis, [(source(i), i) for i in range(lax.axis_size(ax...]
    ppermute x18 -> x16, waiting for transfers between devices: 21.8 us -> 17.7 us  [ring(): lax.ppermute(block, axis, [(source(i), i) for i in range(lax.axis_size(ax...]
    pallas_call x2, Pallas kernels: 16.7 us -> 15.4 us  [pair_solver(): pl.pallas_call(functools.partial(kernel, first), out_shape=[f32(2, G, ROW...]
  transfers between devices with their start and end apart: 22 -> 22, of which waited for: 12 -> 11; matrix products, arithmetic and copies ran while one was open for 2% -> 2% of each run, Pallas kernels for 7% -> 7%
where the time goes in v4:
time: 118 us
  starting transfers between devices  53.9 us (46%)
  waiting for transfers between devices  42.6 us (36%)
  Pallas kernels  16.9 us (14%)
  other arithmetic  3.9 us (3%)
    ppermute x16, starting transfers between devices, ring(): lax.ppermute(block, axis, [(source(i), i) for i in range(lax.axis_size(ax...  28.7 us
    ppermute x16, waiting for transfers between devices, ring(): lax.ppermute(block, axis, [(source(i), i) for i in range(lax.axis_size(ax...  17.7 us
    pallas_call x2, Pallas kernels, pair_solver(): pl.pallas_call(functools.partial(kernel, first), out_shape=[f32(2, G, ROW...  15.4 us
    ppermute x2, waiting for transfers between devices, returned(): lax.ppermute(back, ('band', 'grid'), [(d, s) for s, d in visit_route(v, F...  14.4 us
    ppermute x1, waiting for transfers between devices, on_device(): vis0 = lax.ppermute(lone[0], axes, visit_route(0))  10.5 us
    ppermute x1, starting transfers between devices, scatter_blocks(): far = lax.ppermute(far, ('band', 'grid'), by_core(-2))  9.38 us
    ppermute x2, starting transfers between devices, returned(): lax.ppermute(back, ('band', 'grid'), [(d, s) for s, d in visit_route(v, F...  6.21 us
    ppermute x1, starting transfers between devices, on_device(): vis0 = lax.ppermute(lone[0], axes, visit_route(0))  4.11 us
  transfers between devices with their start and end apart: 22, of which 11 were waited for; matrix products, arithmetic and copies ran while one was open for 2% of the time, Pallas kernels for 7%

profile of v4, /device:TPU:8, one launch (start us, length us, event | category | flops | bytes accessed | tf_op | source)
XLA Modules:
  0.0 118.2 jit_solution(2040468928565080137)
XLA Ops:
  0.0 1.1 slice_select_fusion
  1.1 2.4 %collective-permute-start = (f32[3,2,2304]{2,1,0:T(2,128)S(1)}, f32[3,2,2304]{2,1,0:T(2,128)S(1)}, u32[]{:S(2)}, u32[]{:S(2)}) collective-permute-start(f32[3,2,2304]{2,1,0:T(2,128)S(1)} %slice_select_fusion), channel_id=1, source_target_pairs={{8,0},{9,1},{10,2},{11,3},{12,4},{13,5},{14,6},{15,7},{0,8},{1,9},... | collective-permute-start | bytes 165896 | tf_op jit(solution)/shard_map/ppermute | solution.py:257
  4.4 1.4 %fusion.9.ktab = f32[48,48,256]{2,1,0:T(8,128)S(1)} fusion(f32[256]{0:T(256)S(1)} %or_select_fusion, f32[48,48]{1,0:T(8,128)S(1)} %broadcast_multiply_fusion, s32[]{:T(128)S(6)} %copy.5, s32[256]{0:T(256)S(1)} %fusion.26, s32[48,48]{1,0:T(8,128)S(1)} %broadcast_add_fusion), kind=kLoop, calls=%fused_computation.12 | loop fusion | flops 8847360 | bytes 2379780 | tf_op jit(solution)/shard_map/jit(_where)/select_n | solution.py:253
  6.9 3.3 %collective-permute-start.4 = (f32[24,1152]{1,0:T(8,128)S(1)}, f32[24,1152]{1,0:T(8,128)S(1)}, u32[]{:S(2)}, u32[]{:S(2)}) collective-permute-start(f32[24,1152]{1,0:T(8,128)S(1)} %shard_map.46.refs_0_), channel_id=1, source_target_pairs={{6,0},{7,1},{0,2},{1,3},{2,4},{3,5},{4,6},{5,7},{14,8},{15,9},{8,1... | collective-permute-start | bytes 331784 | tf_op jit(solution)/shard_map/ppermute | solution.py:257
  10.2 3.1 %collective-permute-start.2 = (f32[24,1152]{1,0:T(8,128)S(1)}, f32[24,1152]{1,0:T(8,128)S(1)}, u32[]{:S(2)}, u32[]{:S(2)}) collective-permute-start(f32[24,1152]{1,0:T(8,128)S(1)} %shard_map.46.refs_0_), channel_id=1, source_target_pairs={{2,0},{3,1},{4,2},{5,3},{6,4},{7,5},{0,6},{1,7},{10,8},{11,9},{12,... | collective-permute-start | bytes 331784 | tf_op jit(solution)/shard_map/ppermute | solution.py:257
  13.4 1.1 collective-permute-start.7
  14.5 2.2 %collective-permute-start.1 = (f32[24,1152]{1,0:T(8,128)S(1)}, f32[24,1152]{1,0:T(8,128)S(1)}, u32[]{:S(2)}, u32[]{:S(2)}) collective-permute-start(f32[24,1152]{1,0:T(8,128)S(1)} %shard_map.46.refs_0_), channel_id=1, source_target_pairs={{1,0},{2,1},{3,2},{4,3},{5,4},{6,5},{7,6},{0,7},{9,8},{10,9},{11,1... | collective-permute-start | bytes 331784 | tf_op jit(solution)/shard_map/ppermute | solution.py:257
  16.7 0.7 collective-permute-done.4.refs_6_
  17.5 2.3 %collective-permute-done.2.refs_2_ = f32[24,1152]{1,0:T(8,128)S(1)} collective-permute-done((f32[24,1152]{1,0:T(8,128)S(1)}, f32[24,1152]{1,0:T(8,128)S(1)}, u32[]{:S(2)}, u32[]{:S(2)}) %collective-permute-start.2) | collective-permute-done | bytes 110624 | tf_op jit(solution)/shard_map/ppermute | solution.py:257
  19.8 2.2 %collective-permute-start.5 = (f32[24,1152]{1,0:T(8,128)S(1)}, f32[24,1152]{1,0:T(8,128)S(1)}, u32[]{:S(2)}, u32[]{:S(2)}) collective-permute-start(f32[24,1152]{1,0:T(8,128)S(1)} %broadcast_select_fusion), channel_id=1, source_target_pairs={{2,0},{3,1},{4,2},{5,3},{6,4},{7,5},{0,6},{1,7},{10,8},{11,9},{12,... | collective-permute-start | bytes 331784 | tf_op jit(solution)/shard_map/ppermute | solution.py:320
  22.0 1.9 %collective-permute-start.6 = (f32[24,1152]{1,0:T(8,128)S(1)}, f32[24,1152]{1,0:T(8,128)S(1)}, u32[]{:S(2)}, u32[]{:S(2)}) collective-permute-start(f32[24,1152]{1,0:T(8,128)S(1)} %collective-permute-done.4.refs_6_), channel_id=1, source_target_pairs={{7,0},{0,1},{1,2},{2,3},{3,4},{4,5},{5,6},{6,7},{15,8},{8,9},{9,10... | collective-permute-start | bytes 331784 | tf_op jit(solution)/shard_map/ppermute | solution.py:257
  23.9 1.3 %collective-permute-start.3 = (f32[24,1152]{1,0:T(8,128)S(1)}, f32[24,1152]{1,0:T(8,128)S(1)}, u32[]{:S(2)}, u32[]{:S(2)}) collective-permute-start(f32[24,1152]{1,0:T(8,128)S(1)} %collective-permute-done.2.refs_2_), channel_id=1, source_target_pairs={{1,0},{2,1},{3,2},{4,3},{5,4},{6,5},{7,6},{0,7},{9,8},{10,9},{11,1... | collective-permute-start | bytes 331784 | tf_op jit(solution)/shard_map/ppermute | solution.py:257
  25.3 2.6 %collective-permute-done.6.refs_5_ = f32[24,1152]{1,0:T(8,128)S(1)} collective-permute-done((f32[24,1152]{1,0:T(8,128)S(1)}, f32[24,1152]{1,0:T(8,128)S(1)}, u32[]{:S(2)}, u32[]{:S(2)}) %collective-permute-start.6) | collective-permute-done | bytes 110624 | tf_op jit(solution)/shard_map/ppermute | solution.py:257
  28.7 0.8 shard_map.47
  29.6 4.1 %collective-permute-start.9 = (f32[48,2432]{1,0:T(8,128)S(1)}, f32[48,2432]{1,0:T(8,128)S(1)}, u32[]{:S(2)}, u32[]{:S(2)}) collective-permute-start(f32[48,2432]{1,0:T(8,128)S(1)} %get-tuple-element.53), channel_id=1, source_target_pairs={{160,0},{193,1},{10,2},{67,3},{36,4},{133,5},{174,6},{111,7},{168,... | collective-permute-start | bytes 1400840 | tf_op jit(solution)/shard_map/ppermute | solution.py:358
  33.7 10.5 %collective-permute-done.9.vis = f32[48,2432]{1,0:T(8,128)S(1)} collective-permute-done((f32[48,2432]{1,0:T(8,128)S(1)}, f32[48,2432]{1,0:T(8,128)S(1)}, u32[]{:S(2)}, u32[]{:S(2)}) %collective-permute-start.9) | collective-permute-done | bytes 466976 | tf_op jit(solution)/shard_map/ppermute | solution.py:358
  44.2 3.3 %collective-permute-start.10 = (f32[48,2432]{1,0:T(8,128)S(1)}, f32[48,2432]{1,0:T(8,128)S(1)}, u32[]{:S(2)}, u32[]{:S(2)}) collective-permute-start(f32[48,2432]{1,0:T(8,128)S(1)} %get-tuple-element.54), channel_id=1, source_target_pairs={{32,0},{129,1},{170,2},{107,3},{164,4},{197,5},{14,6},{71,7},{40,8... | collective-permute-start | bytes 1400840 | tf_op jit(solution)/shard_map/ppermute | solution.py:361
  47.6 7.8 %shard_map.48 = (f32[2,48,2304]{2,1,0:T(8,128)S(1)}, f32[2,48,2304]{2,1,0:T(8,128)S(1)}, f32[48,2304]{1,0:T(8,128)S(1)}) custom-call(s32[4]{0:T(128)S(1)} %pad_add_fusion.idx, f32[2,48,2432]{2,1,0:T(8,128)S(1)} %get-tuple-element.51.own, f32[2,48,2432]{2,1,0:T(8,128)S(1)} %collective-permute-done.8.twin, f32[48,2432]{1,0:T(8,128)S(1)} %collective-permute-done.9.vis, ...), custom_call_target="tpu_custom_call" | custom-call | flops 5000000000 | bytes 10000000 | tf_op jit(solution)/shard_map/pallas_call | solution.py:205
  55.4 7.6 %shard_map.49 = (f32[2,48,2304]{2,1,0:T(8,128)S(1)}, f32[2,48,2304]{2,1,0:T(8,128)S(1)}, f32[48,2304]{1,0:T(8,128)S(1)}) custom-call(s32[4]{0:T(128)S(1)} %pad_add_fusion.idx, f32[2,48,2432]{2,1,0:T(8,128)S(1)} %get-tuple-element.51.own, f32[2,48,2432]{2,1,0:T(8,128)S(1)} %collective-permute-done.8.twin, f32[48,2432]{1,0:T(8,128)S(1)} %collective-permute-done.10.vis, ...), custom_call_target="tpu_custom_call" | custom-call | flops 5000000000 | bytes 10000000 | tf_op jit(solution)/shard_map/pallas_call | solution.py:205
  63.6 2.8 %collective-permute-start.13 = (f32[48,2304]{1,0:T(8,128)S(1)}, f32[48,2304]{1,0:T(8,128)S(1)}, u32[]{:S(2)}, u32[]{:S(2)}) collective-permute-start(f32[48,2304]{1,0:T(8,128)S(1)} %get-tuple-element.66), channel_id=1, source_target_pairs={{0,32},{1,129},{2,170},{3,107},{4,164},{5,197},{6,14},{8,40},{9,13... | collective-permute-start | bytes 1327112 | tf_op jit(solution)/shard_map/ppermute | solution.py:304
  66.4 3.4 %collective-permute-start.12 = (f32[48,2304]{1,0:T(8,128)S(1)}, f32[48,2304]{1,0:T(8,128)S(1)}, u32[]{:S(2)}, u32[]{:S(2)}) collective-permute-start(f32[48,2304]{1,0:T(8,128)S(1)} %get-tuple-element.65), channel_id=1, source_target_pairs={{0,160},{1,193},{2,10},{4,36},{5,133},{6,174},{7,111},{8,168},{9,2... | collective-permute-start | bytes 1327112 | tf_op jit(solution)/shard_map/ppermute | solution.py:304
  69.8 5.2 %collective-permute-done.13.c1 = f32[48,2304]{1,0:T(8,128)S(1)} collective-permute-done((f32[48,2304]{1,0:T(8,128)S(1)}, f32[48,2304]{1,0:T(8,128)S(1)}, u32[]{:S(2)}, u32[]{:S(2)}) %collective-permute-start.13) | collective-permute-done | bytes 442400 | tf_op jit(solution)/shard_map/ppermute | solution.py:304
  75.0 9.2 %collective-permute-done.12.c0 = f32[48,2304]{1,0:T(8,128)S(1)} collective-permute-done((f32[48,2304]{1,0:T(8,128)S(1)}, f32[48,2304]{1,0:T(8,128)S(1)}, u32[]{:S(2)}, u32[]{:S(2)}) %collective-permute-start.12) | collective-permute-done | bytes 442400 | tf_op jit(solution)/shard_map/ppermute | solution.py:304
  84.7 9.4 %collective-permute-start.18 = (f32[24,1152]{1,0:T(8,128)S(1)}, f32[24,1152]{1,0:T(8,128)S(1)}, u32[]{:S(2)}, u32[]{:S(2)}) collective-permute-start(f32[24,1152]{1,0:T(8,128)S(1)} %get-tuple-element.74), channel_id=1, source_target_pairs={{6,0},{7,1},{0,2},{1,3},{2,4},{3,5},{4,6},{5,7},{14,8},{15,9},{8,1... | collective-permute-start | bytes 331784 | tf_op jit(solution)/shard_map/ppermute | solution.py:325
  94.1 5.0 %collective-permute-start.15 = (f32[24,1152]{1,0:T(8,128)S(1)}, f32[24,1152]{1,0:T(8,128)S(1)}, u32[]{:S(2)}, u32[]{:S(2)}) collective-permute-start(f32[24,1152]{1,0:T(8,128)S(1)} %get-tuple-element.69), channel_id=1, source_target_pairs={{3,0},{4,1},{5,2},{6,3},{7,4},{0,5},{1,6},{2,7},{11,8},{12,9},{13,... | collective-permute-start | bytes 331784 | tf_op jit(solution)/shard_map/ppermute | solution.py:257
  99.1 3.2 %collective-permute-start.17 = (f32[24,1152]{1,0:T(8,128)S(1)}, f32[24,1152]{1,0:T(8,128)S(1)}, u32[]{:S(2)}, u32[]{:S(2)}) collective-permute-start(f32[24,1152]{1,0:T(8,128)S(1)} %get-tuple-element.71), channel_id=1, source_target_pairs={{1,0},{2,1},{3,2},{4,3},{5,4},{6,5},{7,6},{0,7},{9,8},{10,9},{11,1... | collective-permute-start | bytes 331784 | tf_op jit(solution)/shard_map/ppermute | solution.py:257
  102.4 2.7 %collective-permute-start.19 = (f32[24,1152]{1,0:T(8,128)S(1)}, f32[24,1152]{1,0:T(8,128)S(1)}, u32[]{:S(2)}, u32[]{:S(2)}) collective-permute-start(f32[24,1152]{1,0:T(8,128)S(1)} %get-tuple-element.75), channel_id=1, source_target_pairs={{6,0},{7,1},{0,2},{1,3},{2,4},{3,5},{4,6},{5,7},{14,8},{15,9},{8,1... | collective-permute-start | bytes 331784 | tf_op jit(solution)/shard_map/ppermute | solution.py:257
  105.1 1.5 %collective-permute-start.20 = (f32[24,1152]{1,0:T(8,128)S(1)}, f32[24,1152]{1,0:T(8,128)S(1)}, u32[]{:S(2)}, u32[]{:S(2)}) collective-permute-start(f32[24,1152]{1,0:T(8,128)S(1)} %get-tuple-element.76), channel_id=1, source_target_pairs={{2,0},{3,1},{4,2},{5,3},{6,4},{7,5},{0,6},{1,7},{10,8},{11,9},{12,... | collective-permute-start | bytes 331784 | tf_op jit(solution)/shard_map/ppermute | solution.py:257
  106.6 2.7 %collective-permute-done.19.refs_5_ = f32[24,1152]{1,0:T(8,128)S(1)} collective-permute-done((f32[24,1152]{1,0:T(8,128)S(1)}, f32[24,1152]{1,0:T(8,128)S(1)}, u32[]{:S(2)}, u32[]{:S(2)}) %collective-permute-start.19) | collective-permute-done | bytes 110624 | tf_op jit(solution)/shard_map/ppermute | solution.py:257
  109.3 2.3 %collective-permute-done.20.refs_6_ = f32[24,1152]{1,0:T(8,128)S(1)} collective-permute-done((f32[24,1152]{1,0:T(8,128)S(1)}, f32[24,1152]{1,0:T(8,128)S(1)}, u32[]{:S(2)}, u32[]{:S(2)}) %collective-permute-start.20) | collective-permute-done | bytes 110624 | tf_op jit(solution)/shard_map/ppermute | solution.py:257
  111.8 5.6 %collective-permute-done.21 = f32[3,2,2304]{2,1,0:T(2,128)S(1)} collective-permute-done((f32[3,2,2304]{2,1,0:T(2,128)S(1)}, f32[3,2,2304]{2,1,0:T(2,128)S(1)}, u32[]{:S(2)}, u32[]{:S(2)}) %collective-permute-start.21) | collective-permute-done | bytes 55328 | tf_op jit(solution)/shard_map/ppermute | solution.py:257
  117.5 0.7 maximum_bitcast_fusion
  (44 shorter events, 3.6 us)
Async XLA Ops:
  0.0 47.5 %copy-start.2 = (bf16[96,96]{1,0:T(8,128)(2,1)S(1)}, bf16[96,96]{1,0:T(8,128)(2,1)}, u32[]{:S(2)}) copy-start(bf16[96,96]{1,0:T(8,128)(2,1)} %constant.185.iz) | copy-start | bytes 55300
  0.0 47.5 %copy-start.3 = (bf16[96,96]{1,0:T(8,128)(2,1)S(1)}, bf16[96,96]{1,0:T(8,128)(2,1)}, u32[]{:S(2)}) copy-start(bf16[96,96]{1,0:T(8,128)(2,1)} %constant.177.fz) | copy-start | bytes 55300
  0.0 6.8 %copy-start = (f32[4,3,2304]{2,0,1:T(4,128)S(1)}, f32[4,3,2304]{2,0,1:T(4,128)}, u32[]{:S(2)}) copy-start(f32[4,3,2304]{2,0,1:T(4,128)} %param.4) | copy-start | bytes 331780
  0.0 28.7 %copy-start.1 = (s32[4]{0:T(128)S(1)}, s32[4]{0:T(128)}, u32[]{:S(2)}) copy-start(s32[4]{0:T(128)} %occupation.1) | copy-start | bytes 52
  1.1 5.7 %collective-permute-start = (f32[3,2,2304]{2,1,0:T(2,128)S(1)}, f32[3,2,2304]{2,1,0:T(2,128)S(1)}, u32[]{:S(2)}, u32[]{:S(2)}) collective-permute-start(f32[3,2,2304]{2,1,0:T(2,128)S(1)} %slice_select_fusion), channel_id=1, source_target_pairs={{8,0},{9,1},{10,2},{11,3},{12,4},{13,5},{14,6},{15,7},{0,8},{1,9},... | collective-permute-start | bytes 165896 | tf_op jit(solution)/shard_map/ppermute | solution.py:257
  6.9 10.6 %collective-permute-start.4 = (f32[24,1152]{1,0:T(8,128)S(1)}, f32[24,1152]{1,0:T(8,128)S(1)}, u32[]{:S(2)}, u32[]{:S(2)}) collective-permute-start(f32[24,1152]{1,0:T(8,128)S(1)} %shard_map.46.refs_0_), channel_id=1, source_target_pairs={{6,0},{7,1},{0,2},{1,3},{2,4},{3,5},{4,6},{5,7},{14,8},{15,9},{8,1... | collective-permute-start | bytes 331784 | tf_op jit(solution)/shard_map/ppermute | solution.py:257
  10.2 9.6 %collective-permute-start.2 = (f32[24,1152]{1,0:T(8,128)S(1)}, f32[24,1152]{1,0:T(8,128)S(1)}, u32[]{:S(2)}, u32[]{:S(2)}) collective-permute-start(f32[24,1152]{1,0:T(8,128)S(1)} %shard_map.46.refs_0_), channel_id=1, source_target_pairs={{2,0},{3,1},{4,2},{5,3},{6,4},{7,5},{0,6},{1,7},{10,8},{11,9},{12,... | collective-permute-start | bytes 331784 | tf_op jit(solution)/shard_map/ppermute | solution.py:257
  13.4 11.9 %collective-permute-start.7 = (f32[24,1152]{1,0:T(8,128)S(1)}, f32[24,1152]{1,0:T(8,128)S(1)}, u32[]{:S(2)}, u32[]{:S(2)}) collective-permute-start(f32[24,1152]{1,0:T(8,128)S(1)} %shard_map.46.refs_0_), channel_id=1, source_target_pairs={{7,0},{0,1},{1,2},{2,3},{3,4},{4,5},{5,6},{6,7},{15,8},{8,9},{9,10... | collective-permute-start | bytes 331784 | tf_op jit(solution)/shard_map/ppermute | solution.py:257
  14.5 10.8 %collective-permute-start.1 = (f32[24,1152]{1,0:T(8,128)S(1)}, f32[24,1152]{1,0:T(8,128)S(1)}, u32[]{:S(2)}, u32[]{:S(2)}) collective-permute-start(f32[24,1152]{1,0:T(8,128)S(1)} %shard_map.46.refs_0_), channel_id=1, source_target_pairs={{1,0},{2,1},{3,2},{4,3},{5,4},{6,5},{7,6},{0,7},{9,8},{10,9},{11,1... | collective-permute-start | bytes 331784 | tf_op jit(solution)/shard_map/ppermute | solution.py:257
  19.8 8.2 %collective-permute-start.5 = (f32[24,1152]{1,0:T(8,128)S(1)}, f32[24,1152]{1,0:T(8,128)S(1)}, u32[]{:S(2)}, u32[]{:S(2)}) collective-permute-start(f32[24,1152]{1,0:T(8,128)S(1)} %broadcast_select_fusion), channel_id=1, source_target_pairs={{2,0},{3,1},{4,2},{5,3},{6,4},{7,5},{0,6},{1,7},{10,8},{11,9},{12,... | collective-permute-start | bytes 331784 | tf_op jit(solution)/shard_map/ppermute | solution.py:320
  22.0 6.0 %collective-permute-start.6 = (f32[24,1152]{1,0:T(8,128)S(1)}, f32[24,1152]{1,0:T(8,128)S(1)}, u32[]{:S(2)}, u32[]{:S(2)}) collective-permute-start(f32[24,1152]{1,0:T(8,128)S(1)} %collective-permute-done.4.refs_6_), channel_id=1, source_target_pairs={{7,0},{0,1},{1,2},{2,3},{3,4},{4,5},{5,6},{6,7},{15,8},{8,9},{9,10... | collective-permute-start | bytes 331784 | tf_op jit(solution)/shard_map/ppermute | solution.py:257
  23.9 4.7 %collective-permute-start.3 = (f32[24,1152]{1,0:T(8,128)S(1)}, f32[24,1152]{1,0:T(8,128)S(1)}, u32[]{:S(2)}, u32[]{:S(2)}) collective-permute-start(f32[24,1152]{1,0:T(8,128)S(1)} %collective-permute-done.2.refs_2_), channel_id=1, source_target_pairs={{1,0},{2,1},{3,2},{4,3},{5,4},{6,5},{7,6},{0,7},{9,8},{10,9},{11,1... | collective-permute-start | bytes 331784 | tf_op jit(solution)/shard_map/ppermute | solution.py:257
  29.5 18.1 %collective-permute-start.8 = (f32[2,48,2432]{2,1,0:T(8,128)S(1)}, f32[2,48,2432]{2,1,0:T(8,128)S(1)}, u32[]{:S(2)}, u32[]{:S(2)}) collective-permute-start(f32[2,48,2432]{2,1,0:T(8,128)S(1)} %get-tuple-element.51.own), channel_id=1, source_target_pairs={{16,0},{0,16},{48,32},{32,48},{80,64},{64,80},{112,96},{96,112},{1... | collective-permute-start | bytes 2801672 | tf_op jit(solution)/shard_map/ppermute | solution.py:257
  29.6 14.7 %collective-permute-start.9 = (f32[48,2432]{1,0:T(8,128)S(1)}, f32[48,2432]{1,0:T(8,128)S(1)}, u32[]{:S(2)}, u32[]{:S(2)}) collective-permute-start(f32[48,2432]{1,0:T(8,128)S(1)} %get-tuple-element.53), channel_id=1, source_target_pairs={{160,0},{193,1},{10,2},{67,3},{36,4},{133,5},{174,6},{111,7},{168,... | collective-permute-start | bytes 1400840 | tf_op jit(solution)/shard_map/ppermute | solution.py:358
  44.2 11.1 %collective-permute-start.10 = (f32[48,2432]{1,0:T(8,128)S(1)}, f32[48,2432]{1,0:T(8,128)S(1)}, u32[]{:S(2)}, u32[]{:S(2)}) collective-permute-start(f32[48,2432]{1,0:T(8,128)S(1)} %get-tuple-element.54), channel_id=1, source_target_pairs={{32,0},{129,1},{170,2},{107,3},{164,4},{197,5},{14,6},{71,7},{40,8... | collective-permute-start | bytes 1400840 | tf_op jit(solution)/shard_map/ppermute | solution.py:361
  63.0 21.2 %collective-permute-start.11 = (f32[2,48,2304]{2,1,0:T(8,128)S(1)}, f32[2,48,2304]{2,1,0:T(8,128)S(1)}, u32[]{:S(2)}, u32[]{:S(2)}) collective-permute-start(f32[2,48,2304]{2,1,0:T(8,128)S(1)} %get-tuple-element.64), channel_id=1, source_target_pairs={{16,0},{0,16},{48,32},{32,48},{80,64},{64,80},{112,96},{96,112},{1... | collective-permute-start | bytes 2654216 | tf_op jit(solution)/shard_map/ppermute | solution.py:257
  63.6 11.4 %collective-permute-start.13 = (f32[48,2304]{1,0:T(8,128)S(1)}, f32[48,2304]{1,0:T(8,128)S(1)}, u32[]{:S(2)}, u32[]{:S(2)}) collective-permute-start(f32[48,2304]{1,0:T(8,128)S(1)} %get-tuple-element.66), channel_id=1, source_target_pairs={{0,32},{1,129},{2,170},{3,107},{4,164},{5,197},{6,14},{8,40},{9,13... | collective-permute-start | bytes 1327112 | tf_op jit(solution)/shard_map/ppermute | solution.py:304
  66.4 17.8 %collective-permute-start.12 = (f32[48,2304]{1,0:T(8,128)S(1)}, f32[48,2304]{1,0:T(8,128)S(1)}, u32[]{:S(2)}, u32[]{:S(2)}) collective-permute-start(f32[48,2304]{1,0:T(8,128)S(1)} %get-tuple-element.65), channel_id=1, source_target_pairs={{0,160},{1,193},{2,10},{4,36},{5,133},{6,174},{7,111},{8,168},{9,2... | collective-permute-start | bytes 1327112 | tf_op jit(solution)/shard_map/ppermute | solution.py:304
  84.7 17.7 %collective-permute-start.18 = (f32[24,1152]{1,0:T(8,128)S(1)}, f32[24,1152]{1,0:T(8,128)S(1)}, u32[]{:S(2)}, u32[]{:S(2)}) collective-permute-start(f32[24,1152]{1,0:T(8,128)S(1)} %get-tuple-element.74), channel_id=1, source_target_pairs={{6,0},{7,1},{0,2},{1,3},{2,4},{3,5},{4,6},{5,7},{14,8},{15,9},{8,1... | collective-permute-start | bytes 331784 | tf_op jit(solution)/shard_map/ppermute | solution.py:325
  94.1 11.0 %collective-permute-start.14 = (f32[24,1152]{1,0:T(8,128)S(1)}, f32[24,1152]{1,0:T(8,128)S(1)}, u32[]{:S(2)}, u32[]{:S(2)}) collective-permute-start(f32[24,1152]{1,0:T(8,128)S(1)} %get-tuple-element.68), channel_id=1, source_target_pairs={{5,0},{6,1},{7,2},{0,3},{1,4},{2,5},{3,6},{4,7},{13,8},{14,9},{15,... | collective-permute-start | bytes 331784 | tf_op jit(solution)/shard_map/ppermute | solution.py:257
  94.1 12.5 %collective-permute-start.15 = (f32[24,1152]{1,0:T(8,128)S(1)}, f32[24,1152]{1,0:T(8,128)S(1)}, u32[]{:S(2)}, u32[]{:S(2)}) collective-permute-start(f32[24,1152]{1,0:T(8,128)S(1)} %get-tuple-element.69), channel_id=1, source_target_pairs={{3,0},{4,1},{5,2},{6,3},{7,4},{0,5},{1,6},{2,7},{11,8},{12,9},{13,... | collective-permute-start | bytes 331784 | tf_op jit(solution)/shard_map/ppermute | solution.py:257
  99.1 7.5 %collective-permute-start.16 = (f32[24,1152]{1,0:T(8,128)S(1)}, f32[24,1152]{1,0:T(8,128)S(1)}, u32[]{:S(2)}, u32[]{:S(2)}) collective-permute-start(f32[24,1152]{1,0:T(8,128)S(1)} %get-tuple-element.70), channel_id=1, source_target_pairs={{7,0},{0,1},{1,2},{2,3},{3,4},{4,5},{5,6},{6,7},{15,8},{8,9},{9,10... | collective-permute-start | bytes 331784 | tf_op jit(solution)/shard_map/ppermute | solution.py:257
  99.1 7.5 %collective-permute-start.17 = (f32[24,1152]{1,0:T(8,128)S(1)}, f32[24,1152]{1,0:T(8,128)S(1)}, u32[]{:S(2)}, u32[]{:S(2)}) collective-permute-start(f32[24,1152]{1,0:T(8,128)S(1)} %get-tuple-element.71), channel_id=1, source_target_pairs={{1,0},{2,1},{3,2},{4,3},{5,4},{6,5},{7,6},{0,7},{9,8},{10,9},{11,1... | collective-permute-start | bytes 331784 | tf_op jit(solution)/shard_map/ppermute | solution.py:257
  102.4 6.9 %collective-permute-start.19 = (f32[24,1152]{1,0:T(8,128)S(1)}, f32[24,1152]{1,0:T(8,128)S(1)}, u32[]{:S(2)}, u32[]{:S(2)}) collective-permute-start(f32[24,1152]{1,0:T(8,128)S(1)} %get-tuple-element.75), channel_id=1, source_target_pairs={{6,0},{7,1},{0,2},{1,3},{2,4},{3,5},{4,6},{5,7},{14,8},{15,9},{8,1... | collective-permute-start | bytes 331784 | tf_op jit(solution)/shard_map/ppermute | solution.py:257
  105.1 6.5 %collective-permute-start.20 = (f32[24,1152]{1,0:T(8,128)S(1)}, f32[24,1152]{1,0:T(8,128)S(1)}, u32[]{:S(2)}, u32[]{:S(2)}) collective-permute-start(f32[24,1152]{1,0:T(8,128)S(1)} %get-tuple-element.76), channel_id=1, source_target_pairs={{2,0},{3,1},{4,2},{5,3},{6,4},{7,5},{0,6},{1,7},{10,8},{11,9},{12,... | collective-permute-start | bytes 331784 | tf_op jit(solution)/shard_map/ppermute | solution.py:257
  111.7 5.7 %collective-permute-start.21 = (f32[3,2,2304]{2,1,0:T(2,128)S(1)}, f32[3,2,2304]{2,1,0:T(2,128)S(1)}, u32[]{:S(2)}, u32[]{:S(2)}) collective-permute-start(f32[3,2,2304]{2,1,0:T(2,128)S(1)} %get-tuple-element.78), channel_id=1, source_target_pairs={{8,0},{9,1},{10,2},{11,3},{12,4},{13,5},{14,6},{15,7},{0,8},{1,9},... | collective-permute-start | bytes 165896 | tf_op jit(solution)/shard_map/ppermute | solution.py:257

commit v5 on v4

--- a/solution.py
+++ b/solution.py
@@ -87,20 +87,14 @@
                 outs[k][r:r + 6, :] = a[o, rows, lanes] + b[o, rows, lanes] + back[o][rows, lanes]
 
 
-def merge_body(core, up2, down2, far, to_up2, to_down2):
-    moved = far[...]
-    to_up2[...] = up2[...] + jnp.where(core[0] == 0, moved, 0.0)
-    to_down2[...] = down2[...] + jnp.where(core[0] == 0, 0.0, moved)
-
-
 def unpack_body(y, *refs):
-    keep, give = refs[7:]
+    keep, give = refs[8:]
     flip = y[0] != 0
     for o in range(2):
         for h in range(2):
             r = o * 12 + h * 6
             total = refs[0][r:r + 6, :]
-            for k in range(1, 7):
+            for k in range(1, 8):
                 total = total + refs[k][r:r + 6, :]
             for x in range(3):
                 a, b = total[x:x + 1], total[x + 3:x + 4]
@@ -304,32 +298,18 @@
     return lax.ppermute(back, ("band", "grid"), [(d, s) for s, d in visit_route(v, False)])
 
 
-def by_core(hop):
-    return [
-        (b * 16 + along(-hop if b % 2 else hop)(g), b * 16 + g) for b in range(16) for g in range(16)
-    ]
-
-
-def gather_blocks(b0, core):
+def gather_blocks(b0):
     got = {0: b0}
     for k, source, hop in (
         (2, 0, 2), (6, 0, 6), (1, 0, 1), (7, 0, 7),
-        (3, 2, 1), (5, 6, 7),
+        (3, 2, 1), (5, 6, 7), (4, 2, 2),
     ):
         got[k] = ring(got[source], "grid", along(hop))
-    got[4] = lax.ppermute(jnp.where(core == 0, got[2], got[6]), ("band", "grid"), by_core(2))
     return [got[k] for k in range(8)]
 
 
-def scatter_blocks(core, own, up1, up2, up3, far, down3, down2, down1):
-    far = lax.ppermute(far, ("band", "grid"), by_core(-2))
-    came = [own]
-    for block, hop in ((up3, -3), (down3, 3), (up1, -1), (down1, 1)):
-        came.append(ring(block, "grid", along(hop)))
-    up2, down2 = small_call(
-        merge_body, [f32(24, HALF)] * 2, core.reshape(1), up2, down2, far, scalars=1
-    )
-    return came + [ring(up2, "grid", along(-2)), ring(down2, "grid", along(2))]
+def scatter_blocks(part):
+    return [part[0]] + [ring(part[k], "grid", along(-k)) for k in (4, 3, 5, 2, 6, 1, 7)]
 
 
 def on_device(orbitals, occupation, cutoff):
@@ -343,7 +323,7 @@
     came = ring(give, "grid", partner)
     blk = small_call(pack_body, [f32(24, HALF)], y1, slab, came, scalars=1)
 
-    got = gather_blocks(blk, core)
+    got = gather_blocks(blk)
     e = z * 2 + core
     once = [z == ORDER[v].index(7) for v in range(2)]
     idx = jnp.stack([e // 4 ^ 2 * core, e % 4 ^ 2 * core] + [o.astype(jnp.int32) for o in once])
@@ -366,7 +346,7 @@
     ret1 = returned(back, 1)
     swapped = ring(away, "band", twin_of)
     part = small_call(disperse_body, [f32(24, HALF)] * 8, home, swapped, ret0, ret1)
-    keep, give = small_call(unpack_body, [f32(3, 2, ROW)] * 2, y1, *scatter_blocks(core, *part), scalars=1)
+    keep, give = small_call(unpack_body, [f32(3, 2, ROW)] * 2, y1, *scatter_blocks(part), scalars=1)
     came = ring(give, "grid", partner)
     out = jnp.concatenate([jnp.where(y == 0, keep, came), jnp.where(y == 0, came, keep)], axis=1)
     return out.transpose(1, 0, 2)

time: 118 us -> 120 us (1.017)
  the two profiles are of different devices: /device:TPU:8 before, /device:TPU:32 now
where the time goes in v5:
time: 120 us
  starting transfers between devices  53.6 us (45%)
  waiting for transfers between devices  44.4 us (37%)
  Pallas kernels  16.9 us (14%)
  other arithmetic  3.88 us (3%)
    ppermute x18, starting transfers between devices, ring(): lax.ppermute(block, axis, [(source(i), i) for i in range(lax.axis_size(ax...  40.2 us
    ppermute x18, waiting for transfers between devices, ring(): lax.ppermute(block, axis, [(source(i), i) for i in range(lax.axis_size(ax...  18.8 us
    pallas_call x2, Pallas kernels, pair_solver(): pl.pallas_call(functools.partial(kernel, first), out_shape=[f32(2, G, ROW...  15.4 us
    ppermute x2, waiting for transfers between devices, returned(): lax.ppermute(back, ('band', 'grid'), [(d, s) for s, d in visit_route(v, F...  14 us
    ppermute x1, waiting for transfers between devices, on_device(): vis0 = lax.ppermute(lone[0], axes, visit_route(0))  11.6 us
    ppermute x2, starting transfers between devices, returned(): lax.ppermute(back, ('band', 'grid'), [(d, s) for s, d in visit_route(v, F...  6.93 us
    ppermute x1, starting transfers between devices, on_device(): vis0 = lax.ppermute(lone[0], axes, visit_route(0))  3.9 us
    ppermute x1, starting transfers between devices, on_device(): vis1 = lax.ppermute(held, axes, visit_route(1))  2.58 us
  transfers between devices with their start and end apart: 22, of which 10 were waited for; matrix products, arithmetic and copies ran while one was open for 2% of the time, Pallas kernels for 7%

profile of v5, /device:TPU:32, one launch (start us, length us, event | category | flops | bytes accessed | tf_op | source)
XLA Modules:
  0.0 119.7 jit_solution(204014687142710211)
XLA Ops:
  0.0 1.1 slice_select_fusion
  1.1 3.3 %collective-permute-start = (f32[3,2,2304]{2,1,0:T(2,128)S(1)}, f32[3,2,2304]{2,1,0:T(2,128)S(1)}, u32[]{:S(2)}, u32[]{:S(2)}) collective-permute-start(f32[3,2,2304]{2,1,0:T(2,128)S(1)} %slice_select_fusion), channel_id=1, source_target_pairs={{8,0},{9,1},{10,2},{11,3},{12,4},{13,5},{14,6},{15,7},{0,8},{1,9},... | collective-permute-start | bytes 165896 | tf_op jit(solution)/shard_map/ppermute | solution.py:251
  5.3 1.4 %fusion.9.ktab = f32[48,48,256]{2,1,0:T(8,128)S(1)} fusion(f32[256]{0:T(256)S(1)} %or_select_fusion, f32[48,48]{1,0:T(8,128)S(1)} %broadcast_multiply_fusion, s32[]{:T(128)S(6)} %copy.5, s32[256]{0:T(256)S(1)} %fusion.26, s32[48,48]{1,0:T(8,128)S(1)} %broadcast_add_fusion), kind=kLoop, calls=%fused_computation.12 | loop fusion | flops 8847360 | bytes 2379780 | tf_op jit(solution)/shard_map/jit(_where)/select_n | solution.py:247
  7.1 3.3 %collective-permute-start.5 = (f32[24,1152]{1,0:T(8,128)S(1)}, f32[24,1152]{1,0:T(8,128)S(1)}, u32[]{:S(2)}, u32[]{:S(2)}) collective-permute-start(f32[24,1152]{1,0:T(8,128)S(1)} %shard_map.46.refs_0_), channel_id=1, source_target_pairs={{6,0},{7,1},{0,2},{1,3},{2,4},{3,5},{4,6},{5,7},{14,8},{15,9},{8,1... | collective-permute-start | bytes 331784 | tf_op jit(solution)/shard_map/ppermute | solution.py:251
  10.5 2.2 %collective-permute-start.2 = (f32[24,1152]{1,0:T(8,128)S(1)}, f32[24,1152]{1,0:T(8,128)S(1)}, u32[]{:S(2)}, u32[]{:S(2)}) collective-permute-start(f32[24,1152]{1,0:T(8,128)S(1)} %shard_map.46.refs_0_), channel_id=1, source_target_pairs={{2,0},{3,1},{4,2},{5,3},{6,4},{7,5},{0,6},{1,7},{10,8},{11,9},{12,... | collective-permute-start | bytes 331784 | tf_op jit(solution)/shard_map/ppermute | solution.py:251
  12.8 1.0 collective-permute-start.7
  13.7 1.1 collective-permute-start.1
  14.8 2.5 %collective-permute-done.2.refs_2_ = f32[24,1152]{1,0:T(8,128)S(1)} collective-permute-done((f32[24,1152]{1,0:T(8,128)S(1)}, f32[24,1152]{1,0:T(8,128)S(1)}, u32[]{:S(2)}, u32[]{:S(2)}) %collective-permute-start.2) | collective-permute-done | bytes 110624 | tf_op jit(solution)/shard_map/ppermute | solution.py:251
  17.4 5.1 %collective-permute-start.4 = (f32[24,1152]{1,0:T(8,128)S(1)}, f32[24,1152]{1,0:T(8,128)S(1)}, u32[]{:S(2)}, u32[]{:S(2)}) collective-permute-start(f32[24,1152]{1,0:T(8,128)S(1)} %collective-permute-done.2.refs_2_), channel_id=1, source_target_pairs={{2,0},{3,1},{4,2},{5,3},{6,4},{7,5},{0,6},{1,7},{10,8},{11,9},{12,... | collective-permute-start | bytes 331784 | tf_op jit(solution)/shard_map/ppermute | solution.py:251
  22.4 1.1 collective-permute-start.3
  23.6 0.9 collective-permute-start.6
  24.6 3.8 %collective-permute-done.6.refs_5_ = f32[24,1152]{1,0:T(8,128)S(1)} collective-permute-done((f32[24,1152]{1,0:T(8,128)S(1)}, f32[24,1152]{1,0:T(8,128)S(1)}, u32[]{:S(2)}, u32[]{:S(2)}) %collective-permute-start.6) | collective-permute-done | bytes 110624 | tf_op jit(solution)/shard_map/ppermute | solution.py:251
  28.6 0.8 shard_map.47
  29.5 3.9 %collective-permute-start.9 = (f32[48,2432]{1,0:T(8,128)S(1)}, f32[48,2432]{1,0:T(8,128)S(1)}, u32[]{:S(2)}, u32[]{:S(2)}) collective-permute-start(f32[48,2432]{1,0:T(8,128)S(1)} %get-tuple-element.51), channel_id=1, source_target_pairs={{160,0},{193,1},{10,2},{67,3},{36,4},{133,5},{174,6},{111,7},{168,... | collective-permute-start | bytes 1400840 | tf_op jit(solution)/shard_map/ppermute | solution.py:338
  33.4 11.6 %collective-permute-done.9.vis = f32[48,2432]{1,0:T(8,128)S(1)} collective-permute-done((f32[48,2432]{1,0:T(8,128)S(1)}, f32[48,2432]{1,0:T(8,128)S(1)}, u32[]{:S(2)}, u32[]{:S(2)}) %collective-permute-start.9) | collective-permute-done | bytes 466976 | tf_op jit(solution)/shard_map/ppermute | solution.py:338
  45.0 2.6 %collective-permute-start.10 = (f32[48,2432]{1,0:T(8,128)S(1)}, f32[48,2432]{1,0:T(8,128)S(1)}, u32[]{:S(2)}, u32[]{:S(2)}) collective-permute-start(f32[48,2432]{1,0:T(8,128)S(1)} %get-tuple-element.52), channel_id=1, source_target_pairs={{32,0},{129,1},{170,2},{107,3},{164,4},{197,5},{14,6},{71,7},{40,8... | collective-permute-start | bytes 1400840 | tf_op jit(solution)/shard_map/ppermute | solution.py:341
  47.6 7.8 %shard_map.48 = (f32[2,48,2304]{2,1,0:T(8,128)S(1)}, f32[2,48,2304]{2,1,0:T(8,128)S(1)}, f32[48,2304]{1,0:T(8,128)S(1)}) custom-call(s32[4]{0:T(128)S(1)} %pad_add_fusion.idx, f32[2,48,2432]{2,1,0:T(8,128)S(1)} %get-tuple-element.49.own, f32[2,48,2432]{2,1,0:T(8,128)S(1)} %collective-permute-done.8.twin, f32[48,2432]{1,0:T(8,128)S(1)} %collective-permute-done.9.vis, ...), custom_call_target="tpu_custom_call" | custom-call | flops 5000000000 | bytes 10000000 | tf_op jit(solution)/shard_map/pallas_call | solution.py:199
  55.4 7.6 %shard_map.49 = (f32[2,48,2304]{2,1,0:T(8,128)S(1)}, f32[2,48,2304]{2,1,0:T(8,128)S(1)}, f32[48,2304]{1,0:T(8,128)S(1)}) custom-call(s32[4]{0:T(128)S(1)} %pad_add_fusion.idx, f32[2,48,2432]{2,1,0:T(8,128)S(1)} %get-tuple-element.49.own, f32[2,48,2432]{2,1,0:T(8,128)S(1)} %collective-permute-done.8.twin, f32[48,2432]{1,0:T(8,128)S(1)} %collective-permute-done.10.vis, ...), custom_call_target="tpu_custom_call" | custom-call | flops 5000000000 | bytes 10000000 | tf_op jit(solution)/shard_map/pallas_call | solution.py:199
  63.2 2.3 %collective-permute-start.13 = (f32[48,2304]{1,0:T(8,128)S(1)}, f32[48,2304]{1,0:T(8,128)S(1)}, u32[]{:S(2)}, u32[]{:S(2)}) collective-permute-start(f32[48,2304]{1,0:T(8,128)S(1)} %get-tuple-element.64), channel_id=1, source_target_pairs={{0,32},{1,129},{2,170},{3,107},{4,164},{5,197},{6,14},{8,40},{9,13... | collective-permute-start | bytes 1327112 | tf_op jit(solution)/shard_map/ppermute | solution.py:298
  65.5 4.6 %collective-permute-start.12 = (f32[48,2304]{1,0:T(8,128)S(1)}, f32[48,2304]{1,0:T(8,128)S(1)}, u32[]{:S(2)}, u32[]{:S(2)}) collective-permute-start(f32[48,2304]{1,0:T(8,128)S(1)} %get-tuple-element.63), channel_id=1, source_target_pairs={{0,160},{1,193},{2,10},{4,36},{5,133},{6,174},{7,111},{8,168},{9,2... | collective-permute-start | bytes 1327112 | tf_op jit(solution)/shard_map/ppermute | solution.py:298
  70.1 4.5 %collective-permute-done.13.c1 = f32[48,2304]{1,0:T(8,128)S(1)} collective-permute-done((f32[48,2304]{1,0:T(8,128)S(1)}, f32[48,2304]{1,0:T(8,128)S(1)}, u32[]{:S(2)}, u32[]{:S(2)}) %collective-permute-start.13) | collective-permute-done | bytes 442400 | tf_op jit(solution)/shard_map/ppermute | solution.py:298
  74.6 9.5 %collective-permute-done.12.c0 = f32[48,2304]{1,0:T(8,128)S(1)} collective-permute-done((f32[48,2304]{1,0:T(8,128)S(1)}, f32[48,2304]{1,0:T(8,128)S(1)}, u32[]{:S(2)}, u32[]{:S(2)}) %collective-permute-start.12) | collective-permute-done | bytes 442400 | tf_op jit(solution)/shard_map/ppermute | solution.py:298
  84.6 4.7 %collective-permute-start.14 = (f32[24,1152]{1,0:T(8,128)S(1)}, f32[24,1152]{1,0:T(8,128)S(1)}, u32[]{:S(2)}, u32[]{:S(2)}) collective-permute-start(f32[24,1152]{1,0:T(8,128)S(1)} %get-tuple-element.66), channel_id=1, source_target_pairs={{4,0},{5,1},{6,2},{7,3},{0,4},{1,5},{2,6},{3,7},{12,8},{13,9},{14,... | collective-permute-start | bytes 331784 | tf_op jit(solution)/shard_map/ppermute | solution.py:251
  89.3 4.9 %collective-permute-start.15 = (f32[24,1152]{1,0:T(8,128)S(1)}, f32[24,1152]{1,0:T(8,128)S(1)}, u32[]{:S(2)}, u32[]{:S(2)}) collective-permute-start(f32[24,1152]{1,0:T(8,128)S(1)} %get-tuple-element.67), channel_id=1, source_target_pairs={{5,0},{6,1},{7,2},{0,3},{1,4},{2,5},{3,6},{4,7},{13,8},{14,9},{15,... | collective-permute-start | bytes 331784 | tf_op jit(solution)/shard_map/ppermute | solution.py:251
  94.8 1.5 %collective-permute-start.17 = (f32[24,1152]{1,0:T(8,128)S(1)}, f32[24,1152]{1,0:T(8,128)S(1)}, u32[]{:S(2)}, u32[]{:S(2)}) collective-permute-start(f32[24,1152]{1,0:T(8,128)S(1)} %get-tuple-element.69), channel_id=1, source_target_pairs={{6,0},{7,1},{0,2},{1,3},{2,4},{3,5},{4,6},{5,7},{14,8},{15,9},{8,1... | collective-permute-start | bytes 331784 | tf_op jit(solution)/shard_map/ppermute | solution.py:251
  96.2 2.7 %collective-permute-start.18 = (f32[24,1152]{1,0:T(8,128)S(1)}, f32[24,1152]{1,0:T(8,128)S(1)}, u32[]{:S(2)}, u32[]{:S(2)}) collective-permute-start(f32[24,1152]{1,0:T(8,128)S(1)} %get-tuple-element.70), channel_id=1, source_target_pairs={{2,0},{3,1},{4,2},{5,3},{6,4},{7,5},{0,6},{1,7},{10,8},{11,9},{12,... | collective-permute-start | bytes 331784 | tf_op jit(solution)/shard_map/ppermute | solution.py:251
  98.9 7.6 %collective-permute-start.19 = (f32[24,1152]{1,0:T(8,128)S(1)}, f32[24,1152]{1,0:T(8,128)S(1)}, u32[]{:S(2)}, u32[]{:S(2)}) collective-permute-start(f32[24,1152]{1,0:T(8,128)S(1)} %get-tuple-element.71), channel_id=1, source_target_pairs={{7,0},{0,1},{1,2},{2,3},{3,4},{4,5},{5,6},{6,7},{15,8},{8,9},{9,10... | collective-permute-start | bytes 331784 | tf_op jit(solution)/shard_map/ppermute | solution.py:251
  106.5 1.8 %collective-permute-done.15.refs_2_ = f32[24,1152]{1,0:T(8,128)S(1)} collective-permute-done((f32[24,1152]{1,0:T(8,128)S(1)}, f32[24,1152]{1,0:T(8,128)S(1)}, u32[]{:S(2)}, u32[]{:S(2)}) %collective-permute-start.15) | collective-permute-done | bytes 110624 | tf_op jit(solution)/shard_map/ppermute | solution.py:251
  108.3 2.1 %collective-permute-done.17.refs_4_ = f32[24,1152]{1,0:T(8,128)S(1)} collective-permute-done((f32[24,1152]{1,0:T(8,128)S(1)}, f32[24,1152]{1,0:T(8,128)S(1)}, u32[]{:S(2)}, u32[]{:S(2)}) %collective-permute-start.17) | collective-permute-done | bytes 110624 | tf_op jit(solution)/shard_map/ppermute | solution.py:251
  110.4 2.6 %collective-permute-done.20.refs_7_ = f32[24,1152]{1,0:T(8,128)S(1)} collective-permute-done((f32[24,1152]{1,0:T(8,128)S(1)}, f32[24,1152]{1,0:T(8,128)S(1)}, u32[]{:S(2)}, u32[]{:S(2)}) %collective-permute-start.20) | collective-permute-done | bytes 110624 | tf_op jit(solution)/shard_map/ppermute | solution.py:251
  113.3 5.6 %collective-permute-done.21 = f32[3,2,2304]{2,1,0:T(2,128)S(1)} collective-permute-done((f32[3,2,2304]{2,1,0:T(2,128)S(1)}, f32[3,2,2304]{2,1,0:T(2,128)S(1)}, u32[]{:S(2)}, u32[]{:S(2)}) %collective-permute-start.21) | collective-permute-done | bytes 55328 | tf_op jit(solution)/shard_map/ppermute | solution.py:251
  119.0 0.7 maximum_bitcast_fusion
  (42 shorter events, 2.6 us)
Async XLA Ops:
  0.0 47.6 %copy-start.2 = (bf16[96,96]{1,0:T(8,128)(2,1)S(1)}, bf16[96,96]{1,0:T(8,128)(2,1)}, u32[]{:S(2)}) copy-start(bf16[96,96]{1,0:T(8,128)(2,1)} %constant.185.iz) | copy-start | bytes 55300
  0.0 47.6 %copy-start.3 = (bf16[96,96]{1,0:T(8,128)(2,1)S(1)}, bf16[96,96]{1,0:T(8,128)(2,1)}, u32[]{:S(2)}) copy-start(bf16[96,96]{1,0:T(8,128)(2,1)} %constant.177.fz) | copy-start | bytes 55300
  0.0 7.1 %copy-start = (f32[4,3,2304]{2,0,1:T(4,128)S(1)}, f32[4,3,2304]{2,0,1:T(4,128)}, u32[]{:S(2)}) copy-start(f32[4,3,2304]{2,0,1:T(4,128)} %param.4) | copy-start | bytes 331780
  0.0 28.6 %copy-start.1 = (s32[4]{0:T(128)S(1)}, s32[4]{0:T(128)}, u32[]{:S(2)}) copy-start(s32[4]{0:T(128)} %occupation.1) | copy-start | bytes 52
  1.1 6.0 %collective-permute-start = (f32[3,2,2304]{2,1,0:T(2,128)S(1)}, f32[3,2,2304]{2,1,0:T(2,128)S(1)}, u32[]{:S(2)}, u32[]{:S(2)}) collective-permute-start(f32[3,2,2304]{2,1,0:T(2,128)S(1)} %slice_select_fusion), channel_id=1, source_target_pairs={{8,0},{9,1},{10,2},{11,3},{12,4},{13,5},{14,6},{15,7},{0,8},{1,9},... | collective-permute-start | bytes 165896 | tf_op jit(solution)/shard_map/ppermute | solution.py:251
  7.1 16.5 %collective-permute-start.5 = (f32[24,1152]{1,0:T(8,128)S(1)}, f32[24,1152]{1,0:T(8,128)S(1)}, u32[]{:S(2)}, u32[]{:S(2)}) collective-permute-start(f32[24,1152]{1,0:T(8,128)S(1)} %shard_map.46.refs_0_), channel_id=1, source_target_pairs={{6,0},{7,1},{0,2},{1,3},{2,4},{3,5},{4,6},{5,7},{14,8},{15,9},{8,1... | collective-permute-start | bytes 331784 | tf_op jit(solution)/shard_map/ppermute | solution.py:251
  10.5 6.9 %collective-permute-start.2 = (f32[24,1152]{1,0:T(8,128)S(1)}, f32[24,1152]{1,0:T(8,128)S(1)}, u32[]{:S(2)}, u32[]{:S(2)}) collective-permute-start(f32[24,1152]{1,0:T(8,128)S(1)} %shard_map.46.refs_0_), channel_id=1, source_target_pairs={{2,0},{3,1},{4,2},{5,3},{6,4},{7,5},{0,6},{1,7},{10,8},{11,9},{12,... | collective-permute-start | bytes 331784 | tf_op jit(solution)/shard_map/ppermute | solution.py:251
  12.8 11.8 %collective-permute-start.7 = (f32[24,1152]{1,0:T(8,128)S(1)}, f32[24,1152]{1,0:T(8,128)S(1)}, u32[]{:S(2)}, u32[]{:S(2)}) collective-permute-start(f32[24,1152]{1,0:T(8,128)S(1)} %shard_map.46.refs_0_), channel_id=1, source_target_pairs={{7,0},{0,1},{1,2},{2,3},{3,4},{4,5},{5,6},{6,7},{15,8},{8,9},{9,10... | collective-permute-start | bytes 331784 | tf_op jit(solution)/shard_map/ppermute | solution.py:251
  13.7 10.8 %collective-permute-start.1 = (f32[24,1152]{1,0:T(8,128)S(1)}, f32[24,1152]{1,0:T(8,128)S(1)}, u32[]{:S(2)}, u32[]{:S(2)}) collective-permute-start(f32[24,1152]{1,0:T(8,128)S(1)} %shard_map.46.refs_0_), channel_id=1, source_target_pairs={{1,0},{2,1},{3,2},{4,3},{5,4},{6,5},{7,6},{0,7},{9,8},{10,9},{11,1... | collective-permute-start | bytes 331784 | tf_op jit(solution)/shard_map/ppermute | solution.py:251
  17.4 11.0 %collective-permute-start.4 = (f32[24,1152]{1,0:T(8,128)S(1)}, f32[24,1152]{1,0:T(8,128)S(1)}, u32[]{:S(2)}, u32[]{:S(2)}) collective-permute-start(f32[24,1152]{1,0:T(8,128)S(1)} %collective-permute-done.2.refs_2_), channel_id=1, source_target_pairs={{2,0},{3,1},{4,2},{5,3},{6,4},{7,5},{0,6},{1,7},{10,8},{11,9},{12,... | collective-permute-start | bytes 331784 | tf_op jit(solution)/shard_map/ppermute | solution.py:251
  22.4 6.2 %collective-permute-start.3 = (f32[24,1152]{1,0:T(8,128)S(1)}, f32[24,1152]{1,0:T(8,128)S(1)}, u32[]{:S(2)}, u32[]{:S(2)}) collective-permute-start(f32[24,1152]{1,0:T(8,128)S(1)} %collective-permute-done.2.refs_2_), channel_id=1, source_target_pairs={{1,0},{2,1},{3,2},{4,3},{5,4},{6,5},{7,6},{0,7},{9,8},{10,9},{11,1... | collective-permute-start | bytes 331784 | tf_op jit(solution)/shard_map/ppermute | solution.py:251
  23.6 4.7 %collective-permute-start.6 = (f32[24,1152]{1,0:T(8,128)S(1)}, f32[24,1152]{1,0:T(8,128)S(1)}, u32[]{:S(2)}, u32[]{:S(2)}) collective-permute-start(f32[24,1152]{1,0:T(8,128)S(1)} %collective-permute-done.5.refs_6_), channel_id=1, source_target_pairs={{7,0},{0,1},{1,2},{2,3},{3,4},{4,5},{5,6},{6,7},{15,8},{8,9},{9,10... | collective-permute-start | bytes 331784 | tf_op jit(solution)/shard_map/ppermute | solution.py:251
  29.4 18.2 %collective-permute-start.8 = (f32[2,48,2432]{2,1,0:T(8,128)S(1)}, f32[2,48,2432]{2,1,0:T(8,128)S(1)}, u32[]{:S(2)}, u32[]{:S(2)}) collective-permute-start(f32[2,48,2432]{2,1,0:T(8,128)S(1)} %get-tuple-element.49.own), channel_id=1, source_target_pairs={{16,0},{0,16},{48,32},{32,48},{80,64},{64,80},{112,96},{96,112},{1... | collective-permute-start | bytes 2801672 | tf_op jit(solution)/shard_map/ppermute | solution.py:251
  29.5 15.5 %collective-permute-start.9 = (f32[48,2432]{1,0:T(8,128)S(1)}, f32[48,2432]{1,0:T(8,128)S(1)}, u32[]{:S(2)}, u32[]{:S(2)}) collective-permute-start(f32[48,2432]{1,0:T(8,128)S(1)} %get-tuple-element.51), channel_id=1, source_target_pairs={{160,0},{193,1},{10,2},{67,3},{36,4},{133,5},{174,6},{111,7},{168,... | collective-permute-start | bytes 1400840 | tf_op jit(solution)/shard_map/ppermute | solution.py:338
  45.0 10.4 %collective-permute-start.10 = (f32[48,2432]{1,0:T(8,128)S(1)}, f32[48,2432]{1,0:T(8,128)S(1)}, u32[]{:S(2)}, u32[]{:S(2)}) collective-permute-start(f32[48,2432]{1,0:T(8,128)S(1)} %get-tuple-element.52), channel_id=1, source_target_pairs={{32,0},{129,1},{170,2},{107,3},{164,4},{197,5},{14,6},{71,7},{40,8... | collective-permute-start | bytes 1400840 | tf_op jit(solution)/shard_map/ppermute | solution.py:341
  63.1 21.1 %collective-permute-start.11 = (f32[2,48,2304]{2,1,0:T(8,128)S(1)}, f32[2,48,2304]{2,1,0:T(8,128)S(1)}, u32[]{:S(2)}, u32[]{:S(2)}) collective-permute-start(f32[2,48,2304]{2,1,0:T(8,128)S(1)} %get-tuple-element.62), channel_id=1, source_target_pairs={{16,0},{0,16},{48,32},{32,48},{80,64},{64,80},{112,96},{96,112},{1... | collective-permute-start | bytes 2654216 | tf_op jit(solution)/shard_map/ppermute | solution.py:251
  63.2 11.4 %collective-permute-start.13 = (f32[48,2304]{1,0:T(8,128)S(1)}, f32[48,2304]{1,0:T(8,128)S(1)}, u32[]{:S(2)}, u32[]{:S(2)}) collective-permute-start(f32[48,2304]{1,0:T(8,128)S(1)} %get-tuple-element.64), channel_id=1, source_target_pairs={{0,32},{1,129},{2,170},{3,107},{4,164},{5,197},{6,14},{8,40},{9,13... | collective-permute-start | bytes 1327112 | tf_op jit(solution)/shard_map/ppermute | solution.py:298
  65.5 18.6 %collective-permute-start.12 = (f32[48,2304]{1,0:T(8,128)S(1)}, f32[48,2304]{1,0:T(8,128)S(1)}, u32[]{:S(2)}, u32[]{:S(2)}) collective-permute-start(f32[48,2304]{1,0:T(8,128)S(1)} %get-tuple-element.63), channel_id=1, source_target_pairs={{0,160},{1,193},{2,10},{4,36},{5,133},{6,174},{7,111},{8,168},{9,2... | collective-permute-start | bytes 1327112 | tf_op jit(solution)/shard_map/ppermute | solution.py:298
  84.6 14.3 %collective-permute-start.14 = (f32[24,1152]{1,0:T(8,128)S(1)}, f32[24,1152]{1,0:T(8,128)S(1)}, u32[]{:S(2)}, u32[]{:S(2)}) collective-permute-start(f32[24,1152]{1,0:T(8,128)S(1)} %get-tuple-element.66), channel_id=1, source_target_pairs={{4,0},{5,1},{6,2},{7,3},{0,4},{1,5},{2,6},{3,7},{12,8},{13,9},{14,... | collective-permute-start | bytes 331784 | tf_op jit(solution)/shard_map/ppermute | solution.py:251
  89.3 19.1 %collective-permute-start.15 = (f32[24,1152]{1,0:T(8,128)S(1)}, f32[24,1152]{1,0:T(8,128)S(1)}, u32[]{:S(2)}, u32[]{:S(2)}) collective-permute-start(f32[24,1152]{1,0:T(8,128)S(1)} %get-tuple-element.67), channel_id=1, source_target_pairs={{5,0},{6,1},{7,2},{0,3},{1,4},{2,5},{3,6},{4,7},{13,8},{14,9},{15,... | collective-permute-start | bytes 331784 | tf_op jit(solution)/shard_map/ppermute | solution.py:251
  94.1 14.2 %collective-permute-start.16 = (f32[24,1152]{1,0:T(8,128)S(1)}, f32[24,1152]{1,0:T(8,128)S(1)}, u32[]{:S(2)}, u32[]{:S(2)}) collective-permute-start(f32[24,1152]{1,0:T(8,128)S(1)} %get-tuple-element.68), channel_id=1, source_target_pairs={{3,0},{4,1},{5,2},{6,3},{7,4},{0,5},{1,6},{2,7},{11,8},{12,9},{13,... | collective-permute-start | bytes 331784 | tf_op jit(solution)/shard_map/ppermute | solution.py:251
  94.8 15.7 %collective-permute-start.17 = (f32[24,1152]{1,0:T(8,128)S(1)}, f32[24,1152]{1,0:T(8,128)S(1)}, u32[]{:S(2)}, u32[]{:S(2)}) collective-permute-start(f32[24,1152]{1,0:T(8,128)S(1)} %get-tuple-element.69), channel_id=1, source_target_pairs={{6,0},{7,1},{0,2},{1,3},{2,4},{3,5},{4,6},{5,7},{14,8},{15,9},{8,1... | collective-permute-start | bytes 331784 | tf_op jit(solution)/shard_map/ppermute | solution.py:251
  96.2 14.2 %collective-permute-start.18 = (f32[24,1152]{1,0:T(8,128)S(1)}, f32[24,1152]{1,0:T(8,128)S(1)}, u32[]{:S(2)}, u32[]{:S(2)}) collective-permute-start(f32[24,1152]{1,0:T(8,128)S(1)} %get-tuple-element.70), channel_id=1, source_target_pairs={{2,0},{3,1},{4,2},{5,3},{6,4},{7,5},{0,6},{1,7},{10,8},{11,9},{12,... | collective-permute-start | bytes 331784 | tf_op jit(solution)/shard_map/ppermute | solution.py:251
  98.9 11.5 %collective-permute-start.19 = (f32[24,1152]{1,0:T(8,128)S(1)}, f32[24,1152]{1,0:T(8,128)S(1)}, u32[]{:S(2)}, u32[]{:S(2)}) collective-permute-start(f32[24,1152]{1,0:T(8,128)S(1)} %get-tuple-element.71), channel_id=1, source_target_pairs={{7,0},{0,1},{1,2},{2,3},{3,4},{4,5},{5,6},{6,7},{15,8},{8,9},{9,10... | collective-permute-start | bytes 331784 | tf_op jit(solution)/shard_map/ppermute | solution.py:251
  108.3 4.7 %collective-permute-start.20 = (f32[24,1152]{1,0:T(8,128)S(1)}, f32[24,1152]{1,0:T(8,128)S(1)}, u32[]{:S(2)}, u32[]{:S(2)}) collective-permute-start(f32[24,1152]{1,0:T(8,128)S(1)} %get-tuple-element.72), channel_id=1, source_target_pairs={{1,0},{2,1},{3,2},{4,3},{5,4},{6,5},{7,6},{0,7},{9,8},{10,9},{11,1... | collective-permute-start | bytes 331784 | tf_op jit(solution)/shard_map/ppermute | solution.py:251
  113.2 5.7 %collective-permute-start.21 = (f32[3,2,2304]{2,1,0:T(2,128)S(1)}, f32[3,2,2304]{2,1,0:T(2,128)S(1)}, u32[]{:S(2)}, u32[]{:S(2)}) collective-permute-start(f32[3,2,2304]{2,1,0:T(2,128)S(1)} %get-tuple-element.74), channel_id=1, source_target_pairs={{8,0},{9,1},{10,2},{11,3},{12,4},{13,5},{14,6},{15,7},{0,8},{1,9},... | collective-permute-start | bytes 165896 | tf_op jit(solution)/shard_map/ppermute | solution.py:251

commit v6 on v5

--- a/solution.py
+++ b/solution.py
@@ -301,15 +301,17 @@
 def gather_blocks(b0):
     got = {0: b0}
     for k, source, hop in (
-        (2, 0, 2), (6, 0, 6), (1, 0, 1), (7, 0, 7),
-        (3, 2, 1), (5, 6, 7), (4, 2, 2),
+        (2, 0, 2), (6, 0, 6), (1, 0, 1), (7, 0, 7), (3, 2, 1), (4, 2, 2), (5, 6, 7),
     ):
         got[k] = ring(got[source], "grid", along(hop))
     return [got[k] for k in range(8)]
 
 
 def scatter_blocks(part):
-    return [part[0]] + [ring(part[k], "grid", along(-k)) for k in (4, 3, 5, 2, 6, 1, 7)]
+    came = [part[0]]
+    for k in (3, 5, 4, 2, 6, 1, 7):
+        came.append(ring(part[k], "grid", along(-k)))
+    return came
 
 
 def on_device(orbitals, occupation, cutoff):

time: 120 us -> 119 us (level)
  the two profiles are of different devices: /device:TPU:32 before, /device:TPU:1 now
where the time goes in v6:
time: 119 us
  starting transfers between devices  51 us (43%)
  waiting for transfers between devices  46 us (39%)
  Pallas kernels  16.8 us (14%)
  other arithmetic  3.88 us (3%)
    ppermute x18, starting transfers between devices, ring(): lax.ppermute(block, axis, [(source(i), i) for i in range(lax.axis_size(ax...  35.1 us
    ppermute x18, waiting for transfers between devices, ring(): lax.ppermute(block, axis, [(source(i), i) for i in range(lax.axis_size(ax...  20.5 us
    pallas_call x2, Pallas kernels, pair_solver(): pl.pallas_call(functools.partial(kernel, first), out_shape=[f32(2, G, ROW...  15.4 us
    ppermute x2, waiting for transfers between devices, returned(): lax.ppermute(back, ('band', 'grid'), [(d, s) for s, d in visit_route(v, F...  14.3 us
    ppermute x1, waiting for transfers between devices, on_device(): vis0 = lax.ppermute(lone[0], axes, visit_route(0))  9.96 us
    ppermute x2, starting transfers between devices, returned(): lax.ppermute(back, ('band', 'grid'), [(d, s) for s, d in visit_route(v, F...  9.09 us
    ppermute x1, starting transfers between devices, on_device(): vis0 = lax.ppermute(lone[0], axes, visit_route(0))  4.79 us
  transfers between devices with their start and end apart: 22, of which 11 were waited for; matrix products, arithmetic and copies ran while one was open for 2% of the time, Pallas kernels for 7%

profile of v6, /device:TPU:1, one launch (start us, length us, event | category | flops | bytes accessed | tf_op | source)
XLA Modules:
  0.0 118.6 jit_solution(14195312495958346154)
XLA Ops:
  0.0 1.1 slice_select_fusion
  1.1 3.8 %collective-permute-start = (f32[3,2,2304]{2,1,0:T(2,128)S(1)}, f32[3,2,2304]{2,1,0:T(2,128)S(1)}, u32[]{:S(2)}, u32[]{:S(2)}) collective-permute-start(f32[3,2,2304]{2,1,0:T(2,128)S(1)} %slice_select_fusion), channel_id=1, source_target_pairs={{8,0},{9,1},{10,2},{11,3},{12,4},{13,5},{14,6},{15,7},{0,8},{1,9},... | collective-permute-start | bytes 165896 | tf_op jit(solution)/shard_map/ppermute | solution.py:251
  5.8 1.4 %fusion.9.ktab = f32[48,48,256]{2,1,0:T(8,128)S(1)} fusion(f32[256]{0:T(256)S(1)} %or_select_fusion, f32[48,48]{1,0:T(8,128)S(1)} %broadcast_multiply_fusion, s32[]{:T(128)S(6)} %copy.5, s32[256]{0:T(256)S(1)} %fusion.26, s32[48,48]{1,0:T(8,128)S(1)} %broadcast_add_fusion), kind=kLoop, calls=%fused_computation.12 | loop fusion | flops 8847360 | bytes 2379780 | tf_op jit(solution)/shard_map/jit(_where)/select_n | solution.py:247
  7.7 3.1 %collective-permute-start.5 = (f32[24,1152]{1,0:T(8,128)S(1)}, f32[24,1152]{1,0:T(8,128)S(1)}, u32[]{:S(2)}, u32[]{:S(2)}) collective-permute-start(f32[24,1152]{1,0:T(8,128)S(1)} %shard_map.46.refs_0_), channel_id=1, source_target_pairs={{6,0},{7,1},{0,2},{1,3},{2,4},{3,5},{4,6},{5,7},{14,8},{15,9},{8,1... | collective-permute-start | bytes 331784 | tf_op jit(solution)/shard_map/ppermute | solution.py:251
  10.7 3.1 %collective-permute-start.2 = (f32[24,1152]{1,0:T(8,128)S(1)}, f32[24,1152]{1,0:T(8,128)S(1)}, u32[]{:S(2)}, u32[]{:S(2)}) collective-permute-start(f32[24,1152]{1,0:T(8,128)S(1)} %shard_map.46.refs_0_), channel_id=1, source_target_pairs={{2,0},{3,1},{4,2},{5,3},{6,4},{7,5},{0,6},{1,7},{10,8},{11,9},{12,... | collective-permute-start | bytes 331784 | tf_op jit(solution)/shard_map/ppermute | solution.py:251
  13.9 0.8 collective-permute-start.7
  14.7 1.9 %collective-permute-start.1 = (f32[24,1152]{1,0:T(8,128)S(1)}, f32[24,1152]{1,0:T(8,128)S(1)}, u32[]{:S(2)}, u32[]{:S(2)}) collective-permute-start(f32[24,1152]{1,0:T(8,128)S(1)} %shard_map.46.refs_0_), channel_id=1, source_target_pairs={{1,0},{2,1},{3,2},{4,3},{5,4},{6,5},{7,6},{0,7},{9,8},{10,9},{11,1... | collective-permute-start | bytes 331784 | tf_op jit(solution)/shard_map/ppermute | solution.py:251
  16.7 3.8 %collective-permute-done.2.refs_2_ = f32[24,1152]{1,0:T(8,128)S(1)} collective-permute-done((f32[24,1152]{1,0:T(8,128)S(1)}, f32[24,1152]{1,0:T(8,128)S(1)}, u32[]{:S(2)}, u32[]{:S(2)}) %collective-permute-start.2) | collective-permute-done | bytes 110624 | tf_op jit(solution)/shard_map/ppermute | solution.py:251
  20.4 1.4 %collective-permute-start.4 = (f32[24,1152]{1,0:T(8,128)S(1)}, f32[24,1152]{1,0:T(8,128)S(1)}, u32[]{:S(2)}, u32[]{:S(2)}) collective-permute-start(f32[24,1152]{1,0:T(8,128)S(1)} %collective-permute-done.2.refs_2_), channel_id=1, source_target_pairs={{2,0},{3,1},{4,2},{5,3},{6,4},{7,5},{0,6},{1,7},{10,8},{11,9},{12,... | collective-permute-start | bytes 331784 | tf_op jit(solution)/shard_map/ppermute | solution.py:251
  21.8 1.5 %collective-permute-start.6 = (f32[24,1152]{1,0:T(8,128)S(1)}, f32[24,1152]{1,0:T(8,128)S(1)}, u32[]{:S(2)}, u32[]{:S(2)}) collective-permute-start(f32[24,1152]{1,0:T(8,128)S(1)} %collective-permute-done.5.refs_6_), channel_id=1, source_target_pairs={{7,0},{0,1},{1,2},{2,3},{3,4},{4,5},{5,6},{6,7},{15,8},{8,9},{9,10... | collective-permute-start | bytes 331784 | tf_op jit(solution)/shard_map/ppermute | solution.py:251
  23.4 3.3 %collective-permute-done.6.refs_5_ = f32[24,1152]{1,0:T(8,128)S(1)} collective-permute-done((f32[24,1152]{1,0:T(8,128)S(1)}, f32[24,1152]{1,0:T(8,128)S(1)}, u32[]{:S(2)}, u32[]{:S(2)}) %collective-permute-start.6) | collective-permute-done | bytes 110624 | tf_op jit(solution)/shard_map/ppermute | solution.py:251
  26.7 0.8 shard_map.47
  27.5 5.1 %collective-permute-start.8 = (f32[2,48,2432]{2,1,0:T(8,128)S(1)}, f32[2,48,2432]{2,1,0:T(8,128)S(1)}, u32[]{:S(2)}, u32[]{:S(2)}) collective-permute-start(f32[2,48,2432]{2,1,0:T(8,128)S(1)} %get-tuple-element.49.own), channel_id=1, source_target_pairs={{16,0},{0,16},{48,32},{32,48},{80,64},{64,80},{112,96},{96,112},{1... | collective-permute-start | bytes 2801672 | tf_op jit(solution)/shard_map/ppermute | solution.py:251
  32.5 4.8 %collective-permute-start.9 = (f32[48,2432]{1,0:T(8,128)S(1)}, f32[48,2432]{1,0:T(8,128)S(1)}, u32[]{:S(2)}, u32[]{:S(2)}) collective-permute-start(f32[48,2432]{1,0:T(8,128)S(1)} %get-tuple-element.51), channel_id=1, source_target_pairs={{160,0},{193,1},{10,2},{67,3},{36,4},{133,5},{174,6},{111,7},{168,... | collective-permute-start | bytes 1400840 | tf_op jit(solution)/shard_map/ppermute | solution.py:340
  37.3 10.0 %collective-permute-done.9.vis = f32[48,2432]{1,0:T(8,128)S(1)} collective-permute-done((f32[48,2432]{1,0:T(8,128)S(1)}, f32[48,2432]{1,0:T(8,128)S(1)}, u32[]{:S(2)}, u32[]{:S(2)}) %collective-permute-start.9) | collective-permute-done | bytes 466976 | tf_op jit(solution)/shard_map/ppermute | solution.py:340
  47.3 2.0 %collective-permute-start.10 = (f32[48,2432]{1,0:T(8,128)S(1)}, f32[48,2432]{1,0:T(8,128)S(1)}, u32[]{:S(2)}, u32[]{:S(2)}) collective-permute-start(f32[48,2432]{1,0:T(8,128)S(1)} %get-tuple-element.52), channel_id=1, source_target_pairs={{32,0},{129,1},{170,2},{107,3},{164,4},{197,5},{14,6},{71,7},{40,8... | collective-permute-start | bytes 1400840 | tf_op jit(solution)/shard_map/ppermute | solution.py:343
  49.3 7.8 %shard_map.48 = (f32[2,48,2304]{2,1,0:T(8,128)S(1)}, f32[2,48,2304]{2,1,0:T(8,128)S(1)}, f32[48,2304]{1,0:T(8,128)S(1)}) custom-call(s32[4]{0:T(128)S(1)} %pad_add_fusion.idx, f32[2,48,2432]{2,1,0:T(8,128)S(1)} %get-tuple-element.49.own, f32[2,48,2432]{2,1,0:T(8,128)S(1)} %collective-permute-done.8.twin, f32[48,2432]{1,0:T(8,128)S(1)} %collective-permute-done.9.vis, ...), custom_call_target="tpu_custom_call" | custom-call | flops 5000000000 | bytes 10000000 | tf_op jit(solution)/shard_map/pallas_call | solution.py:199
  57.1 1.2 collective-permute-done.10.vis
  58.3 7.6 %shard_map.49 = (f32[2,48,2304]{2,1,0:T(8,128)S(1)}, f32[2,48,2304]{2,1,0:T(8,128)S(1)}, f32[48,2304]{1,0:T(8,128)S(1)}) custom-call(s32[4]{0:T(128)S(1)} %pad_add_fusion.idx, f32[2,48,2432]{2,1,0:T(8,128)S(1)} %get-tuple-element.49.own, f32[2,48,2432]{2,1,0:T(8,128)S(1)} %collective-permute-done.8.twin, f32[48,2432]{1,0:T(8,128)S(1)} %collective-permute-done.10.vis, ...), custom_call_target="tpu_custom_call" | custom-call | flops 5000000000 | bytes 10000000 | tf_op jit(solution)/shard_map/pallas_call | solution.py:199
  66.1 6.0 %collective-permute-start.13 = (f32[48,2304]{1,0:T(8,128)S(1)}, f32[48,2304]{1,0:T(8,128)S(1)}, u32[]{:S(2)}, u32[]{:S(2)}) collective-permute-start(f32[48,2304]{1,0:T(8,128)S(1)} %get-tuple-element.64), channel_id=1, source_target_pairs={{0,32},{1,129},{2,170},{3,107},{4,164},{5,197},{6,14},{8,40},{9,13... | collective-permute-start | bytes 1327112 | tf_op jit(solution)/shard_map/ppermute | solution.py:298
  72.1 3.1 %collective-permute-start.12 = (f32[48,2304]{1,0:T(8,128)S(1)}, f32[48,2304]{1,0:T(8,128)S(1)}, u32[]{:S(2)}, u32[]{:S(2)}) collective-permute-start(f32[48,2304]{1,0:T(8,128)S(1)} %get-tuple-element.63), channel_id=1, source_target_pairs={{0,160},{1,193},{2,10},{4,36},{5,133},{6,174},{7,111},{8,168},{9,2... | collective-permute-start | bytes 1327112 | tf_op jit(solution)/shard_map/ppermute | solution.py:298
  75.2 3.1 %collective-permute-done.13.c1 = f32[48,2304]{1,0:T(8,128)S(1)} collective-permute-done((f32[48,2304]{1,0:T(8,128)S(1)}, f32[48,2304]{1,0:T(8,128)S(1)}, u32[]{:S(2)}, u32[]{:S(2)}) %collective-permute-start.13) | collective-permute-done | bytes 442400 | tf_op jit(solution)/shard_map/ppermute | solution.py:298
  78.3 11.2 %collective-permute-done.12.c0 = f32[48,2304]{1,0:T(8,128)S(1)} collective-permute-done((f32[48,2304]{1,0:T(8,128)S(1)}, f32[48,2304]{1,0:T(8,128)S(1)}, u32[]{:S(2)}, u32[]{:S(2)}) %collective-permute-start.12) | collective-permute-done | bytes 442400 | tf_op jit(solution)/shard_map/ppermute | solution.py:298
  90.3 4.5 %collective-permute-start.15 = (f32[24,1152]{1,0:T(8,128)S(1)}, f32[24,1152]{1,0:T(8,128)S(1)}, u32[]{:S(2)}, u32[]{:S(2)}) collective-permute-start(f32[24,1152]{1,0:T(8,128)S(1)} %get-tuple-element.67), channel_id=1, source_target_pairs={{3,0},{4,1},{5,2},{6,3},{7,4},{0,5},{1,6},{2,7},{11,8},{12,9},{13,... | collective-permute-start | bytes 331784 | tf_op jit(solution)/shard_map/ppermute | solution.py:251
  94.7 1.1 collective-permute-start.16
  96.2 3.3 %collective-permute-start.18 = (f32[24,1152]{1,0:T(8,128)S(1)}, f32[24,1152]{1,0:T(8,128)S(1)}, u32[]{:S(2)}, u32[]{:S(2)}) collective-permute-start(f32[24,1152]{1,0:T(8,128)S(1)} %get-tuple-element.70), channel_id=1, source_target_pairs={{2,0},{3,1},{4,2},{5,3},{6,4},{7,5},{0,6},{1,7},{10,8},{11,9},{12,... | collective-permute-start | bytes 331784 | tf_op jit(solution)/shard_map/ppermute | solution.py:251
  99.5 2.8 %collective-permute-start.19 = (f32[24,1152]{1,0:T(8,128)S(1)}, f32[24,1152]{1,0:T(8,128)S(1)}, u32[]{:S(2)}, u32[]{:S(2)}) collective-permute-start(f32[24,1152]{1,0:T(8,128)S(1)} %get-tuple-element.71), channel_id=1, source_target_pairs={{7,0},{0,1},{1,2},{2,3},{3,4},{4,5},{5,6},{6,7},{15,8},{8,9},{9,10... | collective-permute-start | bytes 331784 | tf_op jit(solution)/shard_map/ppermute | solution.py:251
  102.3 1.4 %collective-permute-start.20 = (f32[24,1152]{1,0:T(8,128)S(1)}, f32[24,1152]{1,0:T(8,128)S(1)}, u32[]{:S(2)}, u32[]{:S(2)}) collective-permute-start(f32[24,1152]{1,0:T(8,128)S(1)} %get-tuple-element.72), channel_id=1, source_target_pairs={{1,0},{2,1},{3,2},{4,3},{5,4},{6,5},{7,6},{0,7},{9,8},{10,9},{11,1... | collective-permute-start | bytes 331784 | tf_op jit(solution)/shard_map/ppermute | solution.py:251
  103.7 4.3 %collective-permute-done.16.refs_3_ = f32[24,1152]{1,0:T(8,128)S(1)} collective-permute-done((f32[24,1152]{1,0:T(8,128)S(1)}, f32[24,1152]{1,0:T(8,128)S(1)}, u32[]{:S(2)}, u32[]{:S(2)}) %collective-permute-start.16) | collective-permute-done | bytes 110624 | tf_op jit(solution)/shard_map/ppermute | solution.py:251
  108.4 2.6 %collective-permute-done.18.refs_5_ = f32[24,1152]{1,0:T(8,128)S(1)} collective-permute-done((f32[24,1152]{1,0:T(8,128)S(1)}, f32[24,1152]{1,0:T(8,128)S(1)}, u32[]{:S(2)}, u32[]{:S(2)}) %collective-permute-start.18) | collective-permute-done | bytes 110624 | tf_op jit(solution)/shard_map/ppermute | solution.py:251
  111.1 2.0 %collective-permute-done.19.refs_6_ = f32[24,1152]{1,0:T(8,128)S(1)} collective-permute-done((f32[24,1152]{1,0:T(8,128)S(1)}, f32[24,1152]{1,0:T(8,128)S(1)}, u32[]{:S(2)}, u32[]{:S(2)}) %collective-permute-start.19) | collective-permute-done | bytes 110624 | tf_op jit(solution)/shard_map/ppermute | solution.py:251
  113.7 4.1 %collective-permute-done.21 = f32[3,2,2304]{2,1,0:T(2,128)S(1)} collective-permute-done((f32[3,2,2304]{2,1,0:T(2,128)S(1)}, f32[3,2,2304]{2,1,0:T(2,128)S(1)}, u32[]{:S(2)}, u32[]{:S(2)}) %collective-permute-start.21) | collective-permute-done | bytes 55328 | tf_op jit(solution)/shard_map/ppermute | solution.py:251
  (42 shorter events, 3.9 us)
Async XLA Ops:
  0.0 49.3 %copy-start.2 = (bf16[96,96]{1,0:T(8,128)(2,1)S(1)}, bf16[96,96]{1,0:T(8,128)(2,1)}, u32[]{:S(2)}) copy-start(bf16[96,96]{1,0:T(8,128)(2,1)} %constant.185.iz) | copy-start | bytes 55300
  0.0 49.3 %copy-start.3 = (bf16[96,96]{1,0:T(8,128)(2,1)S(1)}, bf16[96,96]{1,0:T(8,128)(2,1)}, u32[]{:S(2)}) copy-start(bf16[96,96]{1,0:T(8,128)(2,1)} %constant.177.fz) | copy-start | bytes 55300
  0.0 7.6 %copy-start = (f32[4,3,2304]{2,0,1:T(4,128)S(1)}, f32[4,3,2304]{2,0,1:T(4,128)}, u32[]{:S(2)}) copy-start(f32[4,3,2304]{2,0,1:T(4,128)} %param.4) | copy-start | bytes 331780
  0.0 26.7 %copy-start.1 = (s32[4]{0:T(128)S(1)}, s32[4]{0:T(128)}, u32[]{:S(2)}) copy-start(s32[4]{0:T(128)} %occupation.1) | copy-start | bytes 52
  1.1 6.5 %collective-permute-start = (f32[3,2,2304]{2,1,0:T(2,128)S(1)}, f32[3,2,2304]{2,1,0:T(2,128)S(1)}, u32[]{:S(2)}, u32[]{:S(2)}) collective-permute-start(f32[3,2,2304]{2,1,0:T(2,128)S(1)} %slice_select_fusion), channel_id=1, source_target_pairs={{8,0},{9,1},{10,2},{11,3},{12,4},{13,5},{14,6},{15,7},{0,8},{1,9},... | collective-permute-start | bytes 165896 | tf_op jit(solution)/shard_map/ppermute | solution.py:251
  7.7 14.2 %collective-permute-start.5 = (f32[24,1152]{1,0:T(8,128)S(1)}, f32[24,1152]{1,0:T(8,128)S(1)}, u32[]{:S(2)}, u32[]{:S(2)}) collective-permute-start(f32[24,1152]{1,0:T(8,128)S(1)} %shard_map.46.refs_0_), channel_id=1, source_target_pairs={{6,0},{7,1},{0,2},{1,3},{2,4},{3,5},{4,6},{5,7},{14,8},{15,9},{8,1... | collective-permute-start | bytes 331784 | tf_op jit(solution)/shard_map/ppermute | solution.py:251
  10.7 9.7 %collective-permute-start.2 = (f32[24,1152]{1,0:T(8,128)S(1)}, f32[24,1152]{1,0:T(8,128)S(1)}, u32[]{:S(2)}, u32[]{:S(2)}) collective-permute-start(f32[24,1152]{1,0:T(8,128)S(1)} %shard_map.46.refs_0_), channel_id=1, source_target_pairs={{2,0},{3,1},{4,2},{5,3},{6,4},{7,5},{0,6},{1,7},{10,8},{11,9},{12,... | collective-permute-start | bytes 331784 | tf_op jit(solution)/shard_map/ppermute | solution.py:251
  13.9 9.5 %collective-permute-start.7 = (f32[24,1152]{1,0:T(8,128)S(1)}, f32[24,1152]{1,0:T(8,128)S(1)}, u32[]{:S(2)}, u32[]{:S(2)}) collective-permute-start(f32[24,1152]{1,0:T(8,128)S(1)} %shard_map.46.refs_0_), channel_id=1, source_target_pairs={{7,0},{0,1},{1,2},{2,3},{3,4},{4,5},{5,6},{6,7},{15,8},{8,9},{9,10... | collective-permute-start | bytes 331784 | tf_op jit(solution)/shard_map/ppermute | solution.py:251
  14.7 8.7 %collective-permute-start.1 = (f32[24,1152]{1,0:T(8,128)S(1)}, f32[24,1152]{1,0:T(8,128)S(1)}, u32[]{:S(2)}, u32[]{:S(2)}) collective-permute-start(f32[24,1152]{1,0:T(8,128)S(1)} %shard_map.46.refs_0_), channel_id=1, source_target_pairs={{1,0},{2,1},{3,2},{4,3},{5,4},{6,5},{7,6},{0,7},{9,8},{10,9},{11,1... | collective-permute-start | bytes 331784 | tf_op jit(solution)/shard_map/ppermute | solution.py:251
  20.4 6.3 %collective-permute-start.4 = (f32[24,1152]{1,0:T(8,128)S(1)}, f32[24,1152]{1,0:T(8,128)S(1)}, u32[]{:S(2)}, u32[]{:S(2)}) collective-permute-start(f32[24,1152]{1,0:T(8,128)S(1)} %collective-permute-done.2.refs_2_), channel_id=1, source_target_pairs={{2,0},{3,1},{4,2},{5,3},{6,4},{7,5},{0,6},{1,7},{10,8},{11,9},{12,... | collective-permute-start | bytes 331784 | tf_op jit(solution)/shard_map/ppermute | solution.py:251
  21.8 4.8 %collective-permute-start.3 = (f32[24,1152]{1,0:T(8,128)S(1)}, f32[24,1152]{1,0:T(8,128)S(1)}, u32[]{:S(2)}, u32[]{:S(2)}) collective-permute-start(f32[24,1152]{1,0:T(8,128)S(1)} %collective-permute-done.2.refs_2_), channel_id=1, source_target_pairs={{1,0},{2,1},{3,2},{4,3},{5,4},{6,5},{7,6},{0,7},{9,8},{10,9},{11,1... | collective-permute-start | bytes 331784 | tf_op jit(solution)/shard_map/ppermute | solution.py:251
  21.8 4.8 %collective-permute-start.6 = (f32[24,1152]{1,0:T(8,128)S(1)}, f32[24,1152]{1,0:T(8,128)S(1)}, u32[]{:S(2)}, u32[]{:S(2)}) collective-permute-start(f32[24,1152]{1,0:T(8,128)S(1)} %collective-permute-done.5.refs_6_), channel_id=1, source_target_pairs={{7,0},{0,1},{1,2},{2,3},{3,4},{4,5},{5,6},{6,7},{15,8},{8,9},{9,10... | collective-permute-start | bytes 331784 | tf_op jit(solution)/shard_map/ppermute | solution.py:251
  27.5 21.8 %collective-permute-start.8 = (f32[2,48,2432]{2,1,0:T(8,128)S(1)}, f32[2,48,2432]{2,1,0:T(8,128)S(1)}, u32[]{:S(2)}, u32[]{:S(2)}) collective-permute-start(f32[2,48,2432]{2,1,0:T(8,128)S(1)} %get-tuple-element.49.own), channel_id=1, source_target_pairs={{16,0},{0,16},{48,32},{32,48},{80,64},{64,80},{112,96},{96,112},{1... | collective-permute-start | bytes 2801672 | tf_op jit(solution)/shard_map/ppermute | solution.py:251
  32.5 14.7 %collective-permute-start.9 = (f32[48,2432]{1,0:T(8,128)S(1)}, f32[48,2432]{1,0:T(8,128)S(1)}, u32[]{:S(2)}, u32[]{:S(2)}) collective-permute-start(f32[48,2432]{1,0:T(8,128)S(1)} %get-tuple-element.51), channel_id=1, source_target_pairs={{160,0},{193,1},{10,2},{67,3},{36,4},{133,5},{174,6},{111,7},{168,... | collective-permute-start | bytes 1400840 | tf_op jit(solution)/shard_map/ppermute | solution.py:340
  47.3 11.0 %collective-permute-start.10 = (f32[48,2432]{1,0:T(8,128)S(1)}, f32[48,2432]{1,0:T(8,128)S(1)}, u32[]{:S(2)}, u32[]{:S(2)}) collective-permute-start(f32[48,2432]{1,0:T(8,128)S(1)} %get-tuple-element.52), channel_id=1, source_target_pairs={{32,0},{129,1},{170,2},{107,3},{164,4},{197,5},{14,6},{71,7},{40,8... | collective-permute-start | bytes 1400840 | tf_op jit(solution)/shard_map/ppermute | solution.py:343
  65.9 23.6 %collective-permute-start.11 = (f32[2,48,2304]{2,1,0:T(8,128)S(1)}, f32[2,48,2304]{2,1,0:T(8,128)S(1)}, u32[]{:S(2)}, u32[]{:S(2)}) collective-permute-start(f32[2,48,2304]{2,1,0:T(8,128)S(1)} %get-tuple-element.62), channel_id=1, source_target_pairs={{16,0},{0,16},{48,32},{32,48},{80,64},{64,80},{112,96},{96,112},{1... | collective-permute-start | bytes 2654216 | tf_op jit(solution)/shard_map/ppermute | solution.py:251
  66.1 12.2 %collective-permute-start.13 = (f32[48,2304]{1,0:T(8,128)S(1)}, f32[48,2304]{1,0:T(8,128)S(1)}, u32[]{:S(2)}, u32[]{:S(2)}) collective-permute-start(f32[48,2304]{1,0:T(8,128)S(1)} %get-tuple-element.64), channel_id=1, source_target_pairs={{0,32},{1,129},{2,170},{3,107},{4,164},{5,197},{6,14},{8,40},{9,13... | collective-permute-start | bytes 1327112 | tf_op jit(solution)/shard_map/ppermute | solution.py:298
  72.1 17.4 %collective-permute-start.12 = (f32[48,2304]{1,0:T(8,128)S(1)}, f32[48,2304]{1,0:T(8,128)S(1)}, u32[]{:S(2)}, u32[]{:S(2)}) collective-permute-start(f32[48,2304]{1,0:T(8,128)S(1)} %get-tuple-element.63), channel_id=1, source_target_pairs={{0,160},{1,193},{2,10},{4,36},{5,133},{6,174},{7,111},{8,168},{9,2... | collective-permute-start | bytes 1327112 | tf_op jit(solution)/shard_map/ppermute | solution.py:298
  90.0 9.5 %collective-permute-start.14 = (f32[24,1152]{1,0:T(8,128)S(1)}, f32[24,1152]{1,0:T(8,128)S(1)}, u32[]{:S(2)}, u32[]{:S(2)}) collective-permute-start(f32[24,1152]{1,0:T(8,128)S(1)} %get-tuple-element.66), channel_id=1, source_target_pairs={{5,0},{6,1},{7,2},{0,3},{1,4},{2,5},{3,6},{4,7},{13,8},{14,9},{15,... | collective-permute-start | bytes 331784 | tf_op jit(solution)/shard_map/ppermute | solution.py:251
  90.3 12.0 %collective-permute-start.15 = (f32[24,1152]{1,0:T(8,128)S(1)}, f32[24,1152]{1,0:T(8,128)S(1)}, u32[]{:S(2)}, u32[]{:S(2)}) collective-permute-start(f32[24,1152]{1,0:T(8,128)S(1)} %get-tuple-element.67), channel_id=1, source_target_pairs={{3,0},{4,1},{5,2},{6,3},{7,4},{0,5},{1,6},{2,7},{11,8},{12,9},{13,... | collective-permute-start | bytes 331784 | tf_op jit(solution)/shard_map/ppermute | solution.py:251
  94.7 13.2 %collective-permute-start.16 = (f32[24,1152]{1,0:T(8,128)S(1)}, f32[24,1152]{1,0:T(8,128)S(1)}, u32[]{:S(2)}, u32[]{:S(2)}) collective-permute-start(f32[24,1152]{1,0:T(8,128)S(1)} %get-tuple-element.68), channel_id=1, source_target_pairs={{4,0},{5,1},{6,2},{7,3},{0,4},{1,5},{2,6},{3,7},{12,8},{13,9},{14,... | collective-permute-start | bytes 331784 | tf_op jit(solution)/shard_map/ppermute | solution.py:251
  95.9 12.6 %collective-permute-start.17 = (f32[24,1152]{1,0:T(8,128)S(1)}, f32[24,1152]{1,0:T(8,128)S(1)}, u32[]{:S(2)}, u32[]{:S(2)}) collective-permute-start(f32[24,1152]{1,0:T(8,128)S(1)} %get-tuple-element.69), channel_id=1, source_target_pairs={{6,0},{7,1},{0,2},{1,3},{2,4},{3,5},{4,6},{5,7},{14,8},{15,9},{8,1... | collective-permute-start | bytes 331784 | tf_op jit(solution)/shard_map/ppermute | solution.py:251
  96.2 14.9 %collective-permute-start.18 = (f32[24,1152]{1,0:T(8,128)S(1)}, f32[24,1152]{1,0:T(8,128)S(1)}, u32[]{:S(2)}, u32[]{:S(2)}) collective-permute-start(f32[24,1152]{1,0:T(8,128)S(1)} %get-tuple-element.70), channel_id=1, source_target_pairs={{2,0},{3,1},{4,2},{5,3},{6,4},{7,5},{0,6},{1,7},{10,8},{11,9},{12,... | collective-permute-start | bytes 331784 | tf_op jit(solution)/shard_map/ppermute | solution.py:251
  99.5 13.6 %collective-permute-start.19 = (f32[24,1152]{1,0:T(8,128)S(1)}, f32[24,1152]{1,0:T(8,128)S(1)}, u32[]{:S(2)}, u32[]{:S(2)}) collective-permute-start(f32[24,1152]{1,0:T(8,128)S(1)} %get-tuple-element.71), channel_id=1, source_target_pairs={{7,0},{0,1},{1,2},{2,3},{3,4},{4,5},{5,6},{6,7},{15,8},{8,9},{9,10... | collective-permute-start | bytes 331784 | tf_op jit(solution)/shard_map/ppermute | solution.py:251
  102.3 10.8 %collective-permute-start.20 = (f32[24,1152]{1,0:T(8,128)S(1)}, f32[24,1152]{1,0:T(8,128)S(1)}, u32[]{:S(2)}, u32[]{:S(2)}) collective-permute-start(f32[24,1152]{1,0:T(8,128)S(1)} %get-tuple-element.72), channel_id=1, source_target_pairs={{1,0},{2,1},{3,2},{4,3},{5,4},{6,5},{7,6},{0,7},{9,8},{10,9},{11,1... | collective-permute-start | bytes 331784 | tf_op jit(solution)/shard_map/ppermute | solution.py:251
  113.2 4.6 %collective-permute-start.21 = (f32[3,2,2304]{2,1,0:T(2,128)S(1)}, f32[3,2,2304]{2,1,0:T(2,128)S(1)}, u32[]{:S(2)}, u32[]{:S(2)}) collective-permute-start(f32[3,2,2304]{2,1,0:T(2,128)S(1)} %get-tuple-element.74), channel_id=1, source_target_pairs={{8,0},{9,1},{10,2},{11,3},{12,4},{13,5},{14,6},{15,7},{0,8},{1,9},... | collective-permute-start | bytes 165896 | tf_op jit(solution)/shard_map/ppermute | solution.py:251

commit v7 on v6

--- a/solution.py
+++ b/solution.py
@@ -136,20 +136,20 @@
     def half_in(kz):
         return apply(fz[...], spec[kz]) * ktab[kz]
 
-    for u in range(12):
+    for u in range(16):
         bufs[-1][u] = half_in(u)
 
     def middle(k, _):
-        done = [apply(iz[...], bufs[-1][u]) for u in range(12)]
-        for u in range(12):
-            bufs[-1][u] = half_in((k + 1) * 12 + u)
-        for u in range(12):
-            spec[k * 12 + u] = done[u]
+        done = [apply(iz[...], bufs[-1][u]) for u in range(16)]
+        for u in range(16):
+            bufs[-1][u] = half_in((k + 1) * 16 + u)
+        for u in range(16):
+            spec[k * 16 + u] = done[u]
         return 0
 
-    lax.fori_loop(0, G // 12 - 1, middle, 0)
-    for u in range(12):
-        spec[G - 12 + u] = apply(iz[...], bufs[-1][u])
+    lax.fori_loop(0, G // 16 - 1, middle, 0)
+    for u in range(16):
+        spec[G - 16 + u] = apply(iz[...], bufs[-1][u])
 
     def spread(w):
         return jnp.concatenate([w] * (LB // 128), axis=1)
@@ -207,7 +207,7 @@
             pltpu.VMEM((WIDE, LB), jnp.float32),
             pltpu.VMEM((LB, WIDE), jnp.float32),
             pltpu.VMEM((YB, G, WIDE), jnp.float32),
-        ] * 2 + [pltpu.VMEM((12, G, WIDE), jnp.float32)],
+        ] * 2 + [pltpu.VMEM((16, G, WIDE), jnp.float32)],
         compiler_params=pltpu.CompilerParams(vmem_limit_bytes=24 << 20),
         cost_estimate=pl.CostEstimate(flops=5 * 10**9, bytes_accessed=10**7, transcendentals=0),
     )(*args)

time: 119 us -> 119 us (level)
  the two profiles are of different devices: /device:TPU:1 before, /device:TPU:48 now
where the time goes in v7:
time: 119 us
  waiting for transfers between devices  54.5 us (46%)
  starting transfers between devices  42.9 us (36%)
  Pallas kernels  16.6 us (14%)
  other arithmetic  3.88 us (3%)
    ppermute x18, starting transfers between devices, ring(): lax.ppermute(block, axis, [(source(i), i) for i in range(lax.axis_size(ax...  31 us
    ppermute x18, waiting for transfers between devices, ring(): lax.ppermute(block, axis, [(source(i), i) for i in range(lax.axis_size(ax...  29.6 us
    pallas_call x2, Pallas kernels, pair_solver(): pl.pallas_call(functools.partial(kernel, first), out_shape=[f32(2, G, ROW...  15.2 us
    ppermute x1, waiting for transfers between devices, on_device(): vis0 = lax.ppermute(lone[0], axes, visit_route(0))  12.3 us
    ppermute x2, waiting for transfers between devices, returned(): lax.ppermute(back, ('band', 'grid'), [(d, s) for s, d in visit_route(v, F...  11.8 us
    ppermute x2, starting transfers between devices, returned(): lax.ppermute(back, ('band', 'grid'), [(d, s) for s, d in visit_route(v, F...  8.04 us
    ppermute x1, starting transfers between devices, on_device(): vis0 = lax.ppermute(lone[0], axes, visit_route(0))  3.19 us
  transfers between devices with their start and end apart: 22, of which 13 were waited for; matrix products, arithmetic and copies ran while one was open for 2% of the time, Pallas kernels for 6%

profile of v7, /device:TPU:48, one launch (start us, length us, event | category | flops | bytes accessed | tf_op | source)
XLA Modules:
  0.0 118.7 jit_solution(5519615423560586646)
XLA Ops:
  0.0 1.1 slice_select_fusion
  2.4 1.4 %fusion.9.ktab = f32[48,48,256]{2,1,0:T(8,128)S(1)} fusion(f32[256]{0:T(256)S(1)} %or_select_fusion, f32[48,48]{1,0:T(8,128)S(1)} %broadcast_multiply_fusion, s32[]{:T(128)S(6)} %copy.5, s32[256]{0:T(256)S(1)} %fusion.26, s32[48,48]{1,0:T(8,128)S(1)} %broadcast_add_fusion), kind=kLoop, calls=%fused_computation.12 | loop fusion | flops 8847360 | bytes 2379780 | tf_op jit(solution)/shard_map/jit(_where)/select_n | solution.py:247
  4.2 2.6 %collective-permute-done.came = f32[3,2,2304]{2,1,0:T(2,128)S(1)} collective-permute-done((f32[3,2,2304]{2,1,0:T(2,128)S(1)}, f32[3,2,2304]{2,1,0:T(2,128)S(1)}, u32[]{:S(2)}, u32[]{:S(2)}) %collective-permute-start) | collective-permute-done | bytes 55328 | tf_op jit(solution)/shard_map/ppermute | solution.py:251
  6.9 3.3 %collective-permute-start.5 = (f32[24,1152]{1,0:T(8,128)S(1)}, f32[24,1152]{1,0:T(8,128)S(1)}, u32[]{:S(2)}, u32[]{:S(2)}) collective-permute-start(f32[24,1152]{1,0:T(8,128)S(1)} %shard_map.46.refs_0_), channel_id=1, source_target_pairs={{6,0},{7,1},{0,2},{1,3},{2,4},{3,5},{4,6},{5,7},{14,8},{15,9},{8,1... | collective-permute-start | bytes 331784 | tf_op jit(solution)/shard_map/ppermute | solution.py:251
  10.2 2.2 %collective-permute-start.2 = (f32[24,1152]{1,0:T(8,128)S(1)}, f32[24,1152]{1,0:T(8,128)S(1)}, u32[]{:S(2)}, u32[]{:S(2)}) collective-permute-start(f32[24,1152]{1,0:T(8,128)S(1)} %shard_map.46.refs_0_), channel_id=1, source_target_pairs={{2,0},{3,1},{4,2},{5,3},{6,4},{7,5},{0,6},{1,7},{10,8},{11,9},{12,... | collective-permute-start | bytes 331784 | tf_op jit(solution)/shard_map/ppermute | solution.py:251
  12.5 1.0 collective-permute-start.7
  13.5 1.1 collective-permute-start.1
  14.6 3.6 %collective-permute-done.2.refs_2_ = f32[24,1152]{1,0:T(8,128)S(1)} collective-permute-done((f32[24,1152]{1,0:T(8,128)S(1)}, f32[24,1152]{1,0:T(8,128)S(1)}, u32[]{:S(2)}, u32[]{:S(2)}) %collective-permute-start.2) | collective-permute-done | bytes 110624 | tf_op jit(solution)/shard_map/ppermute | solution.py:251
  18.2 3.4 %collective-permute-start.4 = (f32[24,1152]{1,0:T(8,128)S(1)}, f32[24,1152]{1,0:T(8,128)S(1)}, u32[]{:S(2)}, u32[]{:S(2)}) collective-permute-start(f32[24,1152]{1,0:T(8,128)S(1)} %collective-permute-done.2.refs_2_), channel_id=1, source_target_pairs={{2,0},{3,1},{4,2},{5,3},{6,4},{7,5},{0,6},{1,7},{10,8},{11,9},{12,... | collective-permute-start | bytes 331784 | tf_op jit(solution)/shard_map/ppermute | solution.py:251
  21.7 1.9 %collective-permute-start.6 = (f32[24,1152]{1,0:T(8,128)S(1)}, f32[24,1152]{1,0:T(8,128)S(1)}, u32[]{:S(2)}, u32[]{:S(2)}) collective-permute-start(f32[24,1152]{1,0:T(8,128)S(1)} %collective-permute-done.5.refs_6_), channel_id=1, source_target_pairs={{7,0},{0,1},{1,2},{2,3},{3,4},{4,5},{5,6},{6,7},{15,8},{8,9},{9,10... | collective-permute-start | bytes 331784 | tf_op jit(solution)/shard_map/ppermute | solution.py:251
  23.7 3.2 %collective-permute-done.6.refs_5_ = f32[24,1152]{1,0:T(8,128)S(1)} collective-permute-done((f32[24,1152]{1,0:T(8,128)S(1)}, f32[24,1152]{1,0:T(8,128)S(1)}, u32[]{:S(2)}, u32[]{:S(2)}) %collective-permute-start.6) | collective-permute-done | bytes 110624 | tf_op jit(solution)/shard_map/ppermute | solution.py:251
  27.0 0.8 shard_map.47
  27.9 3.2 %collective-permute-start.9 = (f32[48,2432]{1,0:T(8,128)S(1)}, f32[48,2432]{1,0:T(8,128)S(1)}, u32[]{:S(2)}, u32[]{:S(2)}) collective-permute-start(f32[48,2432]{1,0:T(8,128)S(1)} %get-tuple-element.51), channel_id=1, source_target_pairs={{160,0},{193,1},{10,2},{67,3},{36,4},{133,5},{174,6},{111,7},{168,... | collective-permute-start | bytes 1400840 | tf_op jit(solution)/shard_map/ppermute | solution.py:340
  31.0 12.3 %collective-permute-done.9.vis = f32[48,2432]{1,0:T(8,128)S(1)} collective-permute-done((f32[48,2432]{1,0:T(8,128)S(1)}, f32[48,2432]{1,0:T(8,128)S(1)}, u32[]{:S(2)}, u32[]{:S(2)}) %collective-permute-start.9) | collective-permute-done | bytes 466976 | tf_op jit(solution)/shard_map/ppermute | solution.py:340
  44.0 7.7 %shard_map.48 = (f32[2,48,2304]{2,1,0:T(8,128)S(1)}, f32[2,48,2304]{2,1,0:T(8,128)S(1)}, f32[48,2304]{1,0:T(8,128)S(1)}) custom-call(s32[4]{0:T(128)S(1)} %pad_add_fusion.idx, f32[2,48,2432]{2,1,0:T(8,128)S(1)} %get-tuple-element.49.own, f32[2,48,2432]{2,1,0:T(8,128)S(1)} %collective-permute-done.8.twin, f32[48,2432]{1,0:T(8,128)S(1)} %collective-permute-done.9.vis, ...), custom_call_target="tpu_custom_call" | custom-call | flops 5000000000 | bytes 10000000 | tf_op jit(solution)/shard_map/pallas_call | solution.py:199
  51.7 0.7 collective-permute-done.10.vis
  52.4 7.5 %shard_map.49 = (f32[2,48,2304]{2,1,0:T(8,128)S(1)}, f32[2,48,2304]{2,1,0:T(8,128)S(1)}, f32[48,2304]{1,0:T(8,128)S(1)}) custom-call(s32[4]{0:T(128)S(1)} %pad_add_fusion.idx, f32[2,48,2432]{2,1,0:T(8,128)S(1)} %get-tuple-element.49.own, f32[2,48,2432]{2,1,0:T(8,128)S(1)} %collective-permute-done.8.twin, f32[48,2432]{1,0:T(8,128)S(1)} %collective-permute-done.10.vis, ...), custom_call_target="tpu_custom_call" | custom-call | flops 5000000000 | bytes 10000000 | tf_op jit(solution)/shard_map/pallas_call | solution.py:199
  59.9 2.7 %collective-permute-start.11 = (f32[2,48,2304]{2,1,0:T(8,128)S(1)}, f32[2,48,2304]{2,1,0:T(8,128)S(1)}, u32[]{:S(2)}, u32[]{:S(2)}) collective-permute-start(f32[2,48,2304]{2,1,0:T(8,128)S(1)} %get-tuple-element.62), channel_id=1, source_target_pairs={{16,0},{0,16},{48,32},{32,48},{80,64},{64,80},{112,96},{96,112},{1... | collective-permute-start | bytes 2654216 | tf_op jit(solution)/shard_map/ppermute | solution.py:251
  62.6 2.5 %collective-permute-start.13 = (f32[48,2304]{1,0:T(8,128)S(1)}, f32[48,2304]{1,0:T(8,128)S(1)}, u32[]{:S(2)}, u32[]{:S(2)}) collective-permute-start(f32[48,2304]{1,0:T(8,128)S(1)} %get-tuple-element.64), channel_id=1, source_target_pairs={{0,32},{1,129},{2,170},{3,107},{4,164},{5,197},{6,14},{8,40},{9,13... | collective-permute-start | bytes 1327112 | tf_op jit(solution)/shard_map/ppermute | solution.py:298
  65.1 5.5 %collective-permute-start.12 = (f32[48,2304]{1,0:T(8,128)S(1)}, f32[48,2304]{1,0:T(8,128)S(1)}, u32[]{:S(2)}, u32[]{:S(2)}) collective-permute-start(f32[48,2304]{1,0:T(8,128)S(1)} %get-tuple-element.63), channel_id=1, source_target_pairs={{0,160},{1,193},{2,10},{4,36},{5,133},{6,174},{7,111},{8,168},{9,2... | collective-permute-start | bytes 1327112 | tf_op jit(solution)/shard_map/ppermute | solution.py:298
  70.7 2.1 %collective-permute-done.13.c1 = f32[48,2304]{1,0:T(8,128)S(1)} collective-permute-done((f32[48,2304]{1,0:T(8,128)S(1)}, f32[48,2304]{1,0:T(8,128)S(1)}, u32[]{:S(2)}, u32[]{:S(2)}) %collective-permute-start.13) | collective-permute-done | bytes 442400 | tf_op jit(solution)/shard_map/ppermute | solution.py:298
  72.8 9.7 %collective-permute-done.12.c0 = f32[48,2304]{1,0:T(8,128)S(1)} collective-permute-done((f32[48,2304]{1,0:T(8,128)S(1)}, f32[48,2304]{1,0:T(8,128)S(1)}, u32[]{:S(2)}, u32[]{:S(2)}) %collective-permute-start.12) | collective-permute-done | bytes 442400 | tf_op jit(solution)/shard_map/ppermute | solution.py:298
  83.0 7.1 %collective-permute-start.14 = (f32[24,1152]{1,0:T(8,128)S(1)}, f32[24,1152]{1,0:T(8,128)S(1)}, u32[]{:S(2)}, u32[]{:S(2)}) collective-permute-start(f32[24,1152]{1,0:T(8,128)S(1)} %get-tuple-element.66), channel_id=1, source_target_pairs={{5,0},{6,1},{7,2},{0,3},{1,4},{2,5},{3,6},{4,7},{13,8},{14,9},{15,... | collective-permute-start | bytes 331784 | tf_op jit(solution)/shard_map/ppermute | solution.py:251
  90.1 2.1 %collective-permute-start.16 = (f32[24,1152]{1,0:T(8,128)S(1)}, f32[24,1152]{1,0:T(8,128)S(1)}, u32[]{:S(2)}, u32[]{:S(2)}) collective-permute-start(f32[24,1152]{1,0:T(8,128)S(1)} %get-tuple-element.68), channel_id=1, source_target_pairs={{4,0},{5,1},{6,2},{7,3},{0,4},{1,5},{2,6},{3,7},{12,8},{13,9},{14,... | collective-permute-start | bytes 331784 | tf_op jit(solution)/shard_map/ppermute | solution.py:251
  92.2 1.8 %collective-permute-start.17 = (f32[24,1152]{1,0:T(8,128)S(1)}, f32[24,1152]{1,0:T(8,128)S(1)}, u32[]{:S(2)}, u32[]{:S(2)}) collective-permute-start(f32[24,1152]{1,0:T(8,128)S(1)} %get-tuple-element.69), channel_id=1, source_target_pairs={{6,0},{7,1},{0,2},{1,3},{2,4},{3,5},{4,6},{5,7},{14,8},{15,9},{8,1... | collective-permute-start | bytes 331784 | tf_op jit(solution)/shard_map/ppermute | solution.py:251
  94.0 2.3 %collective-permute-start.18 = (f32[24,1152]{1,0:T(8,128)S(1)}, f32[24,1152]{1,0:T(8,128)S(1)}, u32[]{:S(2)}, u32[]{:S(2)}) collective-permute-start(f32[24,1152]{1,0:T(8,128)S(1)} %get-tuple-element.70), channel_id=1, source_target_pairs={{2,0},{3,1},{4,2},{5,3},{6,4},{7,5},{0,6},{1,7},{10,8},{11,9},{12,... | collective-permute-start | bytes 331784 | tf_op jit(solution)/shard_map/ppermute | solution.py:251
  96.3 0.7 collective-permute-done.14.refs_1_
  97.0 1.3 %collective-permute-start.19 = (f32[24,1152]{1,0:T(8,128)S(1)}, f32[24,1152]{1,0:T(8,128)S(1)}, u32[]{:S(2)}, u32[]{:S(2)}) collective-permute-start(f32[24,1152]{1,0:T(8,128)S(1)} %get-tuple-element.71), channel_id=1, source_target_pairs={{7,0},{0,1},{1,2},{2,3},{3,4},{4,5},{5,6},{6,7},{15,8},{8,9},{9,10... | collective-permute-start | bytes 331784 | tf_op jit(solution)/shard_map/ppermute | solution.py:251
  98.3 9.1 %collective-permute-done.15.refs_2_ = f32[24,1152]{1,0:T(8,128)S(1)} collective-permute-done((f32[24,1152]{1,0:T(8,128)S(1)}, f32[24,1152]{1,0:T(8,128)S(1)}, u32[]{:S(2)}, u32[]{:S(2)}) %collective-permute-start.15) | collective-permute-done | bytes 110624 | tf_op jit(solution)/shard_map/ppermute | solution.py:251
  107.7 4.4 %collective-permute-done.20.refs_7_ = f32[24,1152]{1,0:T(8,128)S(1)} collective-permute-done((f32[24,1152]{1,0:T(8,128)S(1)}, f32[24,1152]{1,0:T(8,128)S(1)}, u32[]{:S(2)}, u32[]{:S(2)}) %collective-permute-start.20) | collective-permute-done | bytes 110624 | tf_op jit(solution)/shard_map/ppermute | solution.py:251
  112.4 5.6 %collective-permute-done.21 = f32[3,2,2304]{2,1,0:T(2,128)S(1)} collective-permute-done((f32[3,2,2304]{2,1,0:T(2,128)S(1)}, f32[3,2,2304]{2,1,0:T(2,128)S(1)}, u32[]{:S(2)}, u32[]{:S(2)}) %collective-permute-start.21) | collective-permute-done | bytes 55328 | tf_op jit(solution)/shard_map/ppermute | solution.py:251
  118.0 0.7 maximum_bitcast_fusion
  (42 shorter events, 3.1 us)
Async XLA Ops:
  0.0 44.0 %copy-start.2 = (bf16[96,96]{1,0:T(8,128)(2,1)S(1)}, bf16[96,96]{1,0:T(8,128)(2,1)}, u32[]{:S(2)}) copy-start(bf16[96,96]{1,0:T(8,128)(2,1)} %constant.185.iz) | copy-start | bytes 55300
  0.0 44.0 %copy-start.3 = (bf16[96,96]{1,0:T(8,128)(2,1)S(1)}, bf16[96,96]{1,0:T(8,128)(2,1)}, u32[]{:S(2)}) copy-start(bf16[96,96]{1,0:T(8,128)(2,1)} %constant.177.fz) | copy-start | bytes 55300
  0.0 6.8 %copy-start = (f32[4,3,2304]{2,0,1:T(4,128)S(1)}, f32[4,3,2304]{2,0,1:T(4,128)}, u32[]{:S(2)}) copy-start(f32[4,3,2304]{2,0,1:T(4,128)} %param.4) | copy-start | bytes 331780
  0.0 26.9 %copy-start.1 = (s32[4]{0:T(128)S(1)}, s32[4]{0:T(128)}, u32[]{:S(2)}) copy-start(s32[4]{0:T(128)} %occupation.1) | copy-start | bytes 52
  1.1 5.7 %collective-permute-start = (f32[3,2,2304]{2,1,0:T(2,128)S(1)}, f32[3,2,2304]{2,1,0:T(2,128)S(1)}, u32[]{:S(2)}, u32[]{:S(2)}) collective-permute-start(f32[3,2,2304]{2,1,0:T(2,128)S(1)} %slice_select_fusion), channel_id=1, source_target_pairs={{8,0},{9,1},{10,2},{11,3},{12,4},{13,5},{14,6},{15,7},{0,8},{1,9},... | collective-permute-start | bytes 165896 | tf_op jit(solution)/shard_map/ppermute | solution.py:251
  6.9 14.8 %collective-permute-start.5 = (f32[24,1152]{1,0:T(8,128)S(1)}, f32[24,1152]{1,0:T(8,128)S(1)}, u32[]{:S(2)}, u32[]{:S(2)}) collective-permute-start(f32[24,1152]{1,0:T(8,128)S(1)} %shard_map.46.refs_0_), channel_id=1, source_target_pairs={{6,0},{7,1},{0,2},{1,3},{2,4},{3,5},{4,6},{5,7},{14,8},{15,9},{8,1... | collective-permute-start | bytes 331784 | tf_op jit(solution)/shard_map/ppermute | solution.py:251
  10.2 7.9 %collective-permute-start.2 = (f32[24,1152]{1,0:T(8,128)S(1)}, f32[24,1152]{1,0:T(8,128)S(1)}, u32[]{:S(2)}, u32[]{:S(2)}) collective-permute-start(f32[24,1152]{1,0:T(8,128)S(1)} %shard_map.46.refs_0_), channel_id=1, source_target_pairs={{2,0},{3,1},{4,2},{5,3},{6,4},{7,5},{0,6},{1,7},{10,8},{11,9},{12,... | collective-permute-start | bytes 331784 | tf_op jit(solution)/shard_map/ppermute | solution.py:251
  12.5 11.2 %collective-permute-start.7 = (f32[24,1152]{1,0:T(8,128)S(1)}, f32[24,1152]{1,0:T(8,128)S(1)}, u32[]{:S(2)}, u32[]{:S(2)}) collective-permute-start(f32[24,1152]{1,0:T(8,128)S(1)} %shard_map.46.refs_0_), channel_id=1, source_target_pairs={{7,0},{0,1},{1,2},{2,3},{3,4},{4,5},{5,6},{6,7},{15,8},{8,9},{9,10... | collective-permute-start | bytes 331784 | tf_op jit(solution)/shard_map/ppermute | solution.py:251
  13.5 10.2 %collective-permute-start.1 = (f32[24,1152]{1,0:T(8,128)S(1)}, f32[24,1152]{1,0:T(8,128)S(1)}, u32[]{:S(2)}, u32[]{:S(2)}) collective-permute-start(f32[24,1152]{1,0:T(8,128)S(1)} %shard_map.46.refs_0_), channel_id=1, source_target_pairs={{1,0},{2,1},{3,2},{4,3},{5,4},{6,5},{7,6},{0,7},{9,8},{10,9},{11,1... | collective-permute-start | bytes 331784 | tf_op jit(solution)/shard_map/ppermute | solution.py:251
  18.2 8.7 %collective-permute-start.4 = (f32[24,1152]{1,0:T(8,128)S(1)}, f32[24,1152]{1,0:T(8,128)S(1)}, u32[]{:S(2)}, u32[]{:S(2)}) collective-permute-start(f32[24,1152]{1,0:T(8,128)S(1)} %collective-permute-done.2.refs_2_), channel_id=1, source_target_pairs={{2,0},{3,1},{4,2},{5,3},{6,4},{7,5},{0,6},{1,7},{10,8},{11,9},{12,... | collective-permute-start | bytes 331784 | tf_op jit(solution)/shard_map/ppermute | solution.py:251
  21.6 5.4 %collective-permute-start.3 = (f32[24,1152]{1,0:T(8,128)S(1)}, f32[24,1152]{1,0:T(8,128)S(1)}, u32[]{:S(2)}, u32[]{:S(2)}) collective-permute-start(f32[24,1152]{1,0:T(8,128)S(1)} %collective-permute-done.2.refs_2_), channel_id=1, source_target_pairs={{1,0},{2,1},{3,2},{4,3},{5,4},{6,5},{7,6},{0,7},{9,8},{10,9},{11,1... | collective-permute-start | bytes 331784 | tf_op jit(solution)/shard_map/ppermute | solution.py:251
  21.7 5.2 %collective-permute-start.6 = (f32[24,1152]{1,0:T(8,128)S(1)}, f32[24,1152]{1,0:T(8,128)S(1)}, u32[]{:S(2)}, u32[]{:S(2)}) collective-permute-start(f32[24,1152]{1,0:T(8,128)S(1)} %collective-permute-done.5.refs_6_), channel_id=1, source_target_pairs={{7,0},{0,1},{1,2},{2,3},{3,4},{4,5},{5,6},{6,7},{15,8},{8,9},{9,10... | collective-permute-start | bytes 331784 | tf_op jit(solution)/shard_map/ppermute | solution.py:251
  27.8 16.3 %collective-permute-start.8 = (f32[2,48,2432]{2,1,0:T(8,128)S(1)}, f32[2,48,2432]{2,1,0:T(8,128)S(1)}, u32[]{:S(2)}, u32[]{:S(2)}) collective-permute-start(f32[2,48,2432]{2,1,0:T(8,128)S(1)} %get-tuple-element.49.own), channel_id=1, source_target_pairs={{16,0},{0,16},{48,32},{32,48},{80,64},{64,80},{112,96},{96,112},{1... | collective-permute-start | bytes 2801672 | tf_op jit(solution)/shard_map/ppermute | solution.py:251
  27.9 15.5 %collective-permute-start.9 = (f32[48,2432]{1,0:T(8,128)S(1)}, f32[48,2432]{1,0:T(8,128)S(1)}, u32[]{:S(2)}, u32[]{:S(2)}) collective-permute-start(f32[48,2432]{1,0:T(8,128)S(1)} %get-tuple-element.51), channel_id=1, source_target_pairs={{160,0},{193,1},{10,2},{67,3},{36,4},{133,5},{174,6},{111,7},{168,... | collective-permute-start | bytes 1400840 | tf_op jit(solution)/shard_map/ppermute | solution.py:340
  43.4 9.0 %collective-permute-start.10 = (f32[48,2432]{1,0:T(8,128)S(1)}, f32[48,2432]{1,0:T(8,128)S(1)}, u32[]{:S(2)}, u32[]{:S(2)}) collective-permute-start(f32[48,2432]{1,0:T(8,128)S(1)} %get-tuple-element.52), channel_id=1, source_target_pairs={{32,0},{129,1},{170,2},{107,3},{164,4},{197,5},{14,6},{71,7},{40,8... | collective-permute-start | bytes 1400840 | tf_op jit(solution)/shard_map/ppermute | solution.py:343
  59.9 22.6 %collective-permute-start.11 = (f32[2,48,2304]{2,1,0:T(8,128)S(1)}, f32[2,48,2304]{2,1,0:T(8,128)S(1)}, u32[]{:S(2)}, u32[]{:S(2)}) collective-permute-start(f32[2,48,2304]{2,1,0:T(8,128)S(1)} %get-tuple-element.62), channel_id=1, source_target_pairs={{16,0},{0,16},{48,32},{32,48},{80,64},{64,80},{112,96},{96,112},{1... | collective-permute-start | bytes 2654216 | tf_op jit(solution)/shard_map/ppermute | solution.py:251
  62.6 10.2 %collective-permute-start.13 = (f32[48,2304]{1,0:T(8,128)S(1)}, f32[48,2304]{1,0:T(8,128)S(1)}, u32[]{:S(2)}, u32[]{:S(2)}) collective-permute-start(f32[48,2304]{1,0:T(8,128)S(1)} %get-tuple-element.64), channel_id=1, source_target_pairs={{0,32},{1,129},{2,170},{3,107},{4,164},{5,197},{6,14},{8,40},{9,13... | collective-permute-start | bytes 1327112 | tf_op jit(solution)/shard_map/ppermute | solution.py:298
  65.1 17.3 %collective-permute-start.12 = (f32[48,2304]{1,0:T(8,128)S(1)}, f32[48,2304]{1,0:T(8,128)S(1)}, u32[]{:S(2)}, u32[]{:S(2)}) collective-permute-start(f32[48,2304]{1,0:T(8,128)S(1)} %get-tuple-element.63), channel_id=1, source_target_pairs={{0,160},{1,193},{2,10},{4,36},{5,133},{6,174},{7,111},{8,168},{9,2... | collective-permute-start | bytes 1327112 | tf_op jit(solution)/shard_map/ppermute | solution.py:298
  83.0 14.1 %collective-permute-start.14 = (f32[24,1152]{1,0:T(8,128)S(1)}, f32[24,1152]{1,0:T(8,128)S(1)}, u32[]{:S(2)}, u32[]{:S(2)}) collective-permute-start(f32[24,1152]{1,0:T(8,128)S(1)} %get-tuple-element.66), channel_id=1, source_target_pairs={{5,0},{6,1},{7,2},{0,3},{1,4},{2,5},{3,6},{4,7},{13,8},{14,9},{15,... | collective-permute-start | bytes 331784 | tf_op jit(solution)/shard_map/ppermute | solution.py:251
  90.1 17.3 %collective-permute-start.15 = (f32[24,1152]{1,0:T(8,128)S(1)}, f32[24,1152]{1,0:T(8,128)S(1)}, u32[]{:S(2)}, u32[]{:S(2)}) collective-permute-start(f32[24,1152]{1,0:T(8,128)S(1)} %get-tuple-element.67), channel_id=1, source_target_pairs={{3,0},{4,1},{5,2},{6,3},{7,4},{0,5},{1,6},{2,7},{11,8},{12,9},{13,... | collective-permute-start | bytes 331784 | tf_op jit(solution)/shard_map/ppermute | solution.py:251
  90.1 17.3 %collective-permute-start.16 = (f32[24,1152]{1,0:T(8,128)S(1)}, f32[24,1152]{1,0:T(8,128)S(1)}, u32[]{:S(2)}, u32[]{:S(2)}) collective-permute-start(f32[24,1152]{1,0:T(8,128)S(1)} %get-tuple-element.68), channel_id=1, source_target_pairs={{4,0},{5,1},{6,2},{7,3},{0,4},{1,5},{2,6},{3,7},{12,8},{13,9},{14,... | collective-permute-start | bytes 331784 | tf_op jit(solution)/shard_map/ppermute | solution.py:251
  92.2 15.2 %collective-permute-start.17 = (f32[24,1152]{1,0:T(8,128)S(1)}, f32[24,1152]{1,0:T(8,128)S(1)}, u32[]{:S(2)}, u32[]{:S(2)}) collective-permute-start(f32[24,1152]{1,0:T(8,128)S(1)} %get-tuple-element.69), channel_id=1, source_target_pairs={{6,0},{7,1},{0,2},{1,3},{2,4},{3,5},{4,6},{5,7},{14,8},{15,9},{8,1... | collective-permute-start | bytes 331784 | tf_op jit(solution)/shard_map/ppermute | solution.py:251
  94.0 13.4 %collective-permute-start.18 = (f32[24,1152]{1,0:T(8,128)S(1)}, f32[24,1152]{1,0:T(8,128)S(1)}, u32[]{:S(2)}, u32[]{:S(2)}) collective-permute-start(f32[24,1152]{1,0:T(8,128)S(1)} %get-tuple-element.70), channel_id=1, source_target_pairs={{2,0},{3,1},{4,2},{5,3},{6,4},{7,5},{0,6},{1,7},{10,8},{11,9},{12,... | collective-permute-start | bytes 331784 | tf_op jit(solution)/shard_map/ppermute | solution.py:251
  97.0 10.6 %collective-permute-start.19 = (f32[24,1152]{1,0:T(8,128)S(1)}, f32[24,1152]{1,0:T(8,128)S(1)}, u32[]{:S(2)}, u32[]{:S(2)}) collective-permute-start(f32[24,1152]{1,0:T(8,128)S(1)} %get-tuple-element.71), channel_id=1, source_target_pairs={{7,0},{0,1},{1,2},{2,3},{3,4},{4,5},{5,6},{6,7},{15,8},{8,9},{9,10... | collective-permute-start | bytes 331784 | tf_op jit(solution)/shard_map/ppermute | solution.py:251
  107.4 4.7 %collective-permute-start.20 = (f32[24,1152]{1,0:T(8,128)S(1)}, f32[24,1152]{1,0:T(8,128)S(1)}, u32[]{:S(2)}, u32[]{:S(2)}) collective-permute-start(f32[24,1152]{1,0:T(8,128)S(1)} %get-tuple-element.72), channel_id=1, source_target_pairs={{1,0},{2,1},{3,2},{4,3},{5,4},{6,5},{7,6},{0,7},{9,8},{10,9},{11,1... | collective-permute-start | bytes 331784 | tf_op jit(solution)/shard_map/ppermute | solution.py:251
  112.3 5.7 %collective-permute-start.21 = (f32[3,2,2304]{2,1,0:T(2,128)S(1)}, f32[3,2,2304]{2,1,0:T(2,128)S(1)}, u32[]{:S(2)}, u32[]{:S(2)}) collective-permute-start(f32[3,2,2304]{2,1,0:T(2,128)S(1)} %get-tuple-element.74), channel_id=1, source_target_pairs={{8,0},{9,1},{10,2},{11,3},{12,4},{13,5},{14,6},{15,7},{0,8},{1,9},... | collective-permute-start | bytes 165896 | tf_op jit(solution)/shard_map/ppermute | solution.py:251
